TPU v7x, 32 devices: a whole 2x2x4 slice. The times are simulated.
32 devices in a mesh: group: 4 (over y, x), fsdp: 2 (over core), tensor: 4 (over z).
Axes of the slice: x: 2, y: 2, z: 4, core: 2. Of those that a mesh axis runs over, the one named last changes fastest.
Arguments:
- patches: bfloat16 [4, 2, 8, 577, 1024], P('group', None, ('fsdp', 'tensor')), may hold values from -6 to 6
- output_grad: bfloat16 [4, 2, 8, 577, 1024], P('group', None, ('fsdp', 'tensor')), may hold values from -6 to 6
- live_counts: int32 [4, 2, 2], P('group'), may hold values from 1 to 4, as said below
- attn_master: float32 [4, 1024, 1024], P(None, 'fsdp', 'tensor')
- mlp_master: float32 [2, 1024, 4096], P(None, 'fsdp', 'tensor')
- vector_master: float32 [12, 1024], replicated
- attn_moments: float32 [4, 2, 4, 1024, 1024], P('group', None, None, 'fsdp', 'tensor'), as said below
- mlp_moments: float32 [4, 2, 2, 1024, 4096], P('group', None, None, 'fsdp', 'tensor'), as said below
- vector_moments: float32 [4, 2, 12, 1024], P('group'), as said below
- attn_outer: float32 [4, 1024, 1024], P(None, 'fsdp', 'tensor'), may hold values from -0.125 to 0.125
- mlp_outer: float32 [2, 1024, 4096], P(None, 'fsdp', 'tensor'), may hold values from -0.125 to 0.125
- vector_outer: float32 [12, 1024], replicated, may hold values from -0.625 to 0.625
Outputs:
- block_output: bfloat16 [4, 2, 8, 577, 1024], P('group', None, ('fsdp', 'tensor'))
- patches_grad: float32 [4, 2, 8, 577, 1024], P('group', None, ('fsdp', 'tensor'))
- attn_inner: float32 [4, 2, 4, 1024, 1024], P('group', None, None, 'fsdp', 'tensor')
- attn_state: float32 [3, 4, 1024, 1024], P(None, None, 'fsdp', 'tensor')
- attn_copy: bfloat16 [4, 1024, 1024], P(None, 'fsdp', 'tensor')
- mlp_inner: float32 [4, 2, 2, 1024, 4096], P('group', None, None, 'fsdp', 'tensor')
- mlp_state: float32 [3, 2, 1024, 4096], P(None, None, 'fsdp', 'tensor')
- mlp_copy: bfloat16 [2, 1024, 4096], P(None, 'fsdp', 'tensor')
- vector_inner: float32 [4, 2, 12, 1024], P('group')
- vector_state: float32 [3, 12, 1024], replicated
- vector_copy: bfloat16 [12, 1024], replicated
Inputs may be any that keep to these rules, and one draw needn't show every extreme that they name: live_counts[g, m, f] images are live, and they stand first, among the f-th block of 4 image slots of micro-batch m in group g; some entry equals 4. `attn_moments`: second moments are positive. `mlp_moments`: second moments are positive. `vector_moments`: second moments are positive.
All inputs are finite; a program needn't handle non-finite values.
Results may differ from a plain program's by a relative error of at most 0.012.
The roundings to bfloat16 on the way count: a program that leaves them out, or rounds other values in their place, can miss the bound.
Values may be sent and summed in bfloat16 or wider, within the bound.
A program may use at most 320 MiB of HBM per device.

v0:
```python
import functools

import jax
import jax.numpy as jnp
from jax import lax
from jax.experimental import pallas as pl
from jax.experimental.pallas import tpu as pltpu
from jax.sharding import PartitionSpec as P

HD = 64
STEP = 8
IMG_DEV = 4
EPSILON = 1e-06
INNER_RATE = 0.02
VECTOR_RATE = 0.2
WEIGHT_DECAY = 0.1
OUTER_RATE = 0.7
OUTER_MOMENTUM = 0.9
PIECES = ((0, 256), (256, 256), (512, 512))
PARTS = 2
LOW = jnp.bfloat16
F32 = jnp.float32
NN = (((1,), (0,)), ((), ()))
NT = (((1,), (1,)), ((), ()))
TN = (((0,), (0,)), ((), ()))


def dot(a, b, dims=NN):
    return lax.dot_general(a, b, dims, preferred_element_type=F32)


MESH = pl.DeviceIdType.MESH


def params(identity=None):
    if identity is None:
        return pltpu.CompilerParams(vmem_limit_bytes=60 * 2**20)
    return pltpu.CompilerParams(vmem_limit_bytes=60 * 2**20, collective_id=identity, has_side_effects=True)


def partner():
    return (lax.axis_index("group"), 1 - lax.axis_index("fsdp"), lax.axis_index("tensor"))


def greet_partner():
    barrier = pltpu.get_barrier_semaphore()
    pl.semaphore_signal(barrier, inc=1, device_id=partner(), device_id_type=MESH)
    pl.semaphore_wait(barrier, 1)


def to_partner(sent, received, sends, receives, n):
    return pltpu.make_async_remote_copy(
        src_ref=sent.at[n],
        dst_ref=received.at[n],
        send_sem=sends.at[n],
        recv_sem=receives.at[n],
        device_id=partner(),
        device_id_type=MESH,
    )


def bands(depth):
    f = lax.axis_index("fsdp")
    return pl.ds(pl.multiple_of(f * depth, depth), depth), pl.ds(pl.multiple_of((1 - f) * depth, depth), depth)


def exchange_scratch(steps, shape):
    dma = pltpu.SemaphoreType.DMA
    return [
        pltpu.VMEM((steps, *shape), F32),
        pltpu.VMEM((steps, *shape), LOW),
        pltpu.VMEM((steps, *shape), LOW),
        dma((steps,)),
        dma((steps,)),
    ]


def cost(flops, moved, special=0):
    return pl.CostEstimate(flops=int(flops), bytes_accessed=int(moved), transcendentals=int(special))


def padded(rows):
    return -(-rows // 16) * 16


def centred(source):
    centre = source - jnp.mean(source, axis=-1, keepdims=True)
    spread = jnp.mean(centre * centre, axis=-1, keepdims=True)
    inverse = lax.rsqrt(spread + EPSILON)
    return centre * inverse, inverse


def norm_back(upstream, normal, inverse, gain):
    pulled = upstream * gain
    mean_one = jnp.mean(pulled, axis=-1, keepdims=True)
    mean_two = jnp.mean(pulled * normal, axis=-1, keepdims=True)
    return inverse * (pulled - mean_one - normal * mean_two)


def project_kernel(images, seq, x_ref, w_ref, vec_ref, n_ref, out_ref, n_scr):
    j, t = pl.program_id(0), pl.program_id(1)
    span = n_scr.shape[0] // images

    @pl.when((j == 0) & (t == 0))
    def _():
        n_scr[...] = jnp.zeros_like(n_scr)
        for i in range(images):
            normal, _ = centred(x_ref[i].astype(F32))
            n_scr[pl.ds(i * span, seq), :] = (normal * vec_ref[0:1] + vec_ref[1:2]).astype(LOW)
        n_ref[...] = n_scr[...]

    cols = out_ref.shape[-1]
    out = dot(n_scr[...], w_ref[0, 0])
    at = pl.ds(pl.multiple_of(t * cols, cols), cols)
    bias = jnp.where(j == 0, vec_ref[4:5, at], jnp.where(j == 2, vec_ref[5:6, at], 0.0))
    out_ref[0] = (out + bias).astype(LOW)


def project(patches, w_attn, vec):
    images, seq, width = patches.shape
    shards, _, _, cols = w_attn.shape
    rows = images * padded(seq)
    return pl.pallas_call(
        functools.partial(project_kernel, images, seq),
        grid=(3, shards),
        in_specs=[
            pl.BlockSpec((images, seq, width), lambda j, t: (0, 0, 0)),
            pl.BlockSpec((1, 1, width, cols), lambda j, t: (t, j, 0, 0)),
            pl.BlockSpec(vec.shape, lambda j, t: (0, 0)),
        ],
        out_specs=[
            pl.BlockSpec((rows, width), lambda j, t: (0, 0)),
            pl.BlockSpec((1, rows, cols), lambda j, t: (j, 0, t)),
        ],
        out_shape=[
            jax.ShapeDtypeStruct((rows, width), LOW),
            jax.ShapeDtypeStruct((3, rows, width), LOW),
        ],
        scratch_shapes=[pltpu.VMEM((rows, width), LOW)],
        compiler_params=params(),
        cost_estimate=cost(6 * rows * width * width, 16 * rows * width),
        name="project",
    )(patches, w_attn, vec)


def half_lanes(value, which):
    lane = lax.broadcasted_iota(jnp.int32, value.shape, 1)
    return jnp.where((lane >= HD) == bool(which), value, jnp.zeros_like(value))


def attend_kernel(seq, q_ref, k_ref, v_ref, out_ref):
    span = q_ref.shape[1]
    scale = HD**-0.5
    q, k, v = q_ref[0], k_ref[0], v_ref[0]
    parts = []
    for h in range(2):
        scores = dot(q, half_lanes(k, h), NT)
        lane = lax.broadcasted_iota(jnp.int32, scores.shape, 1)
        scores = jnp.where(lane < seq, scores, -1e30)
        top = jnp.max(scores, axis=1, keepdims=True)
        raised = jnp.exp((scores - top) * scale)
        total = jnp.sum(raised, axis=1, keepdims=True)
        probs = (raised * (1.0 / total)).astype(LOW)
        parts.append(dot(probs, v))
    lane = lax.broadcasted_iota(jnp.int32, (span, 2 * HD), 1)
    out_ref[...] = jnp.where(lane < HD, parts[0], parts[1]).astype(LOW)


def attend(qkv, images, seq):
    _, rows, width = qkv.shape
    span = rows // images
    pair = 2 * HD

    def take(j):
        return pl.BlockSpec((1, span, pair), lambda i, h: (j, i, h))

    return pl.pallas_call(
        functools.partial(attend_kernel, seq),
        grid=(images, width // pair),
        in_specs=[take(0), take(1), take(2)],
        out_specs=pl.BlockSpec((span, pair), lambda i, h: (i, h)),
        out_shape=jax.ShapeDtypeStruct((rows, width), LOW),
        compiler_params=params(),
        cost_estimate=cost(16 * rows * span * width, 8 * rows * width, rows * span * (width // HD)),
        name="attend",
    )(qkv, qkv, qkv)


def mix_kernel(seq, alive_ref, att_ref, x_ref, g_ref, w_ref, vec_ref, resid_ref, n_ref, g2_ref, x_scr):
    i = pl.program_id(0)
    shards, _, _, cols = w_ref.shape
    x_scr[...] = jnp.zeros_like(x_scr)
    x_scr[0:seq, :] = x_ref[0].astype(F32)
    total = x_scr[...] + vec_ref[6:7]
    for t in range(shards):
        total = total + dot(att_ref[:, t * cols : (t + 1) * cols], w_ref[t, 0], NT)
    resid_ref[...] = total
    normal, _ = centred(total)
    n_ref[...] = (normal * vec_ref[2:3] + vec_ref[3:4]).astype(LOW)
    x_scr[0:seq, :] = g_ref[0].astype(F32) * alive_ref[i]
    g2_ref[...] = x_scr[...].astype(LOW)


def mix(alive, attended, patches, cotangent, w_attn, vec):
    images, seq, width = patches.shape
    rows = attended.shape[0]
    span = rows // images
    shards, _, _, cols = w_attn.shape
    block = pl.BlockSpec((span, width), lambda i: (i, 0))
    whole = jax.ShapeDtypeStruct((rows, width), LOW)
    return pl.pallas_call(
        functools.partial(mix_kernel, seq),
        grid=(images,),
        in_specs=[
            pl.BlockSpec(memory_space=pltpu.SMEM),
            block,
            pl.BlockSpec((1, seq, width), lambda i: (i, 0, 0)),
            pl.BlockSpec((1, seq, width), lambda i: (i, 0, 0)),
            pl.BlockSpec((shards, 1, width, cols), lambda i: (0, 3, 0, 0)),
            pl.BlockSpec(vec.shape, lambda i: (0, 0)),
        ],
        out_specs=[block, block, block],
        out_shape=[jax.ShapeDtypeStruct((rows, width), F32), whole, whole],
        scratch_shapes=[pltpu.VMEM((span, width), F32)],
        compiler_params=params(),
        cost_estimate=cost(2 * rows * width * width, 16 * rows * width),
        name="mix",
    )(alive, attended, patches, cotangent, w_attn, vec)


def mlp_kernel(first, pairwise, n_ref, g_ref, w1_ref, w2_ref, bias_ref, *refs):
    if not first:
        yi_ref, gi_ref, *refs = refs
    y_ref, gn_ref, dw_ref, db_ref, h_scr, p_scr, loaded, *exchange = refs
    step = pl.program_id(0)
    each, _, width, cols = w1_ref.shape
    if not first:
        loads = (
            pltpu.make_async_copy(yi_ref, y_ref, loaded.at[0]),
            pltpu.make_async_copy(gi_ref, gn_ref, loaded.at[1]),
        )

    @pl.when(step == 0)
    def _():
        if not first:
            for load in loads:
                load.start()
        else:
            y_ref[...] = jnp.zeros_like(y_ref)
            gn_ref[...] = jnp.zeros_like(gn_ref)
        if pairwise:
            greet_partner()

    w1 = jnp.concatenate([w1_ref[t, 0] for t in range(each)], axis=1)
    w2 = jnp.concatenate([w2_ref[t, 0] for t in range(each)], axis=1)
    bias = jnp.concatenate([bias_ref[t] for t in range(each)], axis=1)
    pre = dot(n_ref[...], w1) + bias
    cdf = 0.5 * (1.0 + lax.erf(pre * 0.7071067811865476))
    h_scr[...] = (pre * cdf).astype(LOW)
    slope = cdf + pre * jnp.exp(-0.5 * pre * pre) * 0.3989422804014327
    p_scr[...] = (dot(g_ref[...], w2) * slope).astype(LOW)
    sums = jnp.sum(p_scr[...].astype(F32), axis=0, keepdims=True)
    for t in range(each):
        db_ref[t] = sums[:, t * cols : (t + 1) * cols]

    if pairwise:
        own, sent, received, sends, receives = exchange
        ours, theirs = bands(width // 2)

        slot = lax.rem(step, 2)

        def collect(n):
            at = lax.rem(n, 2)
            to_partner(sent, received, sends, receives, at).wait()
            for which in range(2):
                total = (own[at, which] + received[at, which].astype(F32)).astype(LOW)
                for t in range(each):
                    dw_ref[n * each + t, which] = total[:, t * cols : (t + 1) * cols]

        @pl.when(step > 0)
        def _():
            collect(step - 1)

        sent[slot, 0] = dot(n_ref[:, theirs], p_scr[...], TN).astype(LOW)
        sent[slot, 1] = dot(g_ref[:, theirs], h_scr[...], TN).astype(LOW)
        to_partner(sent, received, sends, receives, slot).start()
        own[slot, 0] = dot(n_ref[:, ours], p_scr[...], TN)
        own[slot, 1] = dot(g_ref[:, ours], h_scr[...], TN)

    else:
        shards, depth = dw_ref.shape[0], dw_ref.shape[3]
        d1 = dot(n_ref[...], p_scr[...], TN).astype(LOW)
        d2 = dot(g_ref[...], h_scr[...], TN).astype(LOW)
        for f in range(shards):
            for t in range(each):
                dw_ref[f, t, 0] = d1[f * depth : (f + 1) * depth, t * cols : (t + 1) * cols]
                dw_ref[f, t, 1] = d2[f * depth : (f + 1) * depth, t * cols : (t + 1) * cols]

    if not first:

        @pl.when(step == 0)
        def _():
            for load in loads:
                load.wait()

    y_ref[...] += dot(h_scr[...], w2, NT)
    gn_ref[...] += dot(p_scr[...], w1, NT)
    if pairwise:

        @pl.when(step == pl.num_programs(0) - 1)
        def _():
            collect(step)


def mlp(part, start, cols, normed, grad_two, w_mlp, bias, carried, fsdp):
    rows, width = normed.shape
    shards = w_mlp.shape[0]
    each = max(512 // cols, 1)
    at = start // cols
    first, pairwise = carried is None, fsdp == 2
    single = pl.Buffered(1)
    full = pl.BlockSpec((rows, width), lambda s: (0, 0), pipeline_mode=single)
    depth = width // fsdp
    steps = shards // each
    acc_shape = jax.ShapeDtypeStruct((rows, width), F32)
    if pairwise:
        out_w = pl.BlockSpec((shards, 2, depth, cols), lambda s: (0, 0, 0, 0), pipeline_mode=single)
        w_shape = jax.ShapeDtypeStruct((shards, 2, depth, cols), LOW)
        extra = exchange_scratch(2, (2, depth, each * cols))
    else:
        out_w = pl.BlockSpec((fsdp, each, 2, depth, cols), lambda s: (0, s, 0, 0, 0))
        w_shape = jax.ShapeDtypeStruct((fsdp, shards, 2, depth, cols), LOW)
        extra = []
    return pl.pallas_call(
        functools.partial(mlp_kernel, first, pairwise),
        grid=(steps,),
        in_specs=[
            full,
            full,
            pl.BlockSpec((each, 1, width, cols), lambda s: (s, 0, 0, at)),
            pl.BlockSpec((each, 1, width, cols), lambda s: (s, 1, 0, at)),
            pl.BlockSpec((each, 1, cols), lambda s: (s, 0, at)),
        ]
        + ([] if first else [pl.BlockSpec(memory_space=pl.ANY)] * 2),
        out_specs=[full, full, out_w, pl.BlockSpec((each, 1, cols), lambda s: (s, 0, 0))],
        out_shape=[acc_shape, acc_shape, w_shape, jax.ShapeDtypeStruct((shards, 1, cols), F32)],
        scratch_shapes=[
            pltpu.VMEM((rows, each * cols), LOW),
            pltpu.VMEM((rows, each * cols), LOW),
            pltpu.SemaphoreType.DMA((2,)),
            *extra,
        ],
        compiler_params=params(2 + part if pairwise else None),
        cost_estimate=cost(12 * rows * width * cols * shards, 24 * rows * width),
        name=f"mlp_{part}",
    )(normed, grad_two, w_mlp, w_mlp, bias, *([] if first else carried))


def turn_kernel(seq, pairwise, alive_ref, resid_ref, y_ref, gn_ref, g2_ref, att_ref, w_ref, vec_ref,
                out_ref, gr_ref, ga_ref, dw_ref, sums_ref, dw_scr, *exchange):
    i = pl.program_id(0)
    if pairwise:
        pl.when(i == 0)(greet_partner)
    shards, _, _, cols = w_ref.shape
    resid = resid_ref[...]
    out_ref[0] = ((resid + y_ref[...] + vec_ref[7:8]) * alive_ref[i]).astype(LOW)[0:seq]
    normal, inverse = centred(resid)
    upstream = gn_ref[...]
    grad_out = g2_ref[...].astype(F32)
    grad_resid = grad_out + norm_back(upstream, normal, inverse, vec_ref[2:3])
    gr_ref[...] = grad_resid
    low = grad_resid.astype(LOW)
    rows = [
        jnp.sum(upstream * normal, axis=0, keepdims=True),
        jnp.sum(upstream, axis=0, keepdims=True),
        jnp.sum(grad_resid, axis=0, keepdims=True),
        jnp.sum(grad_out, axis=0, keepdims=True),
    ]
    rows = jnp.concatenate(rows, axis=0)

    @pl.when(i == 0)
    def _():
        sums_ref[...] = rows

    @pl.when(i != 0)
    def _():
        sums_ref[...] += rows

    for t in range(shards):
        ga_ref[:, t * cols : (t + 1) * cols] = dot(low, w_ref[t, 0]).astype(LOW)
    part = dot(low, att_ref[...], TN)

    @pl.when(i == 0)
    def _():
        dw_scr[...] = part

    @pl.when(i != 0)
    def _():
        dw_scr[...] += part

    @pl.when(i == pl.num_programs(0) - 1)
    def _():
        if pairwise:
            sent, received, sends, receives = exchange
            ours, theirs = bands(dw_scr.shape[0] // 2)
            sent[0] = dw_scr[theirs, :].astype(LOW)
            copy = to_partner(sent, received, sends, receives, 0)
            copy.start()
            copy.wait()
            total = (dw_scr[ours, :] + received[0].astype(F32)).astype(LOW)
            for t in range(shards):
                dw_ref[t, 0] = total[:, t * cols : (t + 1) * cols]
            return
        depth = dw_ref.shape[3]
        for f in range(dw_ref.shape[0]):
            for t in range(shards):
                dw_ref[f, t, 0] = dw_scr[f * depth : (f + 1) * depth, t * cols : (t + 1) * cols].astype(LOW)


def turn(alive, resid, branch, grad_normed, grad_two, attended, w_attn, vec, images, seq, fsdp):
    rows, width = resid.shape
    span = rows // images
    shards, _, _, cols = w_attn.shape
    depth = width // fsdp
    pairwise = fsdp == 2
    lead = () if pairwise else (fsdp,)
    block = pl.BlockSpec((span, width), lambda i: (i, 0))
    return pl.pallas_call(
        functools.partial(turn_kernel, seq, pairwise),
        grid=(images,),
        in_specs=[
            pl.BlockSpec(memory_space=pltpu.SMEM),
            block, block, block, block, block,
            pl.BlockSpec((shards, 1, width, cols), lambda i: (0, 3, 0, 0)),
            pl.BlockSpec(vec.shape, lambda i: (0, 0)),
        ],
        out_specs=[
            pl.BlockSpec((1, seq, width), lambda i: (i, 0, 0)),
            block, block,
            pl.BlockSpec((*lead, shards, 1, depth, cols), lambda i: (0,) * (4 + len(lead))),
            pl.BlockSpec((4, width), lambda i: (0, 0)),
        ],
        out_shape=[
            jax.ShapeDtypeStruct((images, seq, width), LOW),
            jax.ShapeDtypeStruct((rows, width), F32),
            jax.ShapeDtypeStruct((rows, width), LOW),
            jax.ShapeDtypeStruct((*lead, shards, 1, depth, cols), LOW),
            jax.ShapeDtypeStruct((4, width), F32),
        ],
        scratch_shapes=[pltpu.VMEM((width, width), F32)] + (exchange_scratch(1, (depth, width))[1:] if pairwise else []),
        compiler_params=params(6 if pairwise else None),
        cost_estimate=cost(4 * rows * width * width, 24 * rows * width),
        name="turn",
    )(alive, resid, branch, grad_normed, grad_two, attended, w_attn, vec)


def unattend_kernel(seq, q_ref, k_ref, v_ref, g_ref, dq_ref, dk_ref, dv_ref):
    span = q_ref.shape[1]
    scale = HD**-0.5
    q, k, v, g = q_ref[0], k_ref[0], v_ref[0], g_ref[...]
    parts = []
    for h in range(2):
        scores = dot(half_lanes(k, h), q, NT)
        row = lax.broadcasted_iota(jnp.int32, scores.shape, 0)
        scores = jnp.where(row < seq, scores, -1e30)
        top = jnp.max(scores, axis=0, keepdims=True)
        raised = jnp.exp((scores - top) * scale)
        total = jnp.sum(raised, axis=0, keepdims=True)
        probs = raised * (1.0 / total)
        gp = dot(half_lanes(v, h), g, NT)
        delta = jnp.sum(probs * gp, axis=0, keepdims=True)
        gs = (probs * (gp - delta)).astype(LOW)
        dv = dot(probs.astype(LOW), g)
        dk = dot(gs, q)
        dq = dot(gs, k, TN)
        parts.append((dq, dk, dv))
    lane = lax.broadcasted_iota(jnp.int32, (span, 2 * HD), 1) < HD
    dq_ref[0] = (jnp.where(lane, parts[0][0], parts[1][0]) * scale).astype(LOW)
    dk_ref[0] = (jnp.where(lane, parts[0][1], parts[1][1]) * scale).astype(LOW)
    dv_ref[0] = jnp.where(lane, parts[0][2], parts[1][2]).astype(LOW)


def unattend(qkv, grad_attended, images, seq, part, parts, shards):
    _, rows, width = qkv.shape
    span = rows // images
    pair = 2 * HD
    each = width // shards // parts // pair

    def spot(h):
        return (h // each) * (each * parts) + part * each + h % each

    def take(j):
        return pl.BlockSpec((1, span, pair), lambda i, h: (j, i, spot(h)))

    out = pl.BlockSpec((1, span, pair), lambda i, h: (0, i, h))
    shape = jax.ShapeDtypeStruct((1, rows, width // parts), LOW)
    return pl.pallas_call(
        functools.partial(unattend_kernel, seq),
        grid=(images, width // pair // parts),
        in_specs=[take(0), take(1), take(2), pl.BlockSpec((span, pair), lambda i, h: (i, spot(h)))],
        out_specs=[out, out, out],
        out_shape=[shape, shape, shape],
        compiler_params=params(),
        cost_estimate=cost(
            40 * rows * span * width // parts, 14 * rows * width // parts, rows * span * (width // HD) // parts
        ),
        name=f"unattend_{part}",
    )(qkv, qkv, qkv, grad_attended)


def close_kernel(seq, images, pairwise, groups, first, final, n_ref, dq_ref, dk_ref, dv_ref, w_ref, *refs):
    if not first:
        carry_ref, *refs = refs
    elif pairwise:
        more_ref, *refs = refs
    if final:
        x_ref, gr_ref, vec_ref, *refs = refs
        if pairwise:
            diff_ref, *refs = refs
        out_ref, norm_ref, *refs = refs
        if pairwise:
            total_ref, *refs = refs
    else:
        acc_ref, *refs = refs
    dw_ref, sums_ref, acc_scr, *exchange = refs
    j = pl.program_id(0)
    shards, _, _, cols = w_ref.shape
    span = n_ref.shape[0] // images
    if pairwise:
        own, sent, received, sends, receives, *exchange = exchange
        if not final:
            pl.when(j == 0)(greet_partner)
    if pairwise and final:
        mine, landed, sends_two, receives_two, loaded = exchange
        g, f, t = lax.axis_index("group"), lax.axis_index("fsdp"), lax.axis_index("tensor")
        quarter = landed.shape[1]

        def rows(n):
            return pl.ds(pl.multiple_of(n * quarter, quarter), quarter)

        def other(k):
            return (lax.rem(g + k, groups), f, t)

        def part(k):
            return pltpu.make_async_remote_copy(
                src_ref=diff_ref.at[rows(lax.rem(g + k, groups)), :],
                dst_ref=landed.at[k],
                send_sem=sends_two.at[k],
                recv_sem=receives_two.at[k],
                device_id=other(k),
                device_id_type=MESH,
            )

        keep = pltpu.make_async_copy(diff_ref.at[rows(g), :], mine, loaded.at[0])

        @pl.when(j == 0)
        def _():
            barrier = pltpu.get_barrier_semaphore()
            pl.semaphore_signal(barrier, inc=1, device_id=partner(), device_id_type=MESH)
            for k in range(1, groups):
                pl.semaphore_signal(barrier, inc=1, device_id=other(k), device_id_type=MESH)
            pl.semaphore_wait(barrier, groups)
            for k in range(1, groups):
                part(k).start()
            keep.start()

    @pl.when(j == 0)
    def _():
        acc_scr[...] = jnp.zeros_like(acc_scr) if first else carry_ref[...]
        sums_ref[0:1, :] = jnp.sum(dq_ref[0].astype(F32), axis=0, keepdims=True)
        sums_ref[1:2, :] = jnp.sum(dv_ref[0].astype(F32), axis=0, keepdims=True)

    def spread(n, total, f=None):
        for t in range(shards):
            piece = total[:, t * cols : (t + 1) * cols]
            if f is None:
                dw_ref[t, n] = piece
            else:
                dw_ref[f, t, 0] = piece

    def step(ref):
        weight = jnp.concatenate([w_ref[t, 0] for t in range(shards)], axis=1)
        if pairwise:
            ours, theirs = bands(n_ref.shape[1] // 2)
            sent[j] = dot(n_ref[:, theirs], ref[0], TN).astype(LOW)
            to_partner(sent, received, sends, receives, j).start()
            own[j] = dot(n_ref[:, ours], ref[0], TN)
        else:
            depth = dw_ref.shape[3]
            dw = dot(n_ref[...], ref[0], TN).astype(LOW)
            for f in range(dw_ref.shape[0]):
                spread(0, dw[f * depth : (f + 1) * depth], f)
        acc_scr[...] += dot(ref[0], weight, NT)

    @pl.when(j == 0)
    def _():
        step(dq_ref)

    @pl.when(j == 1)
    def _():
        step(dk_ref)

    @pl.when(j == 2)
    def _():
        step(dv_ref)
        if pairwise:
            for n in range(own.shape[0]):
                to_partner(sent, received, sends, receives, n).wait()
                spread(n, (own[n] + received[n].astype(F32)).astype(LOW))
            if first:
                for t in range(shards):
                    for n in range(dw_ref.shape[1] - 3):
                        dw_ref[t, 3 + n] = more_ref[t, 0, :, n * cols : (n + 1) * cols]
        if not final:
            acc_ref[...] = acc_scr[...]
            return
        gain = jnp.zeros((1, vec_ref.shape[1]), F32)
        shift = jnp.zeros((1, vec_ref.shape[1]), F32)
        for i in range(images):
            normal, inverse = centred(x_ref[i].astype(F32))
            upstream = acc_scr[i * span : i * span + seq, :]
            out_ref[i, :, 0, :] = gr_ref[i * span : i * span + seq, :] + norm_back(upstream, normal, inverse, vec_ref[0:1])
            gain += jnp.sum(upstream * normal, axis=0, keepdims=True)
            shift += jnp.sum(upstream, axis=0, keepdims=True)
        norm_ref[0:1, :] = gain
        norm_ref[1:2, :] = shift
        if pairwise:
            keep.wait()
            total = mine[...].astype(F32)
            for k in range(1, groups):
                part(k).wait()
                total = total + landed[k].astype(F32)
            total_ref[...] = total.astype(LOW)


def close(part, parts, normed, grads, w_attn, carry, more, ending, fsdp, groups, images, seq):
    rows, width = normed.shape
    shards, _, _, cols = w_attn.shape
    cols = cols // parts
    lanes = shards * cols
    depth = width // fsdp
    pairwise, first, final = fsdp == 2, carry is None, ending is not None
    single = pl.Buffered(1)
    stack = pl.BlockSpec((1, rows, lanes), lambda j: (0, 0, 0), pipeline_mode=single)
    full = pl.BlockSpec((rows, width), lambda j: (0, 0), pipeline_mode=single)
    image = pl.BlockSpec((images, seq, width), lambda j: (0, 0, 0), pipeline_mode=single)
    if pairwise:
        many = 3 + parts if first else 3
        dw_spec = pl.BlockSpec((shards, many, depth, cols), lambda j: (0, 0, 0, 0), pipeline_mode=single)
        dw_shape = jax.ShapeDtypeStruct((shards, many, depth, cols), LOW)
        extra = exchange_scratch(3, (depth, lanes))
    else:
        dw_spec = pl.BlockSpec((fsdp, shards, 1, depth, cols), lambda j: (0, 0, j, 0, 0))
        dw_shape = jax.ShapeDtypeStruct((fsdp, shards, 3, depth, cols), LOW)
        extra = []
    in_specs = [full, stack, stack, stack, pl.BlockSpec((shards, 1, width, cols), lambda j: (0, j, 0, part))]
    out_specs, out_shape = [], []
    if not first:
        in_specs.append(full)
    elif pairwise:
        in_specs.append(pl.BlockSpec(more.shape, lambda j: (0, 0, 0, 0), pipeline_mode=single))
    if final:
        in_specs += [image, full, pl.BlockSpec((12, width), lambda j: (0, 0))]
        flat = pl.BlockSpec((images, seq, 1, width), lambda j: (0, 0, 0, 0), pipeline_mode=single)
        out_specs += [flat, pl.BlockSpec((2, width), lambda j: (0, 0))]
        out_shape += [jax.ShapeDtypeStruct((images, seq, 1, width), F32), jax.ShapeDtypeStruct((2, width), F32)]
        if pairwise:
            quarter, lanes_two = ending[3].shape[0] // groups, ending[3].shape[1]
            in_specs.append(pl.BlockSpec(memory_space=pl.ANY))
            out_specs.append(pl.BlockSpec((quarter, lanes_two), lambda j: (0, 0), pipeline_mode=single))
            out_shape.append(jax.ShapeDtypeStruct((quarter, lanes_two), LOW))
            dma = pltpu.SemaphoreType.DMA
            extra = [
                *extra,
                pltpu.VMEM((quarter, lanes_two), LOW),
                pltpu.VMEM((groups, quarter, lanes_two), LOW),
                dma((groups,)),
                dma((groups,)),
                dma((1,)),
            ]
    else:
        out_specs.append(full)
        out_shape.append(jax.ShapeDtypeStruct((rows, width), F32))
    return pl.pallas_call(
        functools.partial(close_kernel, seq, images, pairwise, groups, first, final),
        grid=(3,),
        in_specs=in_specs,
        out_specs=[*out_specs, dw_spec, pl.BlockSpec((2, lanes), lambda j: (0, 0))],
        out_shape=[*out_shape, dw_shape, jax.ShapeDtypeStruct((2, lanes), F32)],
        scratch_shapes=[pltpu.VMEM((rows, width), F32), *extra],
        compiler_params=params(7 + part if pairwise else None),
        cost_estimate=cost(12 * rows * width * lanes, 20 * rows * width),
        name=f"close_{part}",
    )(normed, *grads, w_attn, *([carry] if not first else [more] if pairwise else []), *(ending if final else []))


def attend_pair(seq, q, k, v):
    scale = HD**-0.5
    parts = []
    for h in range(2):
        scores = dot(q, half_lanes(k, h), NT)
        lane = lax.broadcasted_iota(jnp.int32, scores.shape, 1)
        scores = jnp.where(lane < seq, scores, -1e30)
        top = jnp.max(scores, axis=1, keepdims=True)
        raised = jnp.exp((scores - top) * scale)
        total = jnp.sum(raised, axis=1, keepdims=True)
        probs = (raised * (1.0 / total)).astype(LOW)
        parts.append(dot(probs, v))
    lane = lax.broadcasted_iota(jnp.int32, parts[0].shape, 1)
    return jnp.where(lane < HD, parts[0], parts[1]).astype(LOW)


def front_kernel(
    images, seq, alive_ref, a_in, m_in, x_ref, g_ref, vec_ref,
    a_out, m_out, n_out, qkv_out, att_out, resid_out, n2_out, g2_out,
    a_wide, m_wide, a_hold, m_hold, n_scr, qkv_scr, att_scr, w_scr, o_scr, x_scr, resid_scr, n2_scr, g2_scr,
    zs, zr, xs, xr, ys, yr, xfs, xfr, yfs, yfr, cs, cr, ls, ws,
):
    g, f, z = lax.axis_index("group"), lax.axis_index("fsdp"), lax.axis_index("tensor")
    shards = lax.axis_size("tensor")
    last = shards - 1
    x_at, y_at = g % 2, g // 2
    east, north = y_at * 2 + (1 - x_at), (1 - y_at) * 2 + x_at
    depth, cols = a_in.shape[1:]
    band = depth // 4
    shared = band * 3 // 8
    rest = band - 2 * shared
    span = n_scr.shape[0] // images

    def place(column):
        cx, cy = column % 2, column // 2
        return 2 * (cx + cy - 2 * cx * cy) + cy

    mine, of_east, of_north = place(g), place(east), place(north)
    z_row = mine * band - shared * (mine % 2)
    lead_east = of_east * band + shared * (of_east % 2)
    lead_north = of_north * band + shared * (of_north % 2)
    chunks = ((a_out, 0, 3), (a_out, 3, 1), (m_out, 0, 1), (m_out, 1, 1))

    def tile(n):
        return pl.multiple_of(n, 16)

    def held(n, t, row, rows):
        out, j, many = chunks[n]
        return out.at[t, pl.ds(j, many), pl.ds(tile(f * depth + row), rows), :]

    def send(part, sems, semr, n, t, to):
        return pltpu.make_async_remote_copy(
            src_ref=part, dst_ref=part, send_sem=sems.at[n, t], recv_sem=semr.at[n, t], device_id=to, device_id_type=MESH
        )

    def along(n, t, up):
        part = held(n, t, z_row, band + shared)
        return pltpu.make_async_remote_copy(
            src_ref=part,
            dst_ref=part,
            send_sem=zs.at[n, t, 0 if up else 1],
            recv_sem=zr.at[n, t],
            device_id=(g, f, z + 1 if up else z - 1),
            device_id_type=MESH,
        )

    def to_east(n, t):
        return send(held(n, t, mine * band, band), xs, xr, n, t, (east, f, z))

    def to_north(n, t):
        return send(held(n, t, mine * band, band), ys, yr, n, t, (north, f, z))

    def north_to_east(n, t):
        return send(held(n, t, lead_north, shared), xfs, xfr, n, t, (east, f, z))

    def east_to_north(n, t):
        return send(held(n, t, lead_east + shared, rest), yfs, yfr, n, t, (north, f, z))

    def across(n, t):
        return send(held(n, t, 0, depth), cs, cr, n, t, (g, 1 - f, z))

    rows = pl.ds(tile(f * depth), depth)
    loads = (
        pltpu.make_async_copy(a_in, a_wide, ls.at[0]),
        pltpu.make_async_copy(m_in, m_wide, ls.at[1]),
    )
    keeps = (
        pltpu.make_async_copy(a_hold, a_out.at[z, :, rows, :], ls.at[2]),
        pltpu.make_async_copy(m_hold, m_out.at[z, :, rows, :], ls.at[3]),
    )
    loads[0].start()

    barrier = pltpu.get_barrier_semaphore()

    def greet(to):
        pl.semaphore_signal(barrier, inc=1, device_id=to, device_id_type=MESH)

    for to in ((east, f, z), (north, f, z), (g, 1 - f, z)):
        greet(to)

    @pl.when(z > 0)
    def _():
        greet((g, f, z - 1))

    @pl.when(z < last)
    def _():
        greet((g, f, z + 1))

    loads[0].wait()
    a_hold[...] = a_wide[...].astype(LOW)
    keeps[0].start()
    pl.semaphore_wait(barrier, 3 + jnp.minimum(z, 1) + jnp.minimum(last - z, 1))
    keeps[0].wait()

    count = len(chunks)

    def when_real(k, up, run):
        @pl.when(z - k >= 0 if up else z + k <= last)
        def _():
            run(z - k if up else z + k)

    def own(n):
        @pl.when(z < last)
        def _():
            along(n, z, True).start()

        @pl.when(z > 0)
        def _():
            along(n, z, False).start()

        across(n, z).start()

    def land(n, k, up):
        def run(t):
            along(n, t, up).wait_recv()

            @pl.when(z < last if up else z > 0)
            def _():
                along(n, t, up).start()

            to_east(n, t).start()
            to_north(n, t).start()

        when_real(k, up, run)

    def relay(n, k, up):
        def run(t):
            to_east(n, t).wait_recv()
            east_to_north(n, t).start()
            to_north(n, t).wait_recv()
            north_to_east(n, t).start()

        when_real(k, up, run)

    def finish(n, k, up):
        def run(t):
            east_to_north(n, t).wait_recv()
            north_to_east(n, t).wait_recv()
            across(n, t).start()

        when_real(k, up, run)

    def both(run, n, k):
        for up in (True, False):
            run(n, k, up)

    def fetch(t):
        return pltpu.make_async_copy(a_out.at[t, pl.ds(0, 3)], w_scr, ws.at[0])

    def maps(t):
        across(0, t).wait_recv()
        fetch(t).start()
        fetch(t).wait()
        here = pl.ds(pl.multiple_of(t * cols, cols), cols)

        def body(j, carry):
            bias = jnp.where(j == 0, vec_ref[4:5, here], jnp.where(j == 2, vec_ref[5:6, here], 0.0))
            qkv_scr[j, :, here] = (dot(n_scr[...], w_scr[j]) + bias).astype(LOW)
            return carry

        lax.fori_loop(0, 3, body, 0)

    def project(n, k, up):
        when_real(k, up, maps)

    own(0)
    loads[1].start()
    n_scr[...] = jnp.zeros_like(n_scr)
    for i in range(images):
        normal, _ = centred(x_ref[i].astype(F32))
        n_scr[pl.ds(i * span, seq), :] = (normal * vec_ref[0:1] + vec_ref[1:2]).astype(LOW)
    puts = [pltpu.make_async_copy(n_scr, n_out, ws.at[1])]
    puts[0].start()
    both(land, 0, 1)
    loads[1].wait()
    m_hold[...] = m_wide[...].astype(LOW)
    keeps[1].start()
    maps(z)
    both(land, 0, 2)
    both(relay, 0, 1)
    keeps[1].wait()
    both(land, 0, 3)
    for n in range(1, count):
        own(n)
    both(relay, 0, 2)
    both(finish, 0, 1)
    both(relay, 0, 3)
    both(finish, 0, 2)
    both(project, 0, 1)
    both(finish, 0, 3)
    both(project, 0, 2)

    rest_items = [(n, k) for k in range(1, last + 1) for n in range(1, count)]
    total = len(rest_items) + 2

    def advance(at):
        if at < len(rest_items):
            both(land, *rest_items[at])
        if 0 <= at - 1 < len(rest_items):
            both(relay, *rest_items[at - 1])
        if 0 <= at - 2 < len(rest_items):
            both(finish, *rest_items[at - 2])

    advance(0)
    both(project, 0, 3)
    puts.append(pltpu.make_async_copy(qkv_scr, qkv_out, ws.at[2]))
    puts[-1].start()

    pair = 2 * HD
    pairs = qkv_scr.shape[2] // pair
    stretch = max(pairs // 4, 1)
    at = 1
    for i in range(images):
        for start in range(0, pairs, stretch):

            def body(h, carry):
                lanes = pl.ds(pl.multiple_of(h * pair, pair), pair)
                here = pl.ds(i * span, span)
                att_scr[here, lanes] = attend_pair(
                    seq, qkv_scr[0, here, lanes], qkv_scr[1, here, lanes], qkv_scr[2, here, lanes]
                )
                return carry

            lax.fori_loop(start, start + stretch, body, 0)
            if at < total:
                advance(at)
                at += 1
    puts.append(pltpu.make_async_copy(att_scr, att_out, ws.at[3]))
    puts[-1].start()
    while at < total - 2:
        advance(at)
        at += 1

    for t in range(shards):
        across(1, t).wait_recv()
    take = pltpu.make_async_copy(a_out.at[:, 3], o_scr, ws.at[0])
    take.start()
    take.wait()
    x_scr[...] = jnp.zeros_like(x_scr)
    for i in range(images):
        here = pl.ds(i * span, span)
        x_scr[0:seq, :] = x_ref[i].astype(F32)
        out = x_scr[...] + vec_ref[6:7]
        for t in range(shards):
            out = out + dot(att_scr[here, t * cols : (t + 1) * cols], o_scr[t], NT)
        resid_scr[here, :] = out
        normal, _ = centred(out)
        n2_scr[here, :] = (normal * vec_ref[2:3] + vec_ref[3:4]).astype(LOW)
        x_scr[0:seq, :] = g_ref[i].astype(F32) * alive_ref[i]
        g2_scr[here, :] = x_scr[...].astype(LOW)
        if at < total:
            advance(at)
            at += 1
    for n, (src, dst) in enumerate(((resid_scr, resid_out), (n2_scr, n2_out), (g2_scr, g2_out))):
        puts.append(pltpu.make_async_copy(src, dst, ws.at[4 + n]))
        puts[-1].start()
    while at < total:
        advance(at)
        at += 1
    for put in puts:
        put.wait()

    for n in range(count):
        @pl.when(z < last)
        def _():
            along(n, z, True).wait_send()

        @pl.when(z > 0)
        def _():
            along(n, z, False).wait_send()

        for t in range(shards):
            across(n, t).wait_send()
            if n > 1:
                across(n, t).wait_recv()

    def settle(n, k, up):
        def run(t):
            @pl.when(z < last if up else z > 0)
            def _():
                along(n, t, up).wait_send()

            to_east(n, t).wait_send()
            to_north(n, t).wait_send()
            east_to_north(n, t).wait_send()
            north_to_east(n, t).wait_send()

        when_real(k, up, run)

    for n in range(count):
        for k in range(1, last + 1):
            both(settle, n, k)


def front(alive, attn_master, mlp_master, patches, cotangent, vec, shards):
    _, depth, a_cols = attn_master.shape
    _, _, m_cols = mlp_master.shape
    images, seq, width = patches.shape
    rows = images * padded(seq)
    anywhere = pl.BlockSpec(memory_space=pl.ANY)
    inside = pl.BlockSpec(memory_space=pltpu.VMEM)
    dma = pltpu.SemaphoreType.DMA
    low = jax.ShapeDtypeStruct((rows, width), LOW)
    return pl.pallas_call(
        functools.partial(front_kernel, images, seq),
        in_specs=[pl.BlockSpec(memory_space=pltpu.SMEM), anywhere, anywhere, inside, inside, inside],
        out_specs=[anywhere] * 8,
        out_shape=[
            jax.ShapeDtypeStruct((shards, 4, width, a_cols), LOW),
            jax.ShapeDtypeStruct((shards, 2, width, m_cols), LOW),
            low,
            jax.ShapeDtypeStruct((3, rows, width), LOW),
            low,
            jax.ShapeDtypeStruct((rows, width), F32),
            low,
            low,
        ],
        scratch_shapes=[
            pltpu.VMEM(attn_master.shape, F32),
            pltpu.VMEM(mlp_master.shape, F32),
            pltpu.VMEM(attn_master.shape, LOW),
            pltpu.VMEM(mlp_master.shape, LOW),
            pltpu.VMEM((rows, width), LOW),
            pltpu.VMEM((3, rows, width), LOW),
            pltpu.VMEM((rows, width), LOW),
            pltpu.VMEM((3, width, a_cols), LOW),
            pltpu.VMEM((shards, width, a_cols), LOW),
            pltpu.VMEM((rows // images, width), F32),
            pltpu.VMEM((rows, width), F32),
            pltpu.VMEM((rows, width), LOW),
            pltpu.VMEM((rows, width), LOW),
            dma((4, shards, 2)),
        ]
        + [dma((4, shards))] * 11
        + [dma((4,)), dma((7,))],
        compiler_params=params(1),
        cost_estimate=cost(8 * rows * width * width, 30 * rows * width),
        name="front",
    )(alive, attn_master, mlp_master, patches, cotangent, vec)


def inner_adamw(master, gradient, first, second, step_rate, decay_rate):
    first_moment = 0.9 * first + 0.1 * gradient
    second_moment = 0.95 * second + 0.05 * gradient * gradient
    step_ratio = (
        first_moment / (1.0 - 0.9**STEP) / (jnp.sqrt(second_moment / (1.0 - 0.95**STEP)) + 1e-08)
    )
    return (master - step_rate * (step_ratio + decay_rate * master), second_moment)


def outer_nesterov(master, outer_old, difference):
    momentum = OUTER_MOMENTUM * outer_old + difference
    return momentum, master - OUTER_RATE * (difference + OUTER_MOMENTUM * momentum)


def inner_kernel(join, count, *refs):
    pieces, (master_ref, moment_ref, *_, inner_ref, diff_ref) = refs[:count], refs[count:]
    gradient = join(*[piece[0] for piece in pieces]).astype(F32)
    master = master_ref[0]
    new, second = inner_adamw(master, gradient, moment_ref[0, 0, 0], moment_ref[0, 1, 0], INNER_RATE, WEIGHT_DECAY)
    inner_ref[0, 0, 0] = gradient
    inner_ref[0, 1, 0] = second
    diff_ref[0] = (master - new).astype(LOW)


def inner_step(join, pieces, unit, units, cols, master, moments, into, name):
    depth = master.shape[1]
    rows = min(depth, 524288 // cols)
    block = pl.BlockSpec((1, rows, cols), lambda u, r: (unit(u)[0], r, unit(u)[1]))
    both = pl.BlockSpec((1, 2, 1, rows, cols), lambda u, r: (0, 0, unit(u)[0], r, unit(u)[1]))
    piece_specs = [pl.BlockSpec((1, rows, piece.shape[2]), lambda u, r: (u, r, 0)) for piece in pieces]
    count = len(pieces)
    return pl.pallas_call(
        functools.partial(inner_kernel, join, count),
        grid=(units, depth // rows),
        in_specs=[*piece_specs, block, both] + ([] if into is None else [pl.BlockSpec(memory_space=pl.ANY)]),
        out_specs=[both, pl.BlockSpec((1, rows, cols), lambda u, r: (u, r, 0))],
        out_shape=[
            jax.ShapeDtypeStruct(moments.shape, F32),
            jax.ShapeDtypeStruct((units, depth, cols), LOW),
        ],
        input_output_aliases={} if into is None else {count + 2: 0},
        compiler_params=params(),
        cost_estimate=cost(30 * units * depth * cols, 24 * units * depth * cols),
        name=name,
    )(*pieces, master, moments, *([] if into is None else [into]))


def outer_kernel(groups, slots, each, g_ref, *refs):
    totals, (master_ref, outer_ref, *_, state_ref, copy_ref) = refs[:slots], refs[slots:]
    rows = copy_ref.shape[1]
    if slots == 1:
        total = totals[0][0]
    else:
        at = pl.program_id(0) * pl.num_programs(1) + pl.program_id(1)
        slot = lax.rem(g_ref[0] + groups - at // each, groups)
        here = pl.ds(pl.multiple_of(lax.rem(at, each) * rows, rows), rows)
        total = totals[0][here, :]
        for n in range(1, slots):
            total = jnp.where(slot == n, totals[n][here, :], total)
    difference = total.astype(F32) / groups
    momentum, fresh = outer_nesterov(master_ref[0], outer_ref[0], difference)
    state_ref[0, 0] = difference
    state_ref[1, 0] = momentum
    state_ref[2, 0] = fresh
    copy_ref[0] = fresh.astype(LOW)


def outer_step(groups, me, totals, unit, units, cols, master, outer_old, into, name):
    depth = master.shape[1]
    slots = len(totals)
    rows = min(depth, 524288 // cols, totals[0].shape[-2])
    each = totals[0].shape[-2] // rows
    block = pl.BlockSpec((1, rows, cols), lambda u, r, g: (unit(u)[0], r, unit(u)[1]))
    state = pl.BlockSpec((3, 1, rows, cols), lambda u, r, g: (0, unit(u)[0], r, unit(u)[1]))
    if slots == 1:
        total = pl.BlockSpec((1, rows, cols), lambda u, r, g: (u, r, 0))
    else:
        total = pl.BlockSpec(totals[0].shape, lambda u, r, g: (0, 0))
    aliased = [] if into is None else [pl.BlockSpec(memory_space=pl.ANY)] * 2
    return pl.pallas_call(
        functools.partial(outer_kernel, groups, slots, each),
        grid_spec=pltpu.PrefetchScalarGridSpec(
            num_scalar_prefetch=1,
            grid=(units, depth // rows),
            in_specs=[*[total] * slots, block, block, *aliased],
            out_specs=[state, block],
        ),
        out_shape=[
            jax.ShapeDtypeStruct((3, *master.shape), F32),
            jax.ShapeDtypeStruct(master.shape, LOW),
        ],
        input_output_aliases={} if into is None else {slots + 3: 0, slots + 4: 1},
        compiler_params=params(),
        cost_estimate=cost(10 * units * depth * cols, 24 * units * depth * cols),
        name=name,
    )(me, *totals, master, outer_old, *([] if into is None else into))


def group_kernel(groups, shards, fsdp, diff_ref, *refs):
    if fsdp:
        part_ref, master_ref, moment_ref, outer_ref, total_ref, inner_ref, state_ref, copy_ref, *refs = refs
    else:
        total_ref, *refs = refs
    landed, summed, sends, receives, sends_two, receives_two, *small = refs
    g, f, t = lax.axis_index("group"), lax.axis_index("fsdp"), lax.axis_index("tensor")
    span = landed.shape[1]

    def rows(n):
        return pl.ds(pl.multiple_of(n * span, span), span)

    def other(k):
        return lax.rem(g + k, groups)

    def back(k):
        return lax.rem(g + groups - k, groups)

    def copy(src, dst, sems, semr, k, to):
        return pltpu.make_async_remote_copy(
            src_ref=src, dst_ref=dst, send_sem=sems.at[k], recv_sem=semr.at[k], device_id=to, device_id_type=MESH
        )

    def part(k):
        return copy(diff_ref.at[rows(other(k)), :], landed.at[k], sends, receives, k, (other(k), f, t))

    def result(k):
        return copy(summed, landed.at[groups + k], sends_two, receives_two, k, (other(k), f, t))

    barrier = pltpu.get_barrier_semaphore()
    for k in range(1, groups):
        pl.semaphore_signal(barrier, inc=1, device_id=(other(k), f, t), device_id_type=MESH)
    members = shards * fsdp
    if fsdp:
        few, mine, one, two, three, four = small
        me = f * shards + t

        def place(k):
            at = lax.rem(me + k, members)
            return (g, at // shards, lax.rem(at, shards))

        def piece(k):
            return copy(part_ref, few.at[k], one, two, k, place(k))

        def share(k):
            return copy(mine, few.at[members + k], three, four, k, (other(k), f, t))

        for k in range(1, members):
            pl.semaphore_signal(barrier, inc=1, device_id=place(k), device_id_type=MESH)
    pl.semaphore_wait(barrier, groups - 1 + max(members - 1, 0))

    for k in range(1, groups):
        part(k).start()
    if fsdp:
        for k in range(1, members):
            piece(k).start()
        few[0] = part_ref[...]
        for k in range(1, members):
            piece(k).wait_recv()
        gradient = jnp.zeros(part_ref.shape, F32)
        for n in range(members):
            gradient = gradient + few[lax.rem(me + members - n, members)]
        master = master_ref[...]
        new, second = inner_adamw(master, gradient, moment_ref[0], moment_ref[1], VECTOR_RATE, 0.0)
        inner_ref[0] = gradient
        inner_ref[1] = second
        mine[...] = master - new
        for k in range(1, groups):
            share(k).start()
        few[members] = mine[...]
    total = diff_ref[rows(g), :].astype(F32)
    for k in range(1, groups):
        part(k).wait_recv()
        total = total + landed[k].astype(F32)
    summed[...] = total.astype(LOW)
    for k in range(1, groups):
        result(k).start()
    total_ref[rows(g), :] = summed[...]
    if fsdp:
        for k in range(1, groups):
            share(k).wait_recv()
        difference = jnp.zeros(part_ref.shape, F32)
        for n in range(groups):
            difference = difference + few[members + lax.rem(g + groups - n, groups)]
        difference = difference / groups
        momentum, fresh = outer_nesterov(master, outer_ref[...], difference)
        state_ref[0] = difference
        state_ref[1] = momentum
        state_ref[2] = fresh
        copy_ref[...] = fresh.astype(LOW)
    for k in range(1, groups):
        result(k).wait_recv()
        total_ref[rows(back(k)), :] = landed[groups + k]
    for k in range(1, groups):
        part(k).wait_send()
        result(k).wait_send()
    if fsdp:
        for k in range(1, members):
            piece(k).wait_send()
        for k in range(1, groups):
            share(k).wait_send()


def group_sum(diff, groups, identity, name, vectors=None, shards=0, fsdp=0):
    flat = diff.reshape(-1, diff.shape[-1])
    span, cols = flat.shape[0] // groups, flat.shape[1]
    dma = pltpu.SemaphoreType.DMA
    whole = pl.BlockSpec(memory_space=pltpu.VMEM)
    out_shape = [jax.ShapeDtypeStruct(flat.shape, LOW)]
    extra = []
    if fsdp:
        shape = vectors[0].shape
        out_shape += [
            jax.ShapeDtypeStruct((2, *shape), F32),
            jax.ShapeDtypeStruct((3, *shape), F32),
            jax.ShapeDtypeStruct(shape, LOW),
        ]
        extra = [
            pltpu.VMEM((fsdp * shards + groups, *shape), F32),
            pltpu.VMEM(shape, F32),
            dma((fsdp * shards,)),
            dma((fsdp * shards,)),
            dma((groups,)),
            dma((groups,)),
        ]
    total, *rest = pl.pallas_call(
        functools.partial(group_kernel, groups, shards, fsdp),
        in_specs=[whole] * (5 if fsdp else 1),
        out_specs=[whole] * len(out_shape),
        out_shape=out_shape,
        scratch_shapes=[
            pltpu.VMEM((2 * groups, span, cols), LOW),
            pltpu.VMEM((span, cols), LOW),
            *[dma((groups,))] * 4,
            *extra,
        ],
        compiler_params=params(identity),
        cost_estimate=cost(4 * flat.size, 8 * flat.size),
        name=name,
    )(flat, *(vectors or []))
    return total.reshape(diff.shape), *rest


def gather_weights(shard):
    whole = lax.all_gather(shard, "tensor", axis=0)
    return lax.all_gather(whole, "fsdp", axis=2, tiled=True)


def around(array, k, groups):
    return lax.ppermute(array, "group", [(i, (i + k) % groups) for i in range(groups)])


def exchange_parts(diff, groups):
    g = lax.axis_index("group")
    quarters = diff.reshape(groups, -1, diff.shape[-1])
    parts = [lax.dynamic_index_in_dim(quarters, lax.rem(g + k, groups), 0, keepdims=False) for k in range(groups)]
    total = sum([around(parts[k], k, groups).astype(F32) for k in range(1, groups)], parts[0].astype(F32))
    return total.astype(LOW)


def exchange_total(own, groups):
    return [own] + [around(own, k, groups) for k in range(1, groups)]


def scatter_gradient(gradient):
    half = gradient if gradient.ndim == 4 else lax.psum_scatter(gradient, "fsdp", scatter_dimension=0)
    return lax.psum_scatter(half, "tensor", scatter_dimension=0)


def local(
    patches,
    output_grad,
    live_counts,
    attn_master,
    mlp_master,
    vector_master,
    attn_moments,
    mlp_moments,
    vector_moments,
    attn_outer,
    mlp_outer,
    vector_outer,
):
    vec = vector_master
    tensor_size, fsdp = lax.axis_size("tensor"), lax.axis_size("fsdp")
    groups = lax.axis_size("group")
    local_images, seq, width = patches.shape[2:]
    slot = (lax.axis_index("fsdp") * tensor_size + lax.axis_index("tensor")) * local_images
    slot = slot + jnp.arange(local_images)
    counts = jnp.take(live_counts[0], slot // IMG_DEV, axis=1)
    alive = ((slot % IMG_DEV)[None, :] < counts).astype(F32).reshape(-1)
    x = patches.reshape(-1, seq, width)
    cotangent = output_grad.reshape(-1, seq, width)
    images = x.shape[0]

    if (groups, fsdp) == (4, 2):
        w_attn, w_mlp, normed_one, qkv, attended, resid, normed_two, grad_two = front(
            alive, attn_master, mlp_master, x, cotangent, vec, tensor_size
        )
    else:
        w_attn = gather_weights(attn_master.astype(LOW))
        w_mlp = gather_weights(mlp_master.astype(LOW))
        normed_one, qkv = project(x, w_attn, vec)
        attended = attend(qkv, images, seq)
        resid, normed_two, grad_two = mix(alive, attended, x, cotangent, w_attn, vec)
    bias = vec[8:].reshape(tensor_size, 1, -1)
    carried = None
    mlp_grads, bias_parts = [], []
    for part, (start, cols) in enumerate(PIECES):
        *carried, dw, db = mlp(part, start, cols, normed_two, grad_two, w_mlp, bias, carried, fsdp)
        mlp_grads.append(scatter_gradient(dw))
        bias_parts.append(db)
    branch, grad_normed = carried
    block_output, grad_resid, grad_attended, dw_out, sums_two = turn(
        alive, resid, branch, grad_normed, grad_two, attended, w_attn, vec, images, seq, fsdp
    )
    def beside(*parts):
        return jnp.concatenate(parts, axis=-1)

    pairwise = fsdp == 2
    me = lax.axis_index("group").astype(jnp.int32).reshape(1)
    half = attn_master.shape[2] // PARTS
    grads = unattend(qkv, grad_attended, images, seq, 0, PARTS, tensor_size)
    head_grad, mlp_grads[0] = lax.optimization_barrier((grads[0], mlp_grads[0]))
    carry, dw_early, head_sums = close(
        0, PARTS, normed_one, (head_grad, *grads[1:]), w_attn, None, dw_out, None, fsdp, groups, images, seq
    )
    if not pairwise:
        halves = jnp.moveaxis(dw_out.reshape(*dw_out.shape[:-1], PARTS, half), -2, 2)
        dw_early = jnp.concatenate([dw_early, halves[:, :, :, 0]], axis=2)
    early_grad = scatter_gradient(dw_early)
    head_sums = [head_sums]
    carry, mlp_grads[1] = lax.optimization_barrier((carry, mlp_grads[1]))
    grads = unattend(qkv, grad_attended, images, seq, 1, PARTS, tensor_size)

    mlp_grads[0], head_grad = lax.optimization_barrier((mlp_grads[0], grads[0]))
    mlp_inner, mlp_diff = inner_step(
        beside, mlp_grads, lambda u: (u, 0), 2, mlp_master.shape[2], mlp_master, mlp_moments, None, "inner_mlp"
    )
    carry, mlp_diff = lax.optimization_barrier((carry, mlp_diff))
    ending = [x, grad_resid, vec]
    if pairwise:
        ending.append(mlp_diff.reshape(-1, mlp_diff.shape[-1]))
    patches_grad, sums_one, *mlp_own, dw_late, sums = close(
        1, PARTS, normed_one, (head_grad, *grads[1:]), w_attn, carry, None, ending, fsdp, groups, images, seq
    )
    if not pairwise:
        mlp_own = [exchange_parts(mlp_diff, groups)]
    mlp_total = exchange_total(mlp_own[0], groups)
    late_grad = scatter_gradient(dw_late)
    head_sums.append(sums)

    def early(u):
        return jnp.minimum(u, 3), jnp.maximum(u - 3, 0)

    def late(u):
        return u, 1

    def first(piece):
        return piece

    attn_inner, early_diff = inner_step(
        first, [early_grad], early, 3 + PARTS, half, attn_master, attn_moments, None, "inner_early"
    )
    head_rows = jnp.concatenate([v.reshape(2, tensor_size, -1) for v in head_sums], axis=-1).reshape(2, width)
    hidden_bias = jnp.concatenate(bias_parts, axis=-1).reshape(-1, width)
    vector_part = jnp.concatenate([sums_one, sums_two[:2], head_rows, sums_two[2:], hidden_bias])

    if pairwise:
        early_total, vector_inner, vector_state, vector_copy = group_sum(
            early_diff,
            groups,
            10,
            "group_early",
            [vector_part, vec, vector_moments[0], vector_outer],
            tensor_size,
            fsdp,
        )
    else:
        (early_total,) = group_sum(early_diff, groups, 10, "group_early")
        vector_grad = lax.psum(vector_part, ("fsdp", "tensor"))
        new_vector, second_vector = inner_adamw(
            vec, vector_grad, vector_moments[0, 0], vector_moments[0, 1], VECTOR_RATE, 0.0
        )
        diff_vector = lax.psum(vec - new_vector, "group") / groups
        momentum, fresh = outer_nesterov(vec, vector_outer, diff_vector)
        vector_inner = jnp.stack([vector_grad, second_vector])
        vector_state, vector_copy = jnp.stack([diff_vector, momentum, fresh]), fresh.astype(LOW)
    attn_state, attn_copy = outer_step(
        groups, me, [early_total], early, 3 + PARTS, half, attn_master, attn_outer, None, "outer_early"
    )
    attn_copy, *mlp_total = lax.optimization_barrier((attn_copy, *mlp_total))
    mlp_state, mlp_copy = outer_step(
        groups,
        me,
        mlp_total,
        lambda u: (u, 0),
        2,
        mlp_master.shape[2],
        mlp_master,
        mlp_outer,
        None,
        "outer_mlp",
    )
    late_grad, mlp_state = lax.optimization_barrier((late_grad, mlp_state))
    attn_inner, late_diff = inner_step(
        first, [late_grad], late, 3, half, attn_master, attn_moments, attn_inner, "inner_late"
    )
    (late_total,) = group_sum(late_diff, groups, 11, "group_late")
    attn_state, attn_copy = outer_step(
        groups, me, [late_total], late, 3, half, attn_master, attn_outer, (attn_state, attn_copy), "outer_late"
    )
    return (
        block_output.reshape(patches.shape),
        patches_grad.reshape(patches.shape),
        attn_inner,
        attn_state,
        attn_copy,
        mlp_inner,
        mlp_state,
        mlp_copy,
        vector_inner[None],
        vector_state,
        vector_copy,
    )


def solution(mesh):
    placed = (
        P("group", None, ("fsdp", "tensor"), None, None),
        P("group", None, ("fsdp", "tensor"), None, None),
        P("group", None, None),
        P(None, "fsdp", "tensor"),
        P(None, "fsdp", "tensor"),
        P(),
        P("group", None, None, "fsdp", "tensor"),
        P("group", None, None, "fsdp", "tensor"),
        P("group", None, None, None),
        P(None, "fsdp", "tensor"),
        P(None, "fsdp", "tensor"),
        P(),
    )
    return jax.shard_map(
        local,
        mesh=mesh,
        in_specs=placed,
        out_specs=(
            P("group", None, ("fsdp", "tensor"), None, None),
            P("group", None, ("fsdp", "tensor"), None, None),
            P("group", None, None, "fsdp", "tensor"),
            P(None, None, "fsdp", "tensor"),
            P(None, "fsdp", "tensor"),
            P("group", None, None, "fsdp", "tensor"),
            P(None, None, "fsdp", "tensor"),
            P(None, "fsdp", "tensor"),
            P("group", None, None, None),
            P(),
            P(),
        ),
        check_vma=False,
    )
```

profile of v0, /device:TPU:9, one launch (start us, length us, event | category | flops | bytes accessed | tf_op | source)
XLA Modules:
  0.0 493.5 jit_solution(12776916773792751403)
XLA Ops:
  8.6 6.1 %copy_bitcast_fusion = (bf16[2,577,1024]{2,1,0:T(8,128)(2,1)}, bf16[2,577,1024]{2,1,0:T(8,128)(2,1)}) fusion(bf16[1,2,1,577,1024]{4,1,3,2,0:T(2,128)(2,1)} %param.13, bf16[1,2,1,577,1024]{4,1,3,2,0:T(2,128)(2,1)} %param.12), kind=kLoop, calls=%fused_computation | loop fusion | bytes 9453568 | tf_op jit(solution)/shard_map/reshape | solution.py:1348
  15.4 118.0 %front.1 = (bf16[4,4,1024,256]{3,2,1,0:T(8,128)(2,1)}, bf16[4,2,1024,1024]{3,2,1,0:T(8,128)(2,1)}, bf16[1184,1024]{1,0:T(8,128)(2,1)}, bf16[3,1184,1024]{2,1,0:T...) custom-call(f32[2]{0:T(128)} %fusion.alive_ref, ...), custom_call_target="tpu_custom_call" | custom-call | flops 9932111872 | bytes 36372480 | tf_op jit(solution)/shard_map/front/pallas_call | solution.py:1020
  133.4 27.5 %mlp_0.1 = (f32[1184,1024]{1,0:T(8,128)}, f32[1184,1024]{1,0:T(8,128)}, bf16[4,2,512,256]{3,2,1,0:T(8,128)(2,1)}, f32[4,1,256]{2,1,0:T(1,128)}) custom-call(bf16[1184,1024]{1,0:T(8,128)(2,1)} %get-tuple-element.82.n_ref, bf16[1184,1024]{1,0:T(8,128)(2,1)} %get-tuple-element.83.g_ref.g2_ref, bf16[4,2,1024,1024]{3,2,1,0:T(8,128)(2,1)} %get-tuple-element.84.w1_ref.w2_ref, ...), custom_call_target="tpu_custom_call" | custom-call | flops 14898167808 | bytes 29097984 | tf_op jit(solution)/shard_map/mlp_0/pallas_call | solution.py:334
  161.0 25.5 %mlp_1.1 = (f32[1184,1024]{1,0:T(8,128)}, f32[1184,1024]{1,0:T(8,128)}, bf16[4,2,512,256]{3,2,1,0:T(8,128)(2,1)}, f32[4,1,256]{2,1,0:T(1,128)}) custom-call(bf16[1184,1024]{1,0:T(8,128)(2,1)} %get-tuple-element.82.n_ref, bf16[1184,1024]{1,0:T(8,128)(2,1)} %get-tuple-element.83.g_ref.g2_ref, bf16[4,2,1024,1024]{3,2,1,0:T(8,128)(2,1)} %get-tuple-element.84.w1_ref.w2_ref, ...), custom_call_target="tpu_custom_call" | custom-call | flops 14898167808 | bytes 29097984 | tf_op jit(solution)/shard_map/mlp_1/pallas_call | solution.py:334
  186.6 44.9 %mlp_2.1 = (f32[1184,1024]{1,0:T(8,128)}, f32[1184,1024]{1,0:T(8,128)}, bf16[4,2,512,512]{3,2,1,0:T(8,128)(2,1)}, f32[4,1,512]{2,1,0:T(1,128)}) custom-call(bf16[1184,1024]{1,0:T(8,128)(2,1)} %get-tuple-element.82.n_ref, bf16[1184,1024]{1,0:T(8,128)(2,1)} %get-tuple-element.83.g_ref.g2_ref, bf16[4,2,1024,1024]{3,2,1,0:T(8,128)(2,1)} %get-tuple-element.84.w1_ref.w2_ref, ...), custom_call_target="tpu_custom_call" | custom-call | flops 29796335616 | bytes 29097984 | tf_op jit(solution)/shard_map/mlp_2/pallas_call | solution.py:334
  231.6 21.7 %turn.1 = (bf16[2,577,1024]{2,1,0:T(8,128)(2,1)}, f32[1184,1024]{1,0:T(8,128)}, bf16[1184,1024]{1,0:T(8,128)(2,1)}, bf16[4,1,512,256]{3,2,1,0:T(8,128)(2,1)}, f32[4,1024]{1,0:T(4,128)}) custom-call(f32[2]{0:T(128)} %fusion.alive_ref, f32[1184,1024]{1,0:T(8,128)} %get-tuple-element.81.resid_ref, f32[1184,1024]{1,0:T(8,128)} %get-tuple-element.89.y_ref, ...), custom_call_target="tpu_custom_call" | custom-call | flops 4966055936 | bytes 29097984 | tf_op jit(solution)/shard_map/turn/pallas_call | solution.py:428
  253.3 28.3 %unattend_0.1 = (bf16[1,1184,512]{2,1,0:T(8,128)(2,1)}, bf16[1,1184,512]{2,1,0:T(8,128)(2,1)}, bf16[1,1184,512]{2,1,0:T(8,128)(2,1)}) custom-call(bf16[3,1184,1024]{2,1,0:T(8,128)(2,1)} %get-tuple-element.95.q_ref.k_ref.v_ref, bf16[3,1184,1024]{2,1,0:T(8,128)(2,1)} %get-tuple-element.95.q_ref.k_ref.v_ref, ...), custom_call_target="tpu_custom_call" | custom-call | flops 14355005440 | bytes 8486912 | tf_op jit(solution)/shard_map/unattend_0/pallas_call | solution.py:497
  281.6 17.5 %close_0.1 = (f32[1184,1024]{1,0:T(8,128)}, bf16[4,5,512,128]{3,2,1,0:T(8,128)(2,1)}, f32[2,512]{1,0:T(2,128)}) custom-call(bf16[1184,1024]{1,0:T(8,128)(2,1)} %get-tuple-element.94.n_ref, bf16[1,1184,512]{2,1,0:T(8,128)(2,1)} %get-tuple-element.104.dq_ref, bf16[1,1184,512]{2,1,0:T(8,128)(2,1)} %get-tuple-element.105.dk_ref, ...), custom_call_target="tpu_custom_call" | custom-call | flops 7449083904 | bytes 24248320 | tf_op jit(solution)/shard_map/close_0/pallas_call | solution.py:684
  299.2 28.3 %unattend_1.1 = (bf16[1,1184,512]{2,1,0:T(8,128)(2,1)}, bf16[1,1184,512]{2,1,0:T(8,128)(2,1)}, bf16[1,1184,512]{2,1,0:T(8,128)(2,1)}) custom-call(bf16[3,1184,1024]{2,1,0:T(8,128)(2,1)} %get-tuple-element.95.q_ref.k_ref.v_ref, bf16[3,1184,1024]{2,1,0:T(8,128)(2,1)} %get-tuple-element.95.q_ref.k_ref.v_ref, ...), custom_call_target="tpu_custom_call" | custom-call | flops 14355005440 | bytes 8486912 | tf_op jit(solution)/shard_map/unattend_1/pallas_call | solution.py:497
  328.3 10.2 %inner_mlp.1 = (f32[1,2,2,512,1024]{4,3,2,1,0:T(8,128)}, bf16[2,512,1024]{2,1,0:T(8,128)(2,1)}) custom-call(bf16[2,512,256]{2,1,0:T(8,128)(2,1)} %bitcast.40, bf16[2,512,256]{2,1,0:T(8,128)(2,1)} %bitcast.41, bf16[2,512,512]{2,1,0:T(8,128)(2,1)} %bitcast.36, f32[2,512,1024]{2,1,0:T(8,128)} %refs_4_.3, f32[1,2,2,512,1024]{4,3,2,1,0:T(8,128)} %refs_4_.2), custom_call_target="tpu_custom_call" | custom-call | flops 31457280 | bytes 25165824 | tf_op jit(solution)/shard_map/inner_mlp/pallas_call | solution.py:1089
  338.5 36.3 %close_1.1 = (f32[2,577,1,1024]{3,2,1,0:T(1,128)}, f32[2,1024]{1,0:T(2,128)}, bf16[256,1024]{1,0:T(8,128)(2,1)}, bf16[4,3,512,128]{3,2,1,0:T(8,128)(2,1)}, f32[2,512]{1,0:T(2,128)}) custom-call(bf16[1184,1024]{1,0:T(8,128)(2,1)} %get-tuple-element.94.n_ref, bf16[1,1184,512]{2,1,0:T(8,128)(2,1)} %get-tuple-element.101.dq_ref, ...), custom_call_target="tpu_custom_call" | custom-call | flops 7449083904 | bytes 24248320 | tf_op jit(solution)/shard_map/close_1/pallas_call | solution.py:684
  374.9 1.4 collective-permute-start.2
  376.5 1.1 collective-permute-start
  378.3 3.8 copy.32
  382.3 1.3 concatenate.11.refs_0_
  383.6 6.3 %inner_early.1 = (f32[1,2,4,512,256]{4,3,2,1,0:T(8,128)}, bf16[5,512,128]{2,1,0:T(8,128)(2,1)}) custom-call(bf16[5,512,128]{2,1,0:T(8,128)(2,1)} %bitcast.39, f32[4,512,256]{2,1,0:T(8,128)} %refs_1_.9, f32[1,2,4,512,256]{4,3,2,1,0:T(8,128)} %refs_2_.6), custom_call_target="tpu_custom_call" | custom-call | flops 9830400 | bytes 7864320 | tf_op jit(solution)/shard_map/inner_early/pallas_call | solution.py:1089
  389.9 45.0 %group_early.1 = (bf16[2560,128]{1,0:T(8,128)(2,1)}, f32[2,12,1024]{2,1,0:T(8,128)}, f32[3,12,1024]{2,1,0:T(8,128)}, bf16[12,1024]{1,0:T(8,128)(2,1)}) custom-call(bf16[2560,128]{1,0:T(8,128)(2,1)} %bitcast.38, f32[12,1024]{1,0:T(8,128)} %concatenate.11.refs_0_, f32[12,1024]{1,0:T(8,128)} %refs_1_.6, f32[2,12,1024]{2,1,0:T(8,128)} %bitcast.42, ...), custom_call_target="tpu_custom_call" | custom-call | flops 1310720 | bytes 2621440 | tf_op jit(solution)/shard_map/group_early/pallas_call | solution.py:1281
  434.9 1.6 copy.34
  436.6 5.6 %outer_early.1 = (f32[3,4,512,256]{3,2,1,0:T(8,128)}, bf16[4,512,256]{2,1,0:T(8,128)(2,1)}) custom-call(s32[1]{0:T(128)} %bitcast.14.g_ref, bf16[5,512,128]{2,1,0:T(8,128)(2,1)} %bitcast.37, f32[4,512,256]{2,1,0:T(8,128)} %refs_1_.9, f32[4,512,256]{2,1,0:T(8,128)} %refs_2_.7), custom_call_target="tpu_custom_call" | custom-call | flops 3276800 | bytes 7864320 | tf_op jit(solution)/shard_map/outer_early/pallas_call | solution.py:1137
  443.1 10.4 %outer_mlp.1 = (f32[3,2,512,1024]{3,2,1,0:T(8,128)}, bf16[2,512,1024]{2,1,0:T(8,128)(2,1)}) custom-call(s32[1]{0:T(128)} %bitcast.14.g_ref, bf16[256,1024]{1,0:T(8,128)(2,1)} %get-tuple-element.132.refs_0_, bf16[256,1024]{1,0:T(8,128)(2,1)} %collective-permute-done.refs_1_, bf16[256,1024]{1,0:T(8,128)(2,1)} %copy-done.2, bf16[256,1024]{1,0:T(8,128)(2,1)} %copy-done.1, ...), custom_call_target="tpu_custom_call" | custom-call | flops 10485760 | bytes 25165824 | tf_op jit(solution)/shard_map/outer_mlp/pallas_call | solution.py:1137
  453.5 4.3 inner_late.1
  457.8 15.7 %group_late.1 = bf16[1536,128]{1,0:T(8,128)(2,1)} custom-call(bf16[1536,128]{1,0:T(8,128)(2,1)} %bitcast.43), custom_call_target="tpu_custom_call" | custom-call | flops 786432 | bytes 1572864 | tf_op jit(solution)/shard_map/group_late/pallas_call | solution.py:1281
  473.6 3.8 outer_late.1
  477.4 7.8 %copy.46 = f32[1,2,1,577,1024]{4,2,3,1,0:T(1,128)} copy(f32[1,2,1,577,1024]{4,2,3,1,0:T(1,128)} %bitcast.32) | data formatting | bytes 9453568
  (62 shorter events, 6.5 us)
Async XLA Ops:
  7.2 274.4 %reduce-scatter.6.cloned.1.call-start = ((), (), s32[]{:S(2)}) async-start(), calls=%async_computation.5 | async-start | bytes 2621440 | tf_op jit(solution)/shard_map/reduce_scatter | solution.py:1322
  8.6 6.1 %copy-start.13 = (s32[1,2,2]{2,1,0:T(2,128)S(1)}, s32[1,2,2]{2,1,0:T(2,128)}, u32[]{:S(2)}) copy-start(s32[1,2,2]{2,1,0:T(2,128)} %param.14) | copy-start | bytes 52
  161.0 166.5 %reduce-scatter.8.cloned.1.call-start = ((), (), s32[]{:S(2)}) async-start(), calls=%async_computation.6 | async-start | bytes 2621440 | tf_op jit(solution)/shard_map/reduce_scatter | solution.py:1322
  186.5 141.7 %reduce-scatter.10.cloned.1.call-start = ((), (), s32[]{:S(2)}) async-start(), calls=%async_computation.7 | async-start | bytes 5242880 | tf_op jit(solution)/shard_map/reduce_scatter | solution.py:1322
  231.5 152.1 %reduce-scatter.14.cloned.1.call-start = ((), (), s32[]{:S(2)}) async-start(), calls=%async_computation.9 | async-start | bytes 3276800 | tf_op jit(solution)/shard_map/reduce_scatter | solution.py:1322
  299.2 154.3 %reduce-scatter.12.cloned.1.call-start = ((), (), s32[]{:S(2)}) async-start(), calls=%async_computation.8 | async-start | bytes 1966080 | tf_op jit(solution)/shard_map/reduce_scatter | solution.py:1322
  338.5 39.1 %copy-start.4 = (f32[1,2,12,1024]{3,1,2,0:T(2,128)S(1)}, f32[1,2,12,1024]{3,1,2,0:T(2,128)}, u32[]{:S(2)}) copy-start(f32[1,2,12,1024]{3,1,2,0:T(2,128)} %param.20) | copy-start | bytes 294916
  338.5 39.8 %copy-start.9 = (f32[4,1,256]{2,1,0:T(1,128)S(1)}, f32[4,1,256]{2,1,0:T(1,128)}, u32[]{:S(2)}) copy-start(f32[4,1,256]{2,1,0:T(1,128)} %get-tuple-element.126) | copy-start | bytes 12292
  338.5 39.8 %copy-start = (bf16[2,577,1024]{2,1,0:T(8,128)(2,1)S(1)}, bf16[2,577,1024]{2,1,0:T(8,128)(2,1)}, u32[]{:S(2)}) copy-start(bf16[2,577,1024]{2,1,0:T(8,128)(2,1)} %get-tuple-element.93) | copy-start | bytes 7090180
  374.9 67.2 %collective-permute-start.2 = (bf16[256,1024]{1,0:T(8,128)(2,1)}, bf16[256,1024]{1,0:T(8,128)(2,1)S(1)}, u32[]{:S(2)}, u32[]{:S(2)}) collective-permute-start(bf16[256,1024]{1,0:T(8,128)(2,1)} %get-tuple-element.132.refs_0_), channel_id=1, source_target_pairs={{0,24},{8,0},{16,8},{24,16},{1,25},{9,1},{17,9},{25,17},{2,26},{10... | collective-permute-start | bytes 1572872 | tf_op jit(solution)/shard_map/ppermute | solution.py:1305
  376.3 65.9 %collective-permute-start.1 = (bf16[256,1024]{1,0:T(8,128)(2,1)}, bf16[256,1024]{1,0:T(8,128)(2,1)S(1)}, u32[]{:S(2)}, u32[]{:S(2)}) collective-permute-start(bf16[256,1024]{1,0:T(8,128)(2,1)} %get-tuple-element.132.refs_0_), channel_id=1, source_target_pairs={{0,16},{8,24},{16,0},{24,8},{1,17},{9,25},{17,1},{25,9},{2,18},{10... | collective-permute-start | bytes 1572872 | tf_op jit(solution)/shard_map/ppermute | solution.py:1305
  376.5 65.6 %collective-permute-start = (bf16[256,1024]{1,0:T(8,128)(2,1)}, bf16[256,1024]{1,0:T(8,128)(2,1)}, u32[]{:S(2)}, u32[]{:S(2)}) collective-permute-start(bf16[256,1024]{1,0:T(8,128)(2,1)} %get-tuple-element.132.refs_0_), channel_id=1, source_target_pairs={{0,8},{8,16},{16,24},{24,0},{1,9},{9,17},{17,25},{25,1},{2,10},{10... | collective-permute-start | bytes 1572872 | tf_op jit(solution)/shard_map/ppermute | solution.py:1305
  378.3 3.9 copy-start.10
  378.3 3.9 copy-start.8
  378.3 3.9 copy-start.6
  378.3 3.9 copy-start.11
  378.3 3.9 copy-start.12
  378.3 4.0 copy-start.7
  442.1 0.8 copy-start.1
  442.1 1.0 copy-start.2
  477.4 7.8 %copy-start.3 = (f32[3,12,1024]{2,1,0:T(8,128)S(1)}, f32[3,12,1024]{2,1,0:T(8,128)}, u32[]{:S(2)}) copy-start(f32[3,12,1024]{2,1,0:T(8,128)} %get-tuple-element.197) | copy-start | bytes 442372
  477.4 8.5 %copy-start.5 = (bf16[12,1024]{1,0:T(8,128)(2,1)S(1)}, bf16[12,1024]{1,0:T(8,128)(2,1)}, u32[]{:S(2)}) copy-start(bf16[12,1024]{1,0:T(8,128)(2,1)} %get-tuple-element.198) | copy-start | bytes 73732
Sparse Core Ops, SparseCore 0:
  161.1 40.6 reduce-scatter.5
  204.2 43.1 reduce-scatter.7
  249.7 78.5 reduce-scatter.9
  330.5 51.6 reduce-scatter.13
  384.5 46.1 reduce-scatter.11
where the time goes:
time: 501 us; the launch traced here: 493 us
  Pallas kernels  449 us (90%)
  local copies, waits for them, and re-layouts  25 us (5%)
  between operations  14.5 us (3%)
    pallas_call x1, Pallas kernels, front(): pl.pallas_call(functools.partial(front_kernel, images, seq), in_specs=[pl...  118 us
    pallas_call x3, Pallas kernels, mlp(): pl.pallas_call(functools.partial(mlp_kernel, first, pairwise), grid=(step...  97.9 us
    pallas_call x2, Pallas kernels, group_sum(): pl.pallas_call(functools.partial(group_kernel, groups, shards, fsdp), in_...  60.7 us
    pallas_call x2, Pallas kernels, unattend(): pl.pallas_call(functools.partial(unattend_kernel, seq), grid=(images, wid...  56.6 us
    pallas_call x2, Pallas kernels, close(): pl.pallas_call(functools.partial(close_kernel, seq, images, pairwise, gro...  53.8 us
    pallas_call x1, Pallas kernels, turn(): pl.pallas_call(functools.partial(turn_kernel, seq, pairwise), grid=(image...  21.7 us
    pallas_call x3, Pallas kernels, inner_step(): pl.pallas_call(functools.partial(inner_kernel, join, count), grid=(units,...  20.9 us
    pallas_call x3, Pallas kernels, outer_step(): pl.pallas_call(functools.partial(outer_kernel, groups, slots, each), grid...  19.8 us
  transfers between devices with their start and end apart: 8, of which 1 were waited for; matrix products, arithmetic and copies ran while one was open for 2% of the time, Pallas kernels for 57%

commit v1 on v0

--- a/solution.py
+++ b/solution.py
@@ -454,7 +454,7 @@
     )(alive, resid, branch, grad_normed, grad_two, attended, w_attn, vec)
 
 
-def unattend_kernel(seq, q_ref, k_ref, v_ref, g_ref, dq_ref, dk_ref, dv_ref):
+def unattend_kernel(seq, q_ref, k_ref, v_ref, g_ref, out_ref):
     span = q_ref.shape[1]
     scale = HD**-0.5
     q, k, v, g = q_ref[0], k_ref[0], v_ref[0], g_ref[...]
@@ -475,9 +475,9 @@
         dq = dot(gs, k, TN)
         parts.append((dq, dk, dv))
     lane = lax.broadcasted_iota(jnp.int32, (span, 2 * HD), 1) < HD
-    dq_ref[0] = (jnp.where(lane, parts[0][0], parts[1][0]) * scale).astype(LOW)
-    dk_ref[0] = (jnp.where(lane, parts[0][1], parts[1][1]) * scale).astype(LOW)
-    dv_ref[0] = jnp.where(lane, parts[0][2], parts[1][2]).astype(LOW)
+    out_ref[0] = (jnp.where(lane, parts[0][0], parts[1][0]) * scale).astype(LOW)
+    out_ref[1] = (jnp.where(lane, parts[0][1], parts[1][1]) * scale).astype(LOW)
+    out_ref[2] = jnp.where(lane, parts[0][2], parts[1][2]).astype(LOW)
 
 
 def unattend(qkv, grad_attended, images, seq, part, parts, shards):
@@ -492,14 +492,12 @@
     def take(j):
         return pl.BlockSpec((1, span, pair), lambda i, h: (j, i, spot(h)))
 
-    out = pl.BlockSpec((1, span, pair), lambda i, h: (0, i, h))
-    shape = jax.ShapeDtypeStruct((1, rows, width // parts), LOW)
     return pl.pallas_call(
         functools.partial(unattend_kernel, seq),
         grid=(images, width // pair // parts),
         in_specs=[take(0), take(1), take(2), pl.BlockSpec((span, pair), lambda i, h: (i, spot(h)))],
-        out_specs=[out, out, out],
-        out_shape=[shape, shape, shape],
+        out_specs=pl.BlockSpec((3, span, pair), lambda i, h: (0, i, h)),
+        out_shape=jax.ShapeDtypeStruct((3, rows, width // parts), LOW),
         compiler_params=params(),
         cost_estimate=cost(
             40 * rows * span * width // parts, 14 * rows * width // parts, rows * span * (width // HD) // parts
@@ -508,7 +506,7 @@
     )(qkv, qkv, qkv, grad_attended)
 
 
-def close_kernel(seq, images, pairwise, groups, first, final, n_ref, dq_ref, dk_ref, dv_ref, w_ref, *refs):
+def close_kernel(seq, images, pairwise, groups, first, final, n_ref, grad_ref, w_ref, *refs):
     if not first:
         carry_ref, *refs = refs
     elif pairwise:
@@ -567,8 +565,13 @@
     @pl.when(j == 0)
     def _():
         acc_scr[...] = jnp.zeros_like(acc_scr) if first else carry_ref[...]
-        sums_ref[0:1, :] = jnp.sum(dq_ref[0].astype(F32), axis=0, keepdims=True)
-        sums_ref[1:2, :] = jnp.sum(dv_ref[0].astype(F32), axis=0, keepdims=True)
+
+    sums = jnp.sum(grad_ref[0].astype(F32), axis=0, keepdims=True)
+    for n, matrix in enumerate((0, 2)):
+
+        @pl.when(j == matrix)
+        def _():
+            sums_ref[n : n + 1, :] = sums
 
     def spread(n, total, f=None):
         for t in range(shards):
@@ -578,31 +581,21 @@
             else:
                 dw_ref[f, t, 0] = piece
 
-    def step(ref):
-        weight = jnp.concatenate([w_ref[t, 0] for t in range(shards)], axis=1)
-        if pairwise:
-            ours, theirs = bands(n_ref.shape[1] // 2)
-            sent[j] = dot(n_ref[:, theirs], ref[0], TN).astype(LOW)
-            to_partner(sent, received, sends, receives, j).start()
-            own[j] = dot(n_ref[:, ours], ref[0], TN)
-        else:
-            depth = dw_ref.shape[3]
-            dw = dot(n_ref[...], ref[0], TN).astype(LOW)
-            for f in range(dw_ref.shape[0]):
-                spread(0, dw[f * depth : (f + 1) * depth], f)
-        acc_scr[...] += dot(ref[0], weight, NT)
-
-    @pl.when(j == 0)
-    def _():
-        step(dq_ref)
-
-    @pl.when(j == 1)
-    def _():
-        step(dk_ref)
+    weight = jnp.concatenate([w_ref[t, 0] for t in range(shards)], axis=1)
+    if pairwise:
+        ours, theirs = bands(n_ref.shape[1] // 2)
+        sent[j] = dot(n_ref[:, theirs], grad_ref[0], TN).astype(LOW)
+        to_partner(sent, received, sends, receives, j).start()
+        own[j] = dot(n_ref[:, ours], grad_ref[0], TN)
+    else:
+        depth = dw_ref.shape[3]
+        dw = dot(n_ref[...], grad_ref[0], TN).astype(LOW)
+        for f in range(dw_ref.shape[0]):
+            spread(0, dw[f * depth : (f + 1) * depth], f)
+    acc_scr[...] += dot(grad_ref[0], weight, NT)
 
     @pl.when(j == 2)
     def _():
-        step(dv_ref)
         if pairwise:
             for n in range(own.shape[0]):
                 to_partner(sent, received, sends, receives, n).wait()
@@ -641,7 +634,7 @@
     depth = width // fsdp
     pairwise, first, final = fsdp == 2, carry is None, ending is not None
     single = pl.Buffered(1)
-    stack = pl.BlockSpec((1, rows, lanes), lambda j: (0, 0, 0), pipeline_mode=single)
+    stack = pl.BlockSpec((1, rows, lanes), lambda j: (j, 0, 0))
     full = pl.BlockSpec((rows, width), lambda j: (0, 0), pipeline_mode=single)
     image = pl.BlockSpec((images, seq, width), lambda j: (0, 0, 0), pipeline_mode=single)
     if pairwise:
@@ -653,7 +646,7 @@
         dw_spec = pl.BlockSpec((fsdp, shards, 1, depth, cols), lambda j: (0, 0, j, 0, 0))
         dw_shape = jax.ShapeDtypeStruct((fsdp, shards, 3, depth, cols), LOW)
         extra = []
-    in_specs = [full, stack, stack, stack, pl.BlockSpec((shards, 1, width, cols), lambda j: (0, j, 0, part))]
+    in_specs = [full, stack, pl.BlockSpec((shards, 1, width, cols), lambda j: (0, j, 0, part))]
     out_specs, out_shape = [], []
     if not first:
         in_specs.append(full)
@@ -691,7 +684,7 @@
         compiler_params=params(7 + part if pairwise else None),
         cost_estimate=cost(12 * rows * width * lanes, 20 * rows * width),
         name=f"close_{part}",
-    )(normed, *grads, w_attn, *([carry] if not first else [more] if pairwise else []), *(ending if final else []))
+    )(normed, grads, w_attn, *([carry] if not first else [more] if pairwise else []), *(ending if final else []))
 
 
 def attend_pair(seq, q, k, v):
@@ -876,15 +869,28 @@
 
         lax.fori_loop(0, 3, body, 0)
 
-    def project(n, k, up):
-        when_real(k, up, maps)
+    def project(k):
+        def body(d, carry):
+            t = z - k + 2 * k * d
+
+            @pl.when((t >= 0) & (t <= last))
+            def _():
+                maps(t)
+
+            return carry
+
+        lax.fori_loop(0, 2, body, 0)
 
     own(0)
     loads[1].start()
     n_scr[...] = jnp.zeros_like(n_scr)
-    for i in range(images):
+
+    def norm_image(i, carry):
         normal, _ = centred(x_ref[i].astype(F32))
-        n_scr[pl.ds(i * span, seq), :] = (normal * vec_ref[0:1] + vec_ref[1:2]).astype(LOW)
+        n_scr[pl.ds(pl.multiple_of(i * span, 16), seq), :] = (normal * vec_ref[0:1] + vec_ref[1:2]).astype(LOW)
+        return carry
+
+    lax.fori_loop(0, images, norm_image, 0)
     puts = [pltpu.make_async_copy(n_scr, n_out, ws.at[1])]
     puts[0].start()
     both(land, 0, 1)
@@ -902,9 +908,9 @@
     both(finish, 0, 1)
     both(relay, 0, 3)
     both(finish, 0, 2)
-    both(project, 0, 1)
+    project(1)
     both(finish, 0, 3)
-    both(project, 0, 2)
+    project(2)
 
     rest_items = [(n, k) for k in range(1, last + 1) for n in range(1, count)]
     total = len(rest_items) + 2
@@ -918,29 +924,32 @@
             both(finish, *rest_items[at - 2])
 
     advance(0)
-    both(project, 0, 3)
+    project(3)
     puts.append(pltpu.make_async_copy(qkv_scr, qkv_out, ws.at[2]))
     puts[-1].start()
 
     pair = 2 * HD
     pairs = qkv_scr.shape[2] // pair
     stretch = max(pairs // 4, 1)
-    at = 1
-    for i in range(images):
-        for start in range(0, pairs, stretch):
-
-            def body(h, carry):
-                lanes = pl.ds(pl.multiple_of(h * pair, pair), pair)
-                here = pl.ds(i * span, span)
-                att_scr[here, lanes] = attend_pair(
-                    seq, qkv_scr[0, here, lanes], qkv_scr[1, here, lanes], qkv_scr[2, here, lanes]
-                )
-                return carry
-
-            lax.fori_loop(start, start + stretch, body, 0)
-            if at < total:
-                advance(at)
-                at += 1
+    segments = images * pairs // stretch
+
+    def segment(n, carry):
+        def body(m, carry):
+            at = n * stretch + m
+            lanes = pl.ds(pl.multiple_of(lax.rem(at, pairs) * pair, pair), pair)
+            here = pl.ds(pl.multiple_of(at // pairs * span, 16), span)
+            att_scr[here, lanes] = attend_pair(
+                seq, qkv_scr[0, here, lanes], qkv_scr[1, here, lanes], qkv_scr[2, here, lanes]
+            )
+            return carry
+
+        lax.fori_loop(0, stretch, body, 0)
+        for c in range(min(segments, total - 3)):
+            pl.when(n == c)(functools.partial(advance, 1 + c))
+        return carry
+
+    lax.fori_loop(0, segments, segment, 0)
+    at = 1 + min(segments, total - 3)
     puts.append(pltpu.make_async_copy(att_scr, att_out, ws.at[3]))
     puts[-1].start()
     while at < total - 2:
@@ -953,8 +962,9 @@
     take.start()
     take.wait()
     x_scr[...] = jnp.zeros_like(x_scr)
-    for i in range(images):
-        here = pl.ds(i * span, span)
+
+    def mix_image(i, carry):
+        here = pl.ds(pl.multiple_of(i * span, 16), span)
         x_scr[0:seq, :] = x_ref[i].astype(F32)
         out = x_scr[...] + vec_ref[6:7]
         for t in range(shards):
@@ -964,9 +974,12 @@
         n2_scr[here, :] = (normal * vec_ref[2:3] + vec_ref[3:4]).astype(LOW)
         x_scr[0:seq, :] = g_ref[i].astype(F32) * alive_ref[i]
         g2_scr[here, :] = x_scr[...].astype(LOW)
-        if at < total:
-            advance(at)
-            at += 1
+        for c in range(min(images, total - at)):
+            pl.when(i == c)(functools.partial(advance, at + c))
+        return carry
+
+    lax.fori_loop(0, images, mix_image, 0)
+    at += min(images, total - at)
     for n, (src, dst) in enumerate(((resid_scr, resid_out), (n2_scr, n2_out), (g2_scr, g2_out))):
         puts.append(pltpu.make_async_copy(src, dst, ws.at[4 + n]))
         puts[-1].start()
@@ -1153,8 +1166,8 @@
     )(me, *totals, master, outer_old, *([] if into is None else into))
 
 
-def group_kernel(groups, shards, fsdp, diff_ref, *refs):
-    if fsdp:
+def group_kernel(groups, shards, vectors, diff_ref, *refs):
+    if vectors:
         part_ref, master_ref, moment_ref, outer_ref, total_ref, inner_ref, state_ref, copy_ref, *refs = refs
     else:
         total_ref, *refs = refs
@@ -1185,44 +1198,63 @@
     barrier = pltpu.get_barrier_semaphore()
     for k in range(1, groups):
         pl.semaphore_signal(barrier, inc=1, device_id=(other(k), f, t), device_id_type=MESH)
-    members = shards * fsdp
-    if fsdp:
-        few, mine, one, two, three, four = small
-        me = f * shards + t
-
-        def place(k):
-            at = lax.rem(me + k, members)
-            return (g, at // shards, lax.rem(at, shards))
-
-        def piece(k):
-            return copy(part_ref, few.at[k], one, two, k, place(k))
-
-        def share(k):
-            return copy(mine, few.at[members + k], three, four, k, (other(k), f, t))
-
-        for k in range(1, members):
-            pl.semaphore_signal(barrier, inc=1, device_id=place(k), device_id_type=MESH)
-    pl.semaphore_wait(barrier, groups - 1 + max(members - 1, 0))
+    if vectors:
+        stage, pair, mine, line, whole, few, diffs, ss, rs, ls, lr, gs, gr = small
+        half = part_ref.shape[0] // 2
+        halves = (pl.ds(0, half), pl.ds(half, half))
+
+        def pick(ref):
+            return jnp.where(f == 0, ref[halves[0], :], ref[halves[1], :])
+
+        def line_copy(k):
+            return copy(mine, line.at[k], ls, lr, k, (g, f, lax.rem(t + k, shards)))
+
+        def few_copy(k):
+            return copy(diffs.at[f], few.at[k], gs, gr, k, (other(k), f, t))
+
+        pair_copy = copy(stage.at[1 - f], pair, ss, rs, 0, partner())
+        whole_copy = copy(whole.at[f], whole.at[f], ss, rs, 1, partner())
+        final_copy = copy(mine, stage.at[f], ss, rs, 2, partner())
+        pl.semaphore_signal(barrier, inc=1, device_id=partner(), device_id_type=MESH)
+        for k in range(1, shards):
+            pl.semaphore_signal(barrier, inc=1, device_id=(g, f, lax.rem(t + k, shards)), device_id_type=MESH)
+        stage[...] = jnp.zeros_like(stage)
+        diffs[...] = jnp.zeros_like(diffs)
+        for n in range(2):
+            stage[n, 0:half] = part_ref[halves[n], :]
+    pl.semaphore_wait(barrier, groups - 1 + (shards if vectors else 0))
 
     for k in range(1, groups):
         part(k).start()
-    if fsdp:
-        for k in range(1, members):
-            piece(k).start()
-        few[0] = part_ref[...]
-        for k in range(1, members):
-            piece(k).wait_recv()
-        gradient = jnp.zeros(part_ref.shape, F32)
-        for n in range(members):
-            gradient = gradient + few[lax.rem(me + members - n, members)]
-        master = master_ref[...]
-        new, second = inner_adamw(master, gradient, moment_ref[0], moment_ref[1], VECTOR_RATE, 0.0)
-        inner_ref[0] = gradient
-        inner_ref[1] = second
-        mine[...] = master - new
+    if vectors:
+        pair_copy.start()
+        pair_copy.wait()
+        mine[...] = stage[f] + pair[...]
+        for k in range(1, shards):
+            line_copy(k).start()
+        line[0] = mine[...]
+        for k in range(1, shards):
+            line_copy(k).wait()
+        gradient = jnp.zeros(mine.shape, F32)
+        for n in range(shards):
+            gradient = gradient + line[lax.rem(t + shards - n, shards)]
+        whole[f] = gradient
+        whole_copy.start()
+        new, _ = inner_adamw(
+            pick(master_ref), gradient[0:half], pick(moment_ref.at[0]), pick(moment_ref.at[1]), VECTOR_RATE, 0.0
+        )
+        diffs[f, 0:half] = pick(master_ref) - new
         for k in range(1, groups):
-            share(k).start()
-        few[members] = mine[...]
+            few_copy(k).start()
+        few[0] = diffs[f]
+        whole_copy.wait()
+        for n in range(2):
+            own = whole[n, 0:half]
+            _, second = inner_adamw(
+                master_ref[halves[n], :], own, moment_ref[0, halves[n], :], moment_ref[1, halves[n], :], VECTOR_RATE, 0.0
+            )
+            inner_ref[0, halves[n], :] = own
+            inner_ref[1, halves[n], :] = second
     total = diff_ref[rows(g), :].astype(F32)
     for k in range(1, groups):
         part(k).wait_recv()
@@ -1231,56 +1263,64 @@
     for k in range(1, groups):
         result(k).start()
     total_ref[rows(g), :] = summed[...]
-    if fsdp:
+    if vectors:
         for k in range(1, groups):
-            share(k).wait_recv()
-        difference = jnp.zeros(part_ref.shape, F32)
+            few_copy(k).wait()
+        difference = jnp.zeros(mine.shape, F32)
         for n in range(groups):
-            difference = difference + few[members + lax.rem(g + groups - n, groups)]
-        difference = difference / groups
-        momentum, fresh = outer_nesterov(master, outer_ref[...], difference)
-        state_ref[0] = difference
-        state_ref[1] = momentum
-        state_ref[2] = fresh
-        copy_ref[...] = fresh.astype(LOW)
+            difference = difference + few[lax.rem(g + groups - n, groups)]
+        mine[...] = difference / groups
+        stage[f] = mine[...]
+        final_copy.start()
+        final_copy.wait()
+        for n in range(2):
+            difference = stage[n, 0:half]
+            momentum, fresh = outer_nesterov(master_ref[halves[n], :], outer_ref[halves[n], :], difference)
+            state_ref[0, halves[n], :] = difference
+            state_ref[1, halves[n], :] = momentum
+            state_ref[2, halves[n], :] = fresh
+            copy_ref[halves[n], :] = fresh.astype(LOW)
     for k in range(1, groups):
         result(k).wait_recv()
         total_ref[rows(back(k)), :] = landed[groups + k]
     for k in range(1, groups):
         part(k).wait_send()
         result(k).wait_send()
-    if fsdp:
-        for k in range(1, members):
-            piece(k).wait_send()
-        for k in range(1, groups):
-            share(k).wait_send()
-
-
-def group_sum(diff, groups, identity, name, vectors=None, shards=0, fsdp=0):
+
+
+def group_sum(diff, groups, identity, name, vectors=None, shards=0):
     flat = diff.reshape(-1, diff.shape[-1])
     span, cols = flat.shape[0] // groups, flat.shape[1]
     dma = pltpu.SemaphoreType.DMA
     whole = pl.BlockSpec(memory_space=pltpu.VMEM)
     out_shape = [jax.ShapeDtypeStruct(flat.shape, LOW)]
     extra = []
-    if fsdp:
+    if vectors:
         shape = vectors[0].shape
+        half = (-(-shape[0] // 16) * 8, shape[1])
         out_shape += [
             jax.ShapeDtypeStruct((2, *shape), F32),
             jax.ShapeDtypeStruct((3, *shape), F32),
             jax.ShapeDtypeStruct(shape, LOW),
         ]
         extra = [
-            pltpu.VMEM((fsdp * shards + groups, *shape), F32),
-            pltpu.VMEM(shape, F32),
-            dma((fsdp * shards,)),
-            dma((fsdp * shards,)),
+            pltpu.VMEM((2, *half), F32),
+            pltpu.VMEM(half, F32),
+            pltpu.VMEM(half, F32),
+            pltpu.VMEM((shards, *half), F32),
+            pltpu.VMEM((2, *half), F32),
+            pltpu.VMEM((groups, *half), F32),
+            pltpu.VMEM((2, *half), F32),
+            dma((3,)),
+            dma((3,)),
+            dma((shards,)),
+            dma((shards,)),
             dma((groups,)),
             dma((groups,)),
         ]
     total, *rest = pl.pallas_call(
-        functools.partial(group_kernel, groups, shards, fsdp),
-        in_specs=[whole] * (5 if fsdp else 1),
+        functools.partial(group_kernel, groups, shards, bool(vectors)),
+        in_specs=[whole] * (5 if vectors else 1),
         out_specs=[whole] * len(out_shape),
         out_shape=out_shape,
         scratch_shapes=[
@@ -1376,9 +1416,9 @@
     me = lax.axis_index("group").astype(jnp.int32).reshape(1)
     half = attn_master.shape[2] // PARTS
     grads = unattend(qkv, grad_attended, images, seq, 0, PARTS, tensor_size)
-    head_grad, mlp_grads[0] = lax.optimization_barrier((grads[0], mlp_grads[0]))
+    grads, mlp_grads[0] = lax.optimization_barrier((grads, mlp_grads[0]))
     carry, dw_early, head_sums = close(
-        0, PARTS, normed_one, (head_grad, *grads[1:]), w_attn, None, dw_out, None, fsdp, groups, images, seq
+        0, PARTS, normed_one, grads, w_attn, None, dw_out, None, fsdp, groups, images, seq
     )
     if not pairwise:
         halves = jnp.moveaxis(dw_out.reshape(*dw_out.shape[:-1], PARTS, half), -2, 2)
@@ -1388,7 +1428,7 @@
     carry, mlp_grads[1] = lax.optimization_barrier((carry, mlp_grads[1]))
     grads = unattend(qkv, grad_attended, images, seq, 1, PARTS, tensor_size)
 
-    mlp_grads[0], head_grad = lax.optimization_barrier((mlp_grads[0], grads[0]))
+    mlp_grads[0], grads = lax.optimization_barrier((mlp_grads[0], grads))
     mlp_inner, mlp_diff = inner_step(
         beside, mlp_grads, lambda u: (u, 0), 2, mlp_master.shape[2], mlp_master, mlp_moments, None, "inner_mlp"
     )
@@ -1397,7 +1437,7 @@
     if pairwise:
         ending.append(mlp_diff.reshape(-1, mlp_diff.shape[-1]))
     patches_grad, sums_one, *mlp_own, dw_late, sums = close(
-        1, PARTS, normed_one, (head_grad, *grads[1:]), w_attn, carry, None, ending, fsdp, groups, images, seq
+        1, PARTS, normed_one, grads, w_attn, carry, None, ending, fsdp, groups, images, seq
     )
     if not pairwise:
         mlp_own = [exchange_parts(mlp_diff, groups)]
@@ -1429,7 +1469,6 @@
             "group_early",
             [vector_part, vec, vector_moments[0], vector_outer],
             tensor_size,
-            fsdp,
         )
     else:
         (early_total,) = group_sum(early_diff, groups, 10, "group_early")

time: 501 us -> 486 us (0.970)
  the two profiles are of different devices: /device:TPU:9 before, /device:TPU:0 now
where the time goes in v1:
time: 486 us; the launch traced here: 477 us
  Pallas kernels  431 us (89%)
  local copies, waits for them, and re-layouts  25.7 us (5%)
  between operations  14.5 us (3%)
    pallas_call x1, Pallas kernels, front(): pl.pallas_call(functools.partial(front_kernel, images, seq), in_specs=[pl...  120 us
    pallas_call x3, Pallas kernels, mlp(): pl.pallas_call(functools.partial(mlp_kernel, first, pairwise), grid=(step...  96.4 us
    pallas_call x2, Pallas kernels, unattend(): pl.pallas_call(functools.partial(unattend_kernel, seq), grid=(images, wid...  56.8 us
    pallas_call x2, Pallas kernels, close(): pl.pallas_call(functools.partial(close_kernel, seq, images, pairwise, gro...  53 us
    pallas_call x2, Pallas kernels, group_sum(): pl.pallas_call(functools.partial(group_kernel, groups, shards, bool(vecto...  41.9 us
    pallas_call x1, Pallas kernels, turn(): pl.pallas_call(functools.partial(turn_kernel, seq, pairwise), grid=(image...  21.7 us
    pallas_call x3, Pallas kernels, inner_step(): pl.pallas_call(functools.partial(inner_kernel, join, count), grid=(units,...  21.2 us
    pallas_call x3, Pallas kernels, outer_step(): pl.pallas_call(functools.partial(outer_kernel, groups, slots, each), grid...  19.8 us
  transfers between devices with their start and end apart: 8, of which 1 were waited for; matrix products, arithmetic and copies ran while one was open for 2% of the time, Pallas kernels for 55%

profile of v1, /device:TPU:0, one launch (start us, length us, event | category | flops | bytes accessed | tf_op | source)
XLA Modules:
  0.0 476.9 jit_solution(1426139562791782706)
XLA Ops:
  8.6 6.1 %copy_bitcast_fusion = (bf16[2,577,1024]{2,1,0:T(8,128)(2,1)}, bf16[2,577,1024]{2,1,0:T(8,128)(2,1)}) fusion(bf16[1,2,1,577,1024]{4,1,3,2,0:T(2,128)(2,1)} %param.13, bf16[1,2,1,577,1024]{4,1,3,2,0:T(2,128)(2,1)} %param.12), kind=kLoop, calls=%fused_computation | loop fusion | bytes 9453568 | tf_op jit(solution)/shard_map/reshape | solution.py:1388
  15.4 120.1 %front.1 = (bf16[4,4,1024,256]{3,2,1,0:T(8,128)(2,1)}, bf16[4,2,1024,1024]{3,2,1,0:T(8,128)(2,1)}, bf16[1184,1024]{1,0:T(8,128)(2,1)}, bf16[3,1184,1024]{2,1,0:T...) custom-call(f32[2]{0:T(128)} %fusion.alive_ref, ...), custom_call_target="tpu_custom_call" | custom-call | flops 9932111872 | bytes 36372480 | tf_op jit(solution)/shard_map/front/pallas_call | solution.py:1033
  135.5 25.7 %mlp_0.1 = (f32[1184,1024]{1,0:T(8,128)}, f32[1184,1024]{1,0:T(8,128)}, bf16[4,2,512,256]{3,2,1,0:T(8,128)(2,1)}, f32[4,1,256]{2,1,0:T(1,128)}) custom-call(bf16[1184,1024]{1,0:T(8,128)(2,1)} %get-tuple-element.76.n_ref, bf16[1184,1024]{1,0:T(8,128)(2,1)} %get-tuple-element.77.g_ref.g2_ref, bf16[4,2,1024,1024]{3,2,1,0:T(8,128)(2,1)} %get-tuple-element.78.w1_ref.w2_ref, ...), custom_call_target="tpu_custom_call" | custom-call | flops 14898167808 | bytes 29097984 | tf_op jit(solution)/shard_map/mlp_0/pallas_call | solution.py:334
  161.2 26.0 %mlp_1.1 = (f32[1184,1024]{1,0:T(8,128)}, f32[1184,1024]{1,0:T(8,128)}, bf16[4,2,512,256]{3,2,1,0:T(8,128)(2,1)}, f32[4,1,256]{2,1,0:T(1,128)}) custom-call(bf16[1184,1024]{1,0:T(8,128)(2,1)} %get-tuple-element.76.n_ref, bf16[1184,1024]{1,0:T(8,128)(2,1)} %get-tuple-element.77.g_ref.g2_ref, bf16[4,2,1024,1024]{3,2,1,0:T(8,128)(2,1)} %get-tuple-element.78.w1_ref.w2_ref, ...), custom_call_target="tpu_custom_call" | custom-call | flops 14898167808 | bytes 29097984 | tf_op jit(solution)/shard_map/mlp_1/pallas_call | solution.py:334
  187.3 44.7 %mlp_2.1 = (f32[1184,1024]{1,0:T(8,128)}, f32[1184,1024]{1,0:T(8,128)}, bf16[4,2,512,512]{3,2,1,0:T(8,128)(2,1)}, f32[4,1,512]{2,1,0:T(1,128)}) custom-call(bf16[1184,1024]{1,0:T(8,128)(2,1)} %get-tuple-element.76.n_ref, bf16[1184,1024]{1,0:T(8,128)(2,1)} %get-tuple-element.77.g_ref.g2_ref, bf16[4,2,1024,1024]{3,2,1,0:T(8,128)(2,1)} %get-tuple-element.78.w1_ref.w2_ref, ...), custom_call_target="tpu_custom_call" | custom-call | flops 29796335616 | bytes 29097984 | tf_op jit(solution)/shard_map/mlp_2/pallas_call | solution.py:334
  232.1 21.7 %turn.1 = (bf16[2,577,1024]{2,1,0:T(8,128)(2,1)}, f32[1184,1024]{1,0:T(8,128)}, bf16[1184,1024]{1,0:T(8,128)(2,1)}, bf16[4,1,512,256]{3,2,1,0:T(8,128)(2,1)}, f32[4,1024]{1,0:T(4,128)}) custom-call(f32[2]{0:T(128)} %fusion.alive_ref, f32[1184,1024]{1,0:T(8,128)} %get-tuple-element.75.resid_ref, f32[1184,1024]{1,0:T(8,128)} %get-tuple-element.83.y_ref, ...), custom_call_target="tpu_custom_call" | custom-call | flops 4966055936 | bytes 29097984 | tf_op jit(solution)/shard_map/turn/pallas_call | solution.py:428
  253.8 28.4 %unattend_0.1.grad_ref = bf16[3,1184,512]{2,1,0:T(8,128)(2,1)} custom-call(bf16[3,1184,1024]{2,1,0:T(8,128)(2,1)} %get-tuple-element.89.q_ref.k_ref.v_ref, bf16[3,1184,1024]{2,1,0:T(8,128)(2,1)} %get-tuple-element.89.q_ref.k_ref.v_ref, bf16[3,1184,1024]{2,1,0:T(8,128)(2,1)} %get-tuple-element.89.q_ref.k_ref.v_ref, bf16[1184,1024]{1,0:T(8,128)(2,1)} %get-tuple-element.90.g_ref), custom_call_target="tpu_custom_call" | custom-call | flops 14355005440 | bytes 8486912 | tf_op jit(solution)/shard_map/unattend_0/pallas_call | solution.py:495
  282.2 17.4 %close_0.1 = (f32[1184,1024]{1,0:T(8,128)}, bf16[4,5,512,128]{3,2,1,0:T(8,128)(2,1)}, f32[2,512]{1,0:T(2,128)}) custom-call(bf16[1184,1024]{1,0:T(8,128)(2,1)} %get-tuple-element.88.n_ref, bf16[3,1184,512]{2,1,0:T(8,128)(2,1)} %unattend_0.1.grad_ref, bf16[4,4,1024,256]{3,2,1,0:T(8,128)(2,1)} %get-tuple-element.86.w_ref, ...), custom_call_target="tpu_custom_call" | custom-call | flops 7449083904 | bytes 24248320 | tf_op jit(solution)/shard_map/close_0/pallas_call | solution.py:677
  299.7 28.4 %unattend_1.1.grad_ref = bf16[3,1184,512]{2,1,0:T(8,128)(2,1)} custom-call(bf16[3,1184,1024]{2,1,0:T(8,128)(2,1)} %get-tuple-element.89.q_ref.k_ref.v_ref, bf16[3,1184,1024]{2,1,0:T(8,128)(2,1)} %get-tuple-element.89.q_ref.k_ref.v_ref, bf16[3,1184,1024]{2,1,0:T(8,128)(2,1)} %get-tuple-element.89.q_ref.k_ref.v_ref, bf16[1184,1024]{1,0:T(8,128)(2,1)} %get-tuple-element.90.g_ref), custom_call_target="tpu_custom_call" | custom-call | flops 14355005440 | bytes 8486912 | tf_op jit(solution)/shard_map/unattend_1/pallas_call | solution.py:495
  328.1 1.4 reduce-scatter.10.cloned.1.call-done
  329.5 10.2 %inner_mlp.1 = (f32[1,2,2,512,1024]{4,3,2,1,0:T(8,128)}, bf16[2,512,1024]{2,1,0:T(8,128)(2,1)}) custom-call(bf16[2,512,256]{2,1,0:T(8,128)(2,1)} %bitcast.40, bf16[2,512,256]{2,1,0:T(8,128)(2,1)} %bitcast.41, bf16[2,512,512]{2,1,0:T(8,128)(2,1)} %bitcast.36, f32[2,512,1024]{2,1,0:T(8,128)} %refs_4_.3, f32[1,2,2,512,1024]{4,3,2,1,0:T(8,128)} %refs_4_.2), custom_call_target="tpu_custom_call" | custom-call | flops 31457280 | bytes 25165824 | tf_op jit(solution)/shard_map/inner_mlp/pallas_call | solution.py:1102
  339.8 35.6 %close_1.1 = (f32[2,577,1,1024]{3,2,1,0:T(1,128)}, f32[2,1024]{1,0:T(2,128)}, bf16[256,1024]{1,0:T(8,128)(2,1)}, bf16[4,3,512,128]{3,2,1,0:T(8,128)(2,1)}, f32[2,512]{1,0:T(2,128)}) custom-call(bf16[1184,1024]{1,0:T(8,128)(2,1)} %get-tuple-element.88.n_ref, bf16[3,1184,512]{2,1,0:T(8,128)(2,1)} %unattend_1.1.grad_ref, ...), custom_call_target="tpu_custom_call" | custom-call | flops 7449083904 | bytes 24248320 | tf_op jit(solution)/shard_map/close_1/pallas_call | solution.py:677
  375.4 2.3 collective-permute-start.2
  380.3 3.8 copy.32
  384.3 1.3 concatenate.11.refs_0_
  385.6 6.6 %inner_early.1 = (f32[1,2,4,512,256]{4,3,2,1,0:T(8,128)}, bf16[5,512,128]{2,1,0:T(8,128)(2,1)}) custom-call(bf16[5,512,128]{2,1,0:T(8,128)(2,1)} %bitcast.39, f32[4,512,256]{2,1,0:T(8,128)} %refs_1_.9, f32[1,2,4,512,256]{4,3,2,1,0:T(8,128)} %refs_2_.6), custom_call_target="tpu_custom_call" | custom-call | flops 9830400 | bytes 7864320 | tf_op jit(solution)/shard_map/inner_early/pallas_call | solution.py:1102
  392.2 26.4 %group_early.1 = (bf16[2560,128]{1,0:T(8,128)(2,1)}, f32[2,12,1024]{2,1,0:T(8,128)}, f32[3,12,1024]{2,1,0:T(8,128)}, bf16[12,1024]{1,0:T(8,128)(2,1)}) custom-call(bf16[2560,128]{1,0:T(8,128)(2,1)} %bitcast.38, f32[12,1024]{1,0:T(8,128)} %concatenate.11.refs_0_, f32[12,1024]{1,0:T(8,128)} %refs_1_.6, f32[2,12,1024]{2,1,0:T(8,128)} %bitcast.42, ...), custom_call_target="tpu_custom_call" | custom-call | flops 1310720 | bytes 2621440 | tf_op jit(solution)/shard_map/group_early/pallas_call | solution.py:1321
  418.5 1.6 copy.34
  420.2 5.6 %outer_early.1 = (f32[3,4,512,256]{3,2,1,0:T(8,128)}, bf16[4,512,256]{2,1,0:T(8,128)(2,1)}) custom-call(s32[1]{0:T(128)} %bitcast.14.g_ref, bf16[5,512,128]{2,1,0:T(8,128)(2,1)} %bitcast.37, f32[4,512,256]{2,1,0:T(8,128)} %refs_1_.9, f32[4,512,256]{2,1,0:T(8,128)} %refs_2_.7), custom_call_target="tpu_custom_call" | custom-call | flops 3276800 | bytes 7864320 | tf_op jit(solution)/shard_map/outer_early/pallas_call | solution.py:1150
  426.7 10.4 %outer_mlp.1 = (f32[3,2,512,1024]{3,2,1,0:T(8,128)}, bf16[2,512,1024]{2,1,0:T(8,128)(2,1)}) custom-call(s32[1]{0:T(128)} %bitcast.14.g_ref, bf16[256,1024]{1,0:T(8,128)(2,1)} %get-tuple-element.120.refs_0_, bf16[256,1024]{1,0:T(8,128)(2,1)} %collective-permute-done.refs_1_, bf16[256,1024]{1,0:T(8,128)(2,1)} %copy-done.2, bf16[256,1024]{1,0:T(8,128)(2,1)} %copy-done.1, ...), custom_call_target="tpu_custom_call" | custom-call | flops 10485760 | bytes 25165824 | tf_op jit(solution)/shard_map/outer_mlp/pallas_call | solution.py:1150
  437.1 4.3 inner_late.1
  441.5 15.5 %group_late.1 = bf16[1536,128]{1,0:T(8,128)(2,1)} custom-call(bf16[1536,128]{1,0:T(8,128)(2,1)} %bitcast.43), custom_call_target="tpu_custom_call" | custom-call | flops 786432 | bytes 1572864 | tf_op jit(solution)/shard_map/group_late/pallas_call | solution.py:1321
  457.0 3.8 outer_late.1
  460.8 7.8 %copy.46 = f32[1,2,1,577,1024]{4,2,3,1,0:T(1,128)} copy(f32[1,2,1,577,1024]{4,2,3,1,0:T(1,128)} %bitcast.32) | data formatting | bytes 9453568
  (60 shorter events, 7.4 us)
Async XLA Ops:
  7.2 275.0 %reduce-scatter.6.cloned.1.call-start = ((), (), s32[]{:S(2)}) async-start(), calls=%async_computation.5 | async-start | bytes 2621440 | tf_op jit(solution)/shard_map/reduce_scatter | solution.py:1362
  8.6 6.1 %copy-start.12 = (s32[1,2,2]{2,1,0:T(2,128)S(1)}, s32[1,2,2]{2,1,0:T(2,128)}, u32[]{:S(2)}) copy-start(s32[1,2,2]{2,1,0:T(2,128)} %param.14) | copy-start | bytes 52
  161.2 167.0 %reduce-scatter.8.cloned.1.call-start = ((), (), s32[]{:S(2)}) async-start(), calls=%async_computation.6 | async-start | bytes 2621440 | tf_op jit(solution)/shard_map/reduce_scatter | solution.py:1362
  187.3 142.2 %reduce-scatter.10.cloned.1.call-start = ((), (), s32[]{:S(2)}) async-start(), calls=%async_computation.7 | async-start | bytes 5242880 | tf_op jit(solution)/shard_map/reduce_scatter | solution.py:1362
  232.0 153.5 %reduce-scatter.14.cloned.1.call-start = ((), (), s32[]{:S(2)}) async-start(), calls=%async_computation.9 | async-start | bytes 3276800 | tf_op jit(solution)/shard_map/reduce_scatter | solution.py:1362
  299.6 137.5 %reduce-scatter.12.cloned.1.call-start = ((), (), s32[]{:S(2)}) async-start(), calls=%async_computation.8 | async-start | bytes 1966080 | tf_op jit(solution)/shard_map/reduce_scatter | solution.py:1362
  339.8 39.2 %copy-start.4 = (f32[1,2,12,1024]{3,1,2,0:T(2,128)S(1)}, f32[1,2,12,1024]{3,1,2,0:T(2,128)}, u32[]{:S(2)}) copy-start(f32[1,2,12,1024]{3,1,2,0:T(2,128)} %param.20) | copy-start | bytes 294916
  339.8 40.6 %copy-start = (bf16[2,577,1024]{2,1,0:T(8,128)(2,1)S(1)}, bf16[2,577,1024]{2,1,0:T(8,128)(2,1)}, u32[]{:S(2)}) copy-start(bf16[2,577,1024]{2,1,0:T(8,128)(2,1)} %get-tuple-element.87) | copy-start | bytes 7090180
  375.3 8.8 %copy-start.6 = (f32[4,1024]{1,0:T(4,128)S(1)}, f32[4,1024]{1,0:T(4,128)}, u32[]{:S(2)}) copy-start(f32[4,1024]{1,0:T(4,128)} %get-tuple-element.111) | copy-start | bytes 49156
  375.4 50.4 %collective-permute-start.2 = (bf16[256,1024]{1,0:T(8,128)(2,1)}, bf16[256,1024]{1,0:T(8,128)(2,1)S(1)}, u32[]{:S(2)}, u32[]{:S(2)}) collective-permute-start(bf16[256,1024]{1,0:T(8,128)(2,1)} %get-tuple-element.120.refs_0_), channel_id=1, source_target_pairs={{0,24},{8,0},{16,8},{24,16},{1,25},{9,1},{17,9},{25,17},{2,26},{10... | collective-permute-start | bytes 1572872 | tf_op jit(solution)/shard_map/ppermute | solution.py:1345
  377.6 48.1 %collective-permute-start.1 = (bf16[256,1024]{1,0:T(8,128)(2,1)}, bf16[256,1024]{1,0:T(8,128)(2,1)S(1)}, u32[]{:S(2)}, u32[]{:S(2)}) collective-permute-start(bf16[256,1024]{1,0:T(8,128)(2,1)} %get-tuple-element.120.refs_0_), channel_id=1, source_target_pairs={{0,16},{8,24},{16,0},{24,8},{1,17},{9,25},{17,1},{25,9},{2,18},{10... | collective-permute-start | bytes 1572872 | tf_op jit(solution)/shard_map/ppermute | solution.py:1345
  378.2 47.6 %collective-permute-start = (bf16[256,1024]{1,0:T(8,128)(2,1)}, bf16[256,1024]{1,0:T(8,128)(2,1)}, u32[]{:S(2)}, u32[]{:S(2)}) collective-permute-start(bf16[256,1024]{1,0:T(8,128)(2,1)} %get-tuple-element.120.refs_0_), channel_id=1, source_target_pairs={{0,8},{8,16},{16,24},{24,0},{1,9},{9,17},{17,25},{25,1},{2,10},{10... | collective-permute-start | bytes 1572872 | tf_op jit(solution)/shard_map/ppermute | solution.py:1345
  378.9 5.2 %copy-start.9 = (f32[4,1,256]{2,1,0:T(1,128)S(1)}, f32[4,1,256]{2,1,0:T(1,128)}, u32[]{:S(2)}) copy-start(f32[4,1,256]{2,1,0:T(1,128)} %get-tuple-element.115) | copy-start | bytes 12292
  378.9 5.2 %copy-start.8 = (f32[4,1,512]{2,1,0:T(1,128)S(1)}, f32[4,1,512]{2,1,0:T(1,128)}, u32[]{:S(2)}) copy-start(f32[4,1,512]{2,1,0:T(1,128)} %get-tuple-element.116) | copy-start | bytes 24580
  379.6 4.6 copy-start.10
  379.6 4.6 copy-start.11
  379.6 4.7 copy-start.7
  425.7 0.8 copy-start.1
  425.8 1.0 copy-start.2
  460.8 7.8 %copy-start.3 = (f32[3,12,1024]{2,1,0:T(8,128)S(1)}, f32[3,12,1024]{2,1,0:T(8,128)}, u32[]{:S(2)}) copy-start(f32[3,12,1024]{2,1,0:T(8,128)} %get-tuple-element.185) | copy-start | bytes 442372
  460.8 8.5 %copy-start.5 = (bf16[12,1024]{1,0:T(8,128)(2,1)S(1)}, bf16[12,1024]{1,0:T(8,128)(2,1)}, u32[]{:S(2)}) copy-start(bf16[12,1024]{1,0:T(8,128)(2,1)} %get-tuple-element.186) | copy-start | bytes 73732
Sparse Core Ops, SparseCore 0:
  161.3 44.0 reduce-scatter.5
  207.8 43.1 reduce-scatter.7
  253.3 76.1 reduce-scatter.9
  331.8 52.5 reduce-scatter.13
  386.7 37.0 reduce-scatter.11

commit v2 on v1

--- a/solution.py
+++ b/solution.py
@@ -506,24 +506,18 @@
     )(qkv, qkv, qkv, grad_attended)
 
 
-def close_kernel(seq, images, pairwise, groups, first, final, n_ref, grad_ref, w_ref, *refs):
+def close_kernel(pairwise, groups, first, final, n_ref, grad_ref, w_ref, *refs):
     if not first:
         carry_ref, *refs = refs
     elif pairwise:
         more_ref, *refs = refs
-    if final:
-        x_ref, gr_ref, vec_ref, *refs = refs
-        if pairwise:
-            diff_ref, *refs = refs
-        out_ref, norm_ref, *refs = refs
-        if pairwise:
-            total_ref, *refs = refs
+    if pairwise and final:
+        diff_ref, acc_ref, total_ref, *refs = refs
     else:
         acc_ref, *refs = refs
     dw_ref, sums_ref, acc_scr, *exchange = refs
     j = pl.program_id(0)
     shards, _, _, cols = w_ref.shape
-    span = n_ref.shape[0] // images
     if pairwise:
         own, sent, received, sends, receives, *exchange = exchange
         if not final:
@@ -604,20 +598,8 @@
                 for t in range(shards):
                     for n in range(dw_ref.shape[1] - 3):
                         dw_ref[t, 3 + n] = more_ref[t, 0, :, n * cols : (n + 1) * cols]
-        if not final:
-            acc_ref[...] = acc_scr[...]
-            return
-        gain = jnp.zeros((1, vec_ref.shape[1]), F32)
-        shift = jnp.zeros((1, vec_ref.shape[1]), F32)
-        for i in range(images):
-            normal, inverse = centred(x_ref[i].astype(F32))
-            upstream = acc_scr[i * span : i * span + seq, :]
-            out_ref[i, :, 0, :] = gr_ref[i * span : i * span + seq, :] + norm_back(upstream, normal, inverse, vec_ref[0:1])
-            gain += jnp.sum(upstream * normal, axis=0, keepdims=True)
-            shift += jnp.sum(upstream, axis=0, keepdims=True)
-        norm_ref[0:1, :] = gain
-        norm_ref[1:2, :] = shift
-        if pairwise:
+        acc_ref[...] = acc_scr[...]
+        if pairwise and final:
             keep.wait()
             total = mine[...].astype(F32)
             for k in range(1, groups):
@@ -626,7 +608,7 @@
             total_ref[...] = total.astype(LOW)
 
 
-def close(part, parts, normed, grads, w_attn, carry, more, ending, fsdp, groups, images, seq):
+def close(part, parts, normed, grads, w_attn, carry, more, ending, fsdp, groups):
     rows, width = normed.shape
     shards, _, _, cols = w_attn.shape
     cols = cols // parts
@@ -636,7 +618,6 @@
     single = pl.Buffered(1)
     stack = pl.BlockSpec((1, rows, lanes), lambda j: (j, 0, 0))
     full = pl.BlockSpec((rows, width), lambda j: (0, 0), pipeline_mode=single)
-    image = pl.BlockSpec((images, seq, width), lambda j: (0, 0, 0), pipeline_mode=single)
     if pairwise:
         many = 3 + parts if first else 3
         dw_spec = pl.BlockSpec((shards, many, depth, cols), lambda j: (0, 0, 0, 0), pipeline_mode=single)
@@ -652,30 +633,24 @@
         in_specs.append(full)
     elif pairwise:
         in_specs.append(pl.BlockSpec(more.shape, lambda j: (0, 0, 0, 0), pipeline_mode=single))
-    if final:
-        in_specs += [image, full, pl.BlockSpec((12, width), lambda j: (0, 0))]
-        flat = pl.BlockSpec((images, seq, 1, width), lambda j: (0, 0, 0, 0), pipeline_mode=single)
-        out_specs += [flat, pl.BlockSpec((2, width), lambda j: (0, 0))]
-        out_shape += [jax.ShapeDtypeStruct((images, seq, 1, width), F32), jax.ShapeDtypeStruct((2, width), F32)]
-        if pairwise:
-            quarter, lanes_two = ending[3].shape[0] // groups, ending[3].shape[1]
-            in_specs.append(pl.BlockSpec(memory_space=pl.ANY))
-            out_specs.append(pl.BlockSpec((quarter, lanes_two), lambda j: (0, 0), pipeline_mode=single))
-            out_shape.append(jax.ShapeDtypeStruct((quarter, lanes_two), LOW))
-            dma = pltpu.SemaphoreType.DMA
-            extra = [
-                *extra,
-                pltpu.VMEM((quarter, lanes_two), LOW),
-                pltpu.VMEM((groups, quarter, lanes_two), LOW),
-                dma((groups,)),
-                dma((groups,)),
-                dma((1,)),
-            ]
-    else:
-        out_specs.append(full)
-        out_shape.append(jax.ShapeDtypeStruct((rows, width), F32))
+    out_specs.append(full)
+    out_shape.append(jax.ShapeDtypeStruct((rows, width), F32))
+    if pairwise and final:
+        quarter, lanes_two = ending.shape[0] // groups, ending.shape[1]
+        in_specs.append(pl.BlockSpec(memory_space=pl.ANY))
+        out_specs.append(pl.BlockSpec((quarter, lanes_two), lambda j: (0, 0), pipeline_mode=single))
+        out_shape.append(jax.ShapeDtypeStruct((quarter, lanes_two), LOW))
+        dma = pltpu.SemaphoreType.DMA
+        extra = [
+            *extra,
+            pltpu.VMEM((quarter, lanes_two), LOW),
+            pltpu.VMEM((groups, quarter, lanes_two), LOW),
+            dma((groups,)),
+            dma((groups,)),
+            dma((1,)),
+        ]
     return pl.pallas_call(
-        functools.partial(close_kernel, seq, images, pairwise, groups, first, final),
+        functools.partial(close_kernel, pairwise, groups, first, final),
         grid=(3,),
         in_specs=in_specs,
         out_specs=[*out_specs, dw_spec, pl.BlockSpec((2, lanes), lambda j: (0, 0))],
@@ -684,7 +659,44 @@
         compiler_params=params(7 + part if pairwise else None),
         cost_estimate=cost(12 * rows * width * lanes, 20 * rows * width),
         name=f"close_{part}",
-    )(normed, grads, w_attn, *([carry] if not first else [more] if pairwise else []), *(ending if final else []))
+    )(normed, grads, w_attn, *([carry] if not first else [more] if pairwise else []), *([ending] if pairwise and final else []))
+
+
+def finish_kernel(acc_ref, gr_ref, x_ref, vec_ref, out_ref, norm_ref):
+    i = pl.program_id(0)
+    seq = out_ref.shape[1]
+    normal, inverse = centred(x_ref[...].astype(F32))
+    upstream = acc_ref[...]
+    grad = gr_ref[...] + norm_back(upstream, normal, inverse, vec_ref[0:1])
+    out_ref[0, :, 0, :] = grad[0:seq]
+    sums = [jnp.sum(upstream * normal, axis=0, keepdims=True), jnp.sum(upstream, axis=0, keepdims=True)]
+    sums = jnp.concatenate(sums, axis=0)
+
+    @pl.when(i == 0)
+    def _():
+        norm_ref[...] = sums
+
+    @pl.when(i != 0)
+    def _():
+        norm_ref[...] += sums
+
+
+def finish(acc, grad_resid, x_rows, vec, images, seq):
+    rows, width = acc.shape
+    block = pl.BlockSpec((rows // images, width), lambda i: (i, 0))
+    return pl.pallas_call(
+        finish_kernel,
+        grid=(images,),
+        in_specs=[block, block, block, pl.BlockSpec(vec.shape, lambda i: (0, 0))],
+        out_specs=[pl.BlockSpec((1, seq, 1, width), lambda i: (i, 0, 0, 0)), pl.BlockSpec((2, width), lambda i: (0, 0))],
+        out_shape=[
+            jax.ShapeDtypeStruct((images, seq, 1, width), F32),
+            jax.ShapeDtypeStruct((2, width), F32),
+        ],
+        compiler_params=params(),
+        cost_estimate=cost(20 * rows * width, 14 * rows * width),
+        name="finish",
+    )(acc, grad_resid, x_rows, vec)
 
 
 def attend_pair(seq, q, k, v):
@@ -705,8 +717,8 @@
 
 def front_kernel(
     images, seq, alive_ref, a_in, m_in, x_ref, g_ref, vec_ref,
-    a_out, m_out, n_out, qkv_out, att_out, resid_out, n2_out, g2_out,
-    a_wide, m_wide, a_hold, m_hold, n_scr, qkv_scr, att_scr, w_scr, o_scr, x_scr, resid_scr, n2_scr, g2_scr,
+    a_out, m_out, n_out, qkv_out, att_out, resid_out, n2_out, g2_out, x_out,
+    a_wide, m_wide, a_hold, m_hold, n_scr, qkv_scr, att_scr, w_scr, o_scr, resid_scr, n2_scr, g2_scr, x_all,
     zs, zr, xs, xr, ys, yr, xfs, xfr, yfs, yfr, cs, cr, ls, ws,
 ):
     g, f, z = lax.axis_index("group"), lax.axis_index("fsdp"), lax.axis_index("tensor")
@@ -884,20 +896,25 @@
     own(0)
     loads[1].start()
     n_scr[...] = jnp.zeros_like(n_scr)
-
-    def norm_image(i, carry):
-        normal, _ = centred(x_ref[i].astype(F32))
-        n_scr[pl.ds(pl.multiple_of(i * span, 16), seq), :] = (normal * vec_ref[0:1] + vec_ref[1:2]).astype(LOW)
-        return carry
-
-    lax.fori_loop(0, images, norm_image, 0)
+    x_all[...] = jnp.zeros_like(x_all)
+    g2_scr[...] = jnp.zeros_like(g2_scr)
+    for i in range(images):
+        here = pl.ds(i * span, seq)
+        image = x_ref[:, i, :]
+        x_all[here, :] = image
+        normal, _ = centred(image.astype(F32))
+        n_scr[here, :] = (normal * vec_ref[0:1] + vec_ref[1:2]).astype(LOW)
     puts = [pltpu.make_async_copy(n_scr, n_out, ws.at[1])]
     puts[0].start()
+    puts.append(pltpu.make_async_copy(x_all, x_out, ws.at[7]))
+    puts[-1].start()
     both(land, 0, 1)
     loads[1].wait()
     m_hold[...] = m_wide[...].astype(LOW)
     keeps[1].start()
     maps(z)
+    for i in range(images):
+        g2_scr[pl.ds(i * span, seq), :] = (g_ref[:, i, :].astype(F32) * alive_ref[i]).astype(LOW)
     both(land, 0, 2)
     both(relay, 0, 1)
     keeps[1].wait()
@@ -961,19 +978,15 @@
     take = pltpu.make_async_copy(a_out.at[:, 3], o_scr, ws.at[0])
     take.start()
     take.wait()
-    x_scr[...] = jnp.zeros_like(x_scr)
 
     def mix_image(i, carry):
         here = pl.ds(pl.multiple_of(i * span, 16), span)
-        x_scr[0:seq, :] = x_ref[i].astype(F32)
-        out = x_scr[...] + vec_ref[6:7]
+        out = x_all[here, :].astype(F32) + vec_ref[6:7]
         for t in range(shards):
             out = out + dot(att_scr[here, t * cols : (t + 1) * cols], o_scr[t], NT)
         resid_scr[here, :] = out
         normal, _ = centred(out)
         n2_scr[here, :] = (normal * vec_ref[2:3] + vec_ref[3:4]).astype(LOW)
-        x_scr[0:seq, :] = g_ref[i].astype(F32) * alive_ref[i]
-        g2_scr[here, :] = x_scr[...].astype(LOW)
         for c in range(min(images, total - at)):
             pl.when(i == c)(functools.partial(advance, at + c))
         return carry
@@ -1024,7 +1037,7 @@
 def front(alive, attn_master, mlp_master, patches, cotangent, vec, shards):
     _, depth, a_cols = attn_master.shape
     _, _, m_cols = mlp_master.shape
-    images, seq, width = patches.shape
+    seq, images, width = patches.shape
     rows = images * padded(seq)
     anywhere = pl.BlockSpec(memory_space=pl.ANY)
     inside = pl.BlockSpec(memory_space=pltpu.VMEM)
@@ -1033,7 +1046,7 @@
     return pl.pallas_call(
         functools.partial(front_kernel, images, seq),
         in_specs=[pl.BlockSpec(memory_space=pltpu.SMEM), anywhere, anywhere, inside, inside, inside],
-        out_specs=[anywhere] * 8,
+        out_specs=[anywhere] * 9,
         out_shape=[
             jax.ShapeDtypeStruct((shards, 4, width, a_cols), LOW),
             jax.ShapeDtypeStruct((shards, 2, width, m_cols), LOW),
@@ -1041,6 +1054,7 @@
             jax.ShapeDtypeStruct((3, rows, width), LOW),
             low,
             jax.ShapeDtypeStruct((rows, width), F32),
+            low,
             low,
             low,
         ],
@@ -1054,14 +1068,14 @@
             pltpu.VMEM((rows, width), LOW),
             pltpu.VMEM((3, width, a_cols), LOW),
             pltpu.VMEM((shards, width, a_cols), LOW),
-            pltpu.VMEM((rows // images, width), F32),
             pltpu.VMEM((rows, width), F32),
+            pltpu.VMEM((rows, width), LOW),
             pltpu.VMEM((rows, width), LOW),
             pltpu.VMEM((rows, width), LOW),
             dma((4, shards, 2)),
         ]
         + [dma((4, shards))] * 11
-        + [dma((4,)), dma((7,))],
+        + [dma((4,)), dma((8,))],
         compiler_params=params(1),
         cost_estimate=cost(8 * rows * width * width, 30 * rows * width),
         name="front",
@@ -1389,8 +1403,11 @@
     images = x.shape[0]
 
     if (groups, fsdp) == (4, 2):
-        w_attn, w_mlp, normed_one, qkv, attended, resid, normed_two, grad_two = front(
-            alive, attn_master, mlp_master, x, cotangent, vec, tensor_size
+        beside_images = [
+            jnp.moveaxis(v.reshape(images, seq, width), 0, 1) for v in (patches, output_grad)
+        ]
+        w_attn, w_mlp, normed_one, qkv, attended, resid, normed_two, grad_two, x_rows = front(
+            alive, attn_master, mlp_master, *beside_images, vec, tensor_size
         )
     else:
         w_attn = gather_weights(attn_master.astype(LOW))
@@ -1398,6 +1415,7 @@
         normed_one, qkv = project(x, w_attn, vec)
         attended = attend(qkv, images, seq)
         resid, normed_two, grad_two = mix(alive, attended, x, cotangent, w_attn, vec)
+        x_rows = jnp.pad(x, ((0, 0), (0, padded(seq) - seq), (0, 0))).reshape(-1, width)
     bias = vec[8:].reshape(tensor_size, 1, -1)
     carried = None
     mlp_grads, bias_parts = [], []
@@ -1418,7 +1436,7 @@
     grads = unattend(qkv, grad_attended, images, seq, 0, PARTS, tensor_size)
     grads, mlp_grads[0] = lax.optimization_barrier((grads, mlp_grads[0]))
     carry, dw_early, head_sums = close(
-        0, PARTS, normed_one, grads, w_attn, None, dw_out, None, fsdp, groups, images, seq
+        0, PARTS, normed_one, grads, w_attn, None, dw_out, None, fsdp, groups
     )
     if not pairwise:
         halves = jnp.moveaxis(dw_out.reshape(*dw_out.shape[:-1], PARTS, half), -2, 2)
@@ -1433,12 +1451,11 @@
         beside, mlp_grads, lambda u: (u, 0), 2, mlp_master.shape[2], mlp_master, mlp_moments, None, "inner_mlp"
     )
     carry, mlp_diff = lax.optimization_barrier((carry, mlp_diff))
-    ending = [x, grad_resid, vec]
-    if pairwise:
-        ending.append(mlp_diff.reshape(-1, mlp_diff.shape[-1]))
-    patches_grad, sums_one, *mlp_own, dw_late, sums = close(
-        1, PARTS, normed_one, grads, w_attn, carry, None, ending, fsdp, groups, images, seq
+    ending = mlp_diff.reshape(-1, mlp_diff.shape[-1])
+    carry, *mlp_own, dw_late, sums = close(
+        1, PARTS, normed_one, grads, w_attn, carry, None, ending, fsdp, groups
     )
+    patches_grad, sums_one = finish(carry, grad_resid, x_rows, vec, images, seq)
     if not pairwise:
         mlp_own = [exchange_parts(mlp_diff, groups)]
     mlp_total = exchange_total(mlp_own[0], groups)

time: 486 us -> 484 us (level)
  local copies, waits for them, and re-layouts: 25.7 us -> 12.5 us
  Pallas kernels: 431 us -> 441 us
    unnamed x33 -> x28, local copies, waits for them, and re-layouts: 16.2 us -> 8.47 us
    pallas_call x2 -> x3, Pallas kernels: 53 us -> 60.1 us  [the longest x2 50.3 us: close(): pl.pallas_call(functools.partial(close_kernel, pairwise, groups, first, f...]
    reshape x1 -> x0, local copies, waits for them, and re-layouts: 6.05 us -> none  [local(): cotangent = output_grad.reshape(-1, seq, width)]
    pallas_call x1, Pallas kernels: 120 us -> 125 us  [front(): pl.pallas_call(functools.partial(front_kernel, images, seq), in_specs=[pl...]
  transfers between devices with their start and end apart: 8 -> 8, of which waited for: 1 -> 1; matrix products, arithmetic and copies ran while one was open for 2% -> 2% of each run, Pallas kernels for 55% -> 56%
where the time goes in v2:
time: 484 us; the launch traced here: 475 us
  Pallas kernels  441 us (91%)
  between operations  14.2 us (3%)
  local copies, waits for them, and re-layouts  12.5 us (3%)
    pallas_call x1, Pallas kernels, front(): pl.pallas_call(functools.partial(front_kernel, images, seq), in_specs=[pl...  125 us
    pallas_call x3, Pallas kernels, mlp(): pl.pallas_call(functools.partial(mlp_kernel, first, pairwise), grid=(step...  96 us
    pallas_call x2, Pallas kernels, unattend(): pl.pallas_call(functools.partial(unattend_kernel, seq), grid=(images, wid...  57 us
    pallas_call x2, Pallas kernels, close(): pl.pallas_call(functools.partial(close_kernel, pairwise, groups, first, f...  50.3 us
    pallas_call x2, Pallas kernels, group_sum(): pl.pallas_call(functools.partial(group_kernel, groups, shards, bool(vecto...  39.7 us
    pallas_call x1, Pallas kernels, turn(): pl.pallas_call(functools.partial(turn_kernel, seq, pairwise), grid=(image...  22 us
    pallas_call x3, Pallas kernels, inner_step(): pl.pallas_call(functools.partial(inner_kernel, join, count), grid=(units,...  20.9 us
    pallas_call x3, Pallas kernels, outer_step(): pl.pallas_call(functools.partial(outer_kernel, groups, slots, each), grid...  19.8 us
  transfers between devices with their start and end apart: 8, of which 1 were waited for; matrix products, arithmetic and copies ran while one was open for 2% of the time, Pallas kernels for 56%

profile of v2, /device:TPU:0, one launch (start us, length us, event | category | flops | bytes accessed | tf_op | source)
XLA Modules:
  0.0 475.2 jit_solution(4551141306170437320)
XLA Ops:
  8.6 1.4 fusion.alive_ref
  10.0 125.1 %front.1 = (bf16[4,4,1024,256]{3,2,1,0:T(8,128)(2,1)}, bf16[4,2,1024,1024]{3,2,1,0:T(8,128)(2,1)}, bf16[1184,1024]{1,0:T(8,128)(2,1)}, bf16[3,1184,1024]{2,1,0:T...) custom-call(f32[2]{0:T(128)} %fusion.alive_ref, ...), custom_call_target="tpu_custom_call" | custom-call | flops 9932111872 | bytes 36372480 | tf_op jit(solution)/shard_map/front/pallas_call | solution.py:1046
  135.2 25.6 %mlp_0.1 = (f32[1184,1024]{1,0:T(8,128)}, f32[1184,1024]{1,0:T(8,128)}, bf16[4,2,512,256]{3,2,1,0:T(8,128)(2,1)}, f32[4,1,256]{2,1,0:T(1,128)}) custom-call(bf16[1184,1024]{1,0:T(8,128)(2,1)} %get-tuple-element.78.n_ref, bf16[1184,1024]{1,0:T(8,128)(2,1)} %get-tuple-element.79.g_ref.g2_ref, bf16[4,2,1024,1024]{3,2,1,0:T(8,128)(2,1)} %get-tuple-element.80.w1_ref.w2_ref, ...), custom_call_target="tpu_custom_call" | custom-call | flops 14898167808 | bytes 29097984 | tf_op jit(solution)/shard_map/mlp_0/pallas_call | solution.py:334
  160.9 25.9 %mlp_1.1 = (f32[1184,1024]{1,0:T(8,128)}, f32[1184,1024]{1,0:T(8,128)}, bf16[4,2,512,256]{3,2,1,0:T(8,128)(2,1)}, f32[4,1,256]{2,1,0:T(1,128)}) custom-call(bf16[1184,1024]{1,0:T(8,128)(2,1)} %get-tuple-element.78.n_ref, bf16[1184,1024]{1,0:T(8,128)(2,1)} %get-tuple-element.79.g_ref.g2_ref, bf16[4,2,1024,1024]{3,2,1,0:T(8,128)(2,1)} %get-tuple-element.80.w1_ref.w2_ref, ...), custom_call_target="tpu_custom_call" | custom-call | flops 14898167808 | bytes 29097984 | tf_op jit(solution)/shard_map/mlp_1/pallas_call | solution.py:334
  186.9 44.5 %mlp_2.1 = (f32[1184,1024]{1,0:T(8,128)}, f32[1184,1024]{1,0:T(8,128)}, bf16[4,2,512,512]{3,2,1,0:T(8,128)(2,1)}, f32[4,1,512]{2,1,0:T(1,128)}) custom-call(bf16[1184,1024]{1,0:T(8,128)(2,1)} %get-tuple-element.78.n_ref, bf16[1184,1024]{1,0:T(8,128)(2,1)} %get-tuple-element.79.g_ref.g2_ref, bf16[4,2,1024,1024]{3,2,1,0:T(8,128)(2,1)} %get-tuple-element.80.w1_ref.w2_ref, ...), custom_call_target="tpu_custom_call" | custom-call | flops 29796335616 | bytes 29097984 | tf_op jit(solution)/shard_map/mlp_2/pallas_call | solution.py:334
  231.4 22.0 %turn.1 = (bf16[2,577,1024]{2,1,0:T(8,128)(2,1)}, f32[1184,1024]{1,0:T(8,128)}, bf16[1184,1024]{1,0:T(8,128)(2,1)}, bf16[4,1,512,256]{3,2,1,0:T(8,128)(2,1)}, f32[4,1024]{1,0:T(4,128)}) custom-call(f32[2]{0:T(128)} %fusion.alive_ref, f32[1184,1024]{1,0:T(8,128)} %get-tuple-element.77.resid_ref, f32[1184,1024]{1,0:T(8,128)} %get-tuple-element.85.y_ref, ...), custom_call_target="tpu_custom_call" | custom-call | flops 4966055936 | bytes 29097984 | tf_op jit(solution)/shard_map/turn/pallas_call | solution.py:428
  253.5 28.4 %unattend_0.1.grad_ref = bf16[3,1184,512]{2,1,0:T(8,128)(2,1)} custom-call(bf16[3,1184,1024]{2,1,0:T(8,128)(2,1)} %get-tuple-element.91.q_ref.k_ref.v_ref, bf16[3,1184,1024]{2,1,0:T(8,128)(2,1)} %get-tuple-element.91.q_ref.k_ref.v_ref, bf16[3,1184,1024]{2,1,0:T(8,128)(2,1)} %get-tuple-element.91.q_ref.k_ref.v_ref, bf16[1184,1024]{1,0:T(8,128)(2,1)} %get-tuple-element.92.g_ref), custom_call_target="tpu_custom_call" | custom-call | flops 14355005440 | bytes 8486912 | tf_op jit(solution)/shard_map/unattend_0/pallas_call | solution.py:495
  281.9 17.1 %close_0.1 = (f32[1184,1024]{1,0:T(8,128)}, bf16[4,5,512,128]{3,2,1,0:T(8,128)(2,1)}, f32[2,512]{1,0:T(2,128)}) custom-call(bf16[1184,1024]{1,0:T(8,128)(2,1)} %get-tuple-element.90.n_ref, bf16[3,1184,512]{2,1,0:T(8,128)(2,1)} %unattend_0.1.grad_ref, bf16[4,4,1024,256]{3,2,1,0:T(8,128)(2,1)} %get-tuple-element.88.w_ref, ...), custom_call_target="tpu_custom_call" | custom-call | flops 7449083904 | bytes 24248320 | tf_op jit(solution)/shard_map/close_0/pallas_call | solution.py:652
  299.1 28.6 %unattend_1.1.grad_ref = bf16[3,1184,512]{2,1,0:T(8,128)(2,1)} custom-call(bf16[3,1184,1024]{2,1,0:T(8,128)(2,1)} %get-tuple-element.91.q_ref.k_ref.v_ref, bf16[3,1184,1024]{2,1,0:T(8,128)(2,1)} %get-tuple-element.91.q_ref.k_ref.v_ref, bf16[3,1184,1024]{2,1,0:T(8,128)(2,1)} %get-tuple-element.91.q_ref.k_ref.v_ref, bf16[1184,1024]{1,0:T(8,128)(2,1)} %get-tuple-element.92.g_ref), custom_call_target="tpu_custom_call" | custom-call | flops 14355005440 | bytes 8486912 | tf_op jit(solution)/shard_map/unattend_1/pallas_call | solution.py:495
  327.7 2.2 reduce-scatter.10.cloned.1.call-done
  329.9 10.2 %inner_mlp.1 = (f32[1,2,2,512,1024]{4,3,2,1,0:T(8,128)}, bf16[2,512,1024]{2,1,0:T(8,128)(2,1)}) custom-call(bf16[2,512,256]{2,1,0:T(8,128)(2,1)} %bitcast.40, bf16[2,512,256]{2,1,0:T(8,128)(2,1)} %bitcast.41, bf16[2,512,512]{2,1,0:T(8,128)(2,1)} %bitcast.36, f32[2,512,1024]{2,1,0:T(8,128)} %refs_4_.3, f32[1,2,2,512,1024]{4,3,2,1,0:T(8,128)} %refs_4_.2), custom_call_target="tpu_custom_call" | custom-call | flops 31457280 | bytes 25165824 | tf_op jit(solution)/shard_map/inner_mlp/pallas_call | solution.py:1116
  340.1 33.2 %close_1.1 = (f32[1184,1024]{1,0:T(8,128)}, bf16[256,1024]{1,0:T(8,128)(2,1)}, bf16[4,3,512,128]{3,2,1,0:T(8,128)(2,1)}, f32[2,512]{1,0:T(2,128)}) custom-call(bf16[1184,1024]{1,0:T(8,128)(2,1)} %get-tuple-element.90.n_ref, bf16[3,1184,512]{2,1,0:T(8,128)(2,1)} %unattend_1.1.grad_ref, bf16[4,4,1024,256]{3,2,1,0:T(8,128)(2,1)} %get-tuple-element.88.w_ref, ...), custom_call_target="tpu_custom_call" | custom-call | flops 7449083904 | bytes 24248320 | tf_op jit(solution)/shard_map/close_1/pallas_call | solution.py:652
  373.4 2.3 collective-permute-start.2
  378.5 3.8 copy.30
  382.5 9.8 %finish.1 = (f32[2,577,1,1024]{3,2,1,0:T(1,128)}, f32[2,1024]{1,0:T(2,128)}) custom-call(f32[1184,1024]{1,0:T(8,128)} %get-tuple-element.107.acc_ref, f32[1184,1024]{1,0:T(8,128)} %get-tuple-element.108.gr_ref, bf16[1184,1024]{1,0:T(8,128)(2,1)} %get-tuple-element.109.x_ref, f32[12,1024]{1,0:T(8,128)} %refs_1_.6), custom_call_target="tpu_custom_call" | custom-call | flops 24248320 | bytes 16973824 | tf_op jit(solution)/shard_map/finish/pallas_call | solution.py:687
  392.3 2.0 concatenate.11.refs_0_
  394.3 6.3 %inner_early.1 = (f32[1,2,4,512,256]{4,3,2,1,0:T(8,128)}, bf16[5,512,128]{2,1,0:T(8,128)(2,1)}) custom-call(bf16[5,512,128]{2,1,0:T(8,128)(2,1)} %bitcast.39, f32[4,512,256]{2,1,0:T(8,128)} %refs_1_.9, f32[1,2,4,512,256]{4,3,2,1,0:T(8,128)} %refs_2_.6), custom_call_target="tpu_custom_call" | custom-call | flops 9830400 | bytes 7864320 | tf_op jit(solution)/shard_map/inner_early/pallas_call | solution.py:1116
  400.6 24.7 %group_early.1 = (bf16[2560,128]{1,0:T(8,128)(2,1)}, f32[2,12,1024]{2,1,0:T(8,128)}, f32[3,12,1024]{2,1,0:T(8,128)}, bf16[12,1024]{1,0:T(8,128)(2,1)}) custom-call(bf16[2560,128]{1,0:T(8,128)(2,1)} %bitcast.38, f32[12,1024]{1,0:T(8,128)} %concatenate.11.refs_0_, f32[12,1024]{1,0:T(8,128)} %refs_1_.6, f32[2,12,1024]{2,1,0:T(8,128)} %bitcast.42, ...), custom_call_target="tpu_custom_call" | custom-call | flops 1310720 | bytes 2621440 | tf_op jit(solution)/shard_map/group_early/pallas_call | solution.py:1335
  425.3 1.6 copy.32
  426.9 5.6 %outer_early.1 = (f32[3,4,512,256]{3,2,1,0:T(8,128)}, bf16[4,512,256]{2,1,0:T(8,128)(2,1)}) custom-call(s32[1]{0:T(128)} %bitcast.16.g_ref, bf16[5,512,128]{2,1,0:T(8,128)(2,1)} %bitcast.37, f32[4,512,256]{2,1,0:T(8,128)} %refs_1_.9, f32[4,512,256]{2,1,0:T(8,128)} %refs_2_.7), custom_call_target="tpu_custom_call" | custom-call | flops 3276800 | bytes 7864320 | tf_op jit(solution)/shard_map/outer_early/pallas_call | solution.py:1164
  433.5 10.4 %outer_mlp.1 = (f32[3,2,512,1024]{3,2,1,0:T(8,128)}, bf16[2,512,1024]{2,1,0:T(8,128)(2,1)}) custom-call(s32[1]{0:T(128)} %bitcast.16.g_ref, bf16[256,1024]{1,0:T(8,128)(2,1)} %get-tuple-element.124.refs_0_, bf16[256,1024]{1,0:T(8,128)(2,1)} %collective-permute-done.refs_1_, bf16[256,1024]{1,0:T(8,128)(2,1)} %copy-done.2, bf16[256,1024]{1,0:T(8,128)(2,1)} %copy-done.1, ...), custom_call_target="tpu_custom_call" | custom-call | flops 10485760 | bytes 25165824 | tf_op jit(solution)/shard_map/outer_mlp/pallas_call | solution.py:1164
  443.9 4.3 inner_late.1
  448.2 15.0 %group_late.1 = bf16[1536,128]{1,0:T(8,128)(2,1)} custom-call(bf16[1536,128]{1,0:T(8,128)(2,1)} %bitcast.43), custom_call_target="tpu_custom_call" | custom-call | flops 786432 | bytes 1572864 | tf_op jit(solution)/shard_map/group_late/pallas_call | solution.py:1335
  463.3 3.9 outer_late.1
  (55 shorter events, 6.9 us)
Async XLA Ops:
  7.2 274.7 %reduce-scatter.6.cloned.1.call-start = ((), (), s32[]{:S(2)}) async-start(), calls=%async_computation.5 | async-start | bytes 2621440 | tf_op jit(solution)/shard_map/reduce_scatter | solution.py:1376
  160.8 166.9 %reduce-scatter.8.cloned.1.call-start = ((), (), s32[]{:S(2)}) async-start(), calls=%async_computation.6 | async-start | bytes 2621440 | tf_op jit(solution)/shard_map/reduce_scatter | solution.py:1376
  186.8 143.0 %reduce-scatter.10.cloned.1.call-start = ((), (), s32[]{:S(2)}) async-start(), calls=%async_computation.7 | async-start | bytes 5242880 | tf_op jit(solution)/shard_map/reduce_scatter | solution.py:1376
  231.4 162.9 %reduce-scatter.14.cloned.1.call-start = ((), (), s32[]{:S(2)}) async-start(), calls=%async_computation.9 | async-start | bytes 3276800 | tf_op jit(solution)/shard_map/reduce_scatter | solution.py:1376
  299.0 144.9 %reduce-scatter.12.cloned.1.call-start = ((), (), s32[]{:S(2)}) async-start(), calls=%async_computation.8 | async-start | bytes 1966080 | tf_op jit(solution)/shard_map/reduce_scatter | solution.py:1376
  340.1 37.0 %copy-start.4 = (f32[1,2,12,1024]{3,1,2,0:T(2,128)S(1)}, f32[1,2,12,1024]{3,1,2,0:T(2,128)}, u32[]{:S(2)}) copy-start(f32[1,2,12,1024]{3,1,2,0:T(2,128)} %param.20) | copy-start | bytes 294916
  340.1 38.4 %copy-start = (bf16[2,577,1024]{2,1,0:T(8,128)(2,1)S(1)}, bf16[2,577,1024]{2,1,0:T(8,128)(2,1)}, u32[]{:S(2)}) copy-start(bf16[2,577,1024]{2,1,0:T(8,128)(2,1)} %get-tuple-element.89) | copy-start | bytes 7090180
  373.3 9.0 %copy-start.6 = (f32[4,1024]{1,0:T(4,128)S(1)}, f32[4,1024]{1,0:T(4,128)}, u32[]{:S(2)}) copy-start(f32[4,1024]{1,0:T(4,128)} %get-tuple-element.115) | copy-start | bytes 49156
  373.4 59.1 %collective-permute-start.2 = (bf16[256,1024]{1,0:T(8,128)(2,1)}, bf16[256,1024]{1,0:T(8,128)(2,1)S(1)}, u32[]{:S(2)}, u32[]{:S(2)}) collective-permute-start(bf16[256,1024]{1,0:T(8,128)(2,1)} %get-tuple-element.124.refs_0_), channel_id=1, source_target_pairs={{0,24},{8,0},{16,8},{24,16},{1,25},{9,1},{17,9},{25,17},{2,26},{10... | collective-permute-start | bytes 1572872 | tf_op jit(solution)/shard_map/ppermute | solution.py:1359
  375.6 56.8 %collective-permute-start.1 = (bf16[256,1024]{1,0:T(8,128)(2,1)}, bf16[256,1024]{1,0:T(8,128)(2,1)S(1)}, u32[]{:S(2)}, u32[]{:S(2)}) collective-permute-start(bf16[256,1024]{1,0:T(8,128)(2,1)} %get-tuple-element.124.refs_0_), channel_id=1, source_target_pairs={{0,16},{8,24},{16,0},{24,8},{1,17},{9,25},{17,1},{25,9},{2,18},{10... | collective-permute-start | bytes 1572872 | tf_op jit(solution)/shard_map/ppermute | solution.py:1359
  376.2 56.3 %collective-permute-start = (bf16[256,1024]{1,0:T(8,128)(2,1)}, bf16[256,1024]{1,0:T(8,128)(2,1)}, u32[]{:S(2)}, u32[]{:S(2)}) collective-permute-start(bf16[256,1024]{1,0:T(8,128)(2,1)} %get-tuple-element.124.refs_0_), channel_id=1, source_target_pairs={{0,8},{8,16},{16,24},{24,0},{1,9},{9,17},{17,25},{25,1},{2,10},{10... | collective-permute-start | bytes 1572872 | tf_op jit(solution)/shard_map/ppermute | solution.py:1359
  377.1 5.2 %copy-start.8 = (f32[4,1,256]{2,1,0:T(1,128)S(1)}, f32[4,1,256]{2,1,0:T(1,128)}, u32[]{:S(2)}) copy-start(f32[4,1,256]{2,1,0:T(1,128)} %get-tuple-element.119) | copy-start | bytes 12292
  377.1 5.2 %copy-start.7 = (f32[4,1,512]{2,1,0:T(1,128)S(1)}, f32[4,1,512]{2,1,0:T(1,128)}, u32[]{:S(2)}) copy-start(f32[4,1,512]{2,1,0:T(1,128)} %get-tuple-element.120) | copy-start | bytes 24580
  377.8 4.6 copy-start.9
  377.8 4.6 copy-start.10
  432.5 0.8 copy-start.1
  432.5 1.0 copy-start.2
  463.2 3.9 copy-start.3
  463.3 4.6 copy-start.5
Sparse Core Ops, SparseCore 0:
  160.9 44.8 reduce-scatter.5
  208.2 43.1 reduce-scatter.7
  253.7 76.0 reduce-scatter.9
  332.1 52.6 reduce-scatter.13
  387.1 37.0 reduce-scatter.11

commit v3 on v2

--- a/solution.py
+++ b/solution.py
@@ -506,56 +506,17 @@
     )(qkv, qkv, qkv, grad_attended)
 
 
-def close_kernel(pairwise, groups, first, final, n_ref, grad_ref, w_ref, *refs):
+def close_kernel(pairwise, first, n_ref, grad_ref, w_ref, *refs):
     if not first:
         carry_ref, *refs = refs
     elif pairwise:
         more_ref, *refs = refs
-    if pairwise and final:
-        diff_ref, acc_ref, total_ref, *refs = refs
-    else:
-        acc_ref, *refs = refs
-    dw_ref, sums_ref, acc_scr, *exchange = refs
+    acc_ref, dw_ref, sums_ref, acc_scr, *exchange = refs
     j = pl.program_id(0)
     shards, _, _, cols = w_ref.shape
     if pairwise:
-        own, sent, received, sends, receives, *exchange = exchange
-        if not final:
-            pl.when(j == 0)(greet_partner)
-    if pairwise and final:
-        mine, landed, sends_two, receives_two, loaded = exchange
-        g, f, t = lax.axis_index("group"), lax.axis_index("fsdp"), lax.axis_index("tensor")
-        quarter = landed.shape[1]
-
-        def rows(n):
-            return pl.ds(pl.multiple_of(n * quarter, quarter), quarter)
-
-        def other(k):
-            return (lax.rem(g + k, groups), f, t)
-
-        def part(k):
-            return pltpu.make_async_remote_copy(
-                src_ref=diff_ref.at[rows(lax.rem(g + k, groups)), :],
-                dst_ref=landed.at[k],
-                send_sem=sends_two.at[k],
-                recv_sem=receives_two.at[k],
-                device_id=other(k),
-                device_id_type=MESH,
-            )
-
-        keep = pltpu.make_async_copy(diff_ref.at[rows(g), :], mine, loaded.at[0])
-
-        @pl.when(j == 0)
-        def _():
-            barrier = pltpu.get_barrier_semaphore()
-            pl.semaphore_signal(barrier, inc=1, device_id=partner(), device_id_type=MESH)
-            for k in range(1, groups):
-                pl.semaphore_signal(barrier, inc=1, device_id=other(k), device_id_type=MESH)
-            pl.semaphore_wait(barrier, groups)
-            for k in range(1, groups):
-                part(k).start()
-            keep.start()
-
+        own, sent, received, sends, receives = exchange
+        pl.when(j == 0)(greet_partner)
     @pl.when(j == 0)
     def _():
         acc_scr[...] = jnp.zeros_like(acc_scr) if first else carry_ref[...]
@@ -599,22 +560,15 @@
                     for n in range(dw_ref.shape[1] - 3):
                         dw_ref[t, 3 + n] = more_ref[t, 0, :, n * cols : (n + 1) * cols]
         acc_ref[...] = acc_scr[...]
-        if pairwise and final:
-            keep.wait()
-            total = mine[...].astype(F32)
-            for k in range(1, groups):
-                part(k).wait()
-                total = total + landed[k].astype(F32)
-            total_ref[...] = total.astype(LOW)
-
-
-def close(part, parts, normed, grads, w_attn, carry, more, ending, fsdp, groups):
+
+
+def close(part, parts, normed, grads, w_attn, carry, more, fsdp):
     rows, width = normed.shape
     shards, _, _, cols = w_attn.shape
     cols = cols // parts
     lanes = shards * cols
     depth = width // fsdp
-    pairwise, first, final = fsdp == 2, carry is None, ending is not None
+    pairwise, first = fsdp == 2, carry is None
     single = pl.Buffered(1)
     stack = pl.BlockSpec((1, rows, lanes), lambda j: (j, 0, 0))
     full = pl.BlockSpec((rows, width), lambda j: (0, 0), pipeline_mode=single)
@@ -635,22 +589,8 @@
         in_specs.append(pl.BlockSpec(more.shape, lambda j: (0, 0, 0, 0), pipeline_mode=single))
     out_specs.append(full)
     out_shape.append(jax.ShapeDtypeStruct((rows, width), F32))
-    if pairwise and final:
-        quarter, lanes_two = ending.shape[0] // groups, ending.shape[1]
-        in_specs.append(pl.BlockSpec(memory_space=pl.ANY))
-        out_specs.append(pl.BlockSpec((quarter, lanes_two), lambda j: (0, 0), pipeline_mode=single))
-        out_shape.append(jax.ShapeDtypeStruct((quarter, lanes_two), LOW))
-        dma = pltpu.SemaphoreType.DMA
-        extra = [
-            *extra,
-            pltpu.VMEM((quarter, lanes_two), LOW),
-            pltpu.VMEM((groups, quarter, lanes_two), LOW),
-            dma((groups,)),
-            dma((groups,)),
-            dma((1,)),
-        ]
     return pl.pallas_call(
-        functools.partial(close_kernel, pairwise, groups, first, final),
+        functools.partial(close_kernel, pairwise, first),
         grid=(3,),
         in_specs=in_specs,
         out_specs=[*out_specs, dw_spec, pl.BlockSpec((2, lanes), lambda j: (0, 0))],
@@ -659,7 +599,7 @@
         compiler_params=params(7 + part if pairwise else None),
         cost_estimate=cost(12 * rows * width * lanes, 20 * rows * width),
         name=f"close_{part}",
-    )(normed, grads, w_attn, *([carry] if not first else [more] if pairwise else []), *([ending] if pairwise and final else []))
+    )(normed, grads, w_attn, *([carry] if not first else [more] if pairwise else []))
 
 
 def finish_kernel(acc_ref, gr_ref, x_ref, vec_ref, out_ref, norm_ref):
@@ -913,8 +853,6 @@
     m_hold[...] = m_wide[...].astype(LOW)
     keeps[1].start()
     maps(z)
-    for i in range(images):
-        g2_scr[pl.ds(i * span, seq), :] = (g_ref[:, i, :].astype(F32) * alive_ref[i]).astype(LOW)
     both(land, 0, 2)
     both(relay, 0, 1)
     keeps[1].wait()
@@ -969,6 +907,8 @@
     at = 1 + min(segments, total - 3)
     puts.append(pltpu.make_async_copy(att_scr, att_out, ws.at[3]))
     puts[-1].start()
+    for i in range(images):
+        g2_scr[pl.ds(i * span, seq), :] = (g_ref[:, i, :].astype(F32) * alive_ref[i]).astype(LOW)
     while at < total - 2:
         advance(at)
         at += 1
@@ -1363,11 +1303,11 @@
     g = lax.axis_index("group")
     quarters = diff.reshape(groups, -1, diff.shape[-1])
     parts = [lax.dynamic_index_in_dim(quarters, lax.rem(g + k, groups), 0, keepdims=False) for k in range(groups)]
-    total = sum([around(parts[k], k, groups).astype(F32) for k in range(1, groups)], parts[0].astype(F32))
-    return total.astype(LOW)
-
-
-def exchange_total(own, groups):
+    return parts[0], [around(parts[k], k, groups) for k in range(1, groups)]
+
+
+def exchange_total(own, parts, groups):
+    own = sum([part.astype(F32) for part in parts], own.astype(F32)).astype(LOW)
     return [own] + [around(own, k, groups) for k in range(1, groups)]
 
 
@@ -1436,7 +1376,7 @@
     grads = unattend(qkv, grad_attended, images, seq, 0, PARTS, tensor_size)
     grads, mlp_grads[0] = lax.optimization_barrier((grads, mlp_grads[0]))
     carry, dw_early, head_sums = close(
-        0, PARTS, normed_one, grads, w_attn, None, dw_out, None, fsdp, groups
+        0, PARTS, normed_one, grads, w_attn, None, dw_out, fsdp
     )
     if not pairwise:
         halves = jnp.moveaxis(dw_out.reshape(*dw_out.shape[:-1], PARTS, half), -2, 2)
@@ -1446,19 +1386,15 @@
     carry, mlp_grads[1] = lax.optimization_barrier((carry, mlp_grads[1]))
     grads = unattend(qkv, grad_attended, images, seq, 1, PARTS, tensor_size)
 
-    mlp_grads[0], grads = lax.optimization_barrier((mlp_grads[0], grads))
+    carry, dw_late, sums = close(1, PARTS, normed_one, grads, w_attn, carry, None, fsdp)
+
+    mlp_grads[0], carry = lax.optimization_barrier((mlp_grads[0], carry))
     mlp_inner, mlp_diff = inner_step(
         beside, mlp_grads, lambda u: (u, 0), 2, mlp_master.shape[2], mlp_master, mlp_moments, None, "inner_mlp"
     )
-    carry, mlp_diff = lax.optimization_barrier((carry, mlp_diff))
-    ending = mlp_diff.reshape(-1, mlp_diff.shape[-1])
-    carry, *mlp_own, dw_late, sums = close(
-        1, PARTS, normed_one, grads, w_attn, carry, None, ending, fsdp, groups
-    )
+    own, parts = exchange_parts(mlp_diff, groups)
+    carry, own = lax.optimization_barrier((carry, own))
     patches_grad, sums_one = finish(carry, grad_resid, x_rows, vec, images, seq)
-    if not pairwise:
-        mlp_own = [exchange_parts(mlp_diff, groups)]
-    mlp_total = exchange_total(mlp_own[0], groups)
     late_grad = scatter_gradient(dw_late)
     head_sums.append(sums)
 
@@ -1471,13 +1407,16 @@
     def first(piece):
         return piece
 
+    head_rows = jnp.concatenate([v.reshape(2, tensor_size, -1) for v in head_sums], axis=-1).reshape(2, width)
+    hidden_bias = jnp.concatenate(bias_parts, axis=-1).reshape(-1, width)
+    vector_part = jnp.concatenate([sums_one, sums_two[:2], head_rows, sums_two[2:], hidden_bias])
+    early_grad, vector_part = lax.optimization_barrier((early_grad, vector_part))
     attn_inner, early_diff = inner_step(
         first, [early_grad], early, 3 + PARTS, half, attn_master, attn_moments, None, "inner_early"
     )
-    head_rows = jnp.concatenate([v.reshape(2, tensor_size, -1) for v in head_sums], axis=-1).reshape(2, width)
-    hidden_bias = jnp.concatenate(bias_parts, axis=-1).reshape(-1, width)
-    vector_part = jnp.concatenate([sums_one, sums_two[:2], head_rows, sums_two[2:], hidden_bias])
-
+
+    own, *parts, early_diff = lax.optimization_barrier((own, *parts, early_diff))
+    mlp_total = exchange_total(own, parts, groups)
     if pairwise:
         early_total, vector_inner, vector_state, vector_copy = group_sum(
             early_diff,

time: 484 us -> 499 us (1.031)
  waiting for transfers between devices: 2.28 us -> 14.1 us
  Pallas kernels: 441 us -> 436 us
    pallas_call x2, Pallas kernels: 50.3 us -> 35 us  [close(): pl.pallas_call(functools.partial(close_kernel, pairwise, first), grid=(3,...]
    pallas_call x2, Pallas kernels: 39.7 us -> 51.8 us  [group_sum(): pl.pallas_call(functools.partial(group_kernel, groups, shards, bool(vecto...]
    reduce_scatter x5, waiting for transfers between devices: 2.19 us -> 14 us  [scatter_gradient(): return lax.psum_scatter(half, 'tensor', scatter_dimension=0)]
  transfers between devices with their start and end apart: 8 -> 11, of which waited for: 1 -> 1; matrix products, arithmetic and copies ran while one was open for 2% -> 3% of each run, Pallas kernels for 56% -> 54%
where the time goes in v3:
time: 499 us; the launch traced here: 490 us
  Pallas kernels  436 us (87%)
  local copies, waits for them, and re-layouts  14.6 us (3%)
  between operations  14.6 us (3%)
  waiting for transfers between devices  14.1 us (3%)
  starting transfers between devices  7.27 us (1%)
    pallas_call x1, Pallas kernels, front(): pl.pallas_call(functools.partial(front_kernel, images, seq), in_specs=[pl...  124 us
    pallas_call x3, Pallas kernels, mlp(): pl.pallas_call(functools.partial(mlp_kernel, first, pairwise), grid=(step...  96 us
    pallas_call x2, Pallas kernels, unattend(): pl.pallas_call(functools.partial(unattend_kernel, seq), grid=(images, wid...  57 us
    pallas_call x2, Pallas kernels, group_sum(): pl.pallas_call(functools.partial(group_kernel, groups, shards, bool(vecto...  51.8 us
    pallas_call x2, Pallas kernels, close(): pl.pallas_call(functools.partial(close_kernel, pairwise, first), grid=(3,...  35 us
    pallas_call x1, Pallas kernels, turn(): pl.pallas_call(functools.partial(turn_kernel, seq, pairwise), grid=(image...  21.7 us
    pallas_call x3, Pallas kernels, inner_step(): pl.pallas_call(functools.partial(inner_kernel, join, count), grid=(units,...  21.1 us
    pallas_call x3, Pallas kernels, outer_step(): pl.pallas_call(functools.partial(outer_kernel, groups, slots, each), grid...  19.8 us
  transfers between devices with their start and end apart: 11, of which 1 were waited for; matrix products, arithmetic and copies ran while one was open for 3% of the time, Pallas kernels for 54%

profile of v3, /device:TPU:0, one launch (start us, length us, event | category | flops | bytes accessed | tf_op | source)
XLA Modules:
  0.0 489.8 jit_solution(4687730089527660367)
XLA Ops:
  10.0 123.8 %front.1 = (bf16[4,4,1024,256]{3,2,1,0:T(8,128)(2,1)}, bf16[4,2,1024,1024]{3,2,1,0:T(8,128)(2,1)}, bf16[1184,1024]{1,0:T(8,128)(2,1)}, bf16[3,1184,1024]{2,1,0:T...) custom-call(f32[2]{0:T(128)} %fusion.1.alive_ref, ...), custom_call_target="tpu_custom_call" | custom-call | flops 9932111872 | bytes 36372480 | tf_op jit(solution)/shard_map/front/pallas_call | solution.py:986
  133.8 25.4 %mlp_0.1 = (f32[1184,1024]{1,0:T(8,128)}, f32[1184,1024]{1,0:T(8,128)}, bf16[4,2,512,256]{3,2,1,0:T(8,128)(2,1)}, f32[4,1,256]{2,1,0:T(1,128)}) custom-call(bf16[1184,1024]{1,0:T(8,128)(2,1)} %get-tuple-element.84.n_ref, bf16[1184,1024]{1,0:T(8,128)(2,1)} %get-tuple-element.85.g_ref.g2_ref, bf16[4,2,1024,1024]{3,2,1,0:T(8,128)(2,1)} %get-tuple-element.86.w1_ref.w2_ref, ...), custom_call_target="tpu_custom_call" | custom-call | flops 14898167808 | bytes 29097984 | tf_op jit(solution)/shard_map/mlp_0/pallas_call | solution.py:334
  159.3 25.9 %mlp_1.1 = (f32[1184,1024]{1,0:T(8,128)}, f32[1184,1024]{1,0:T(8,128)}, bf16[4,2,512,256]{3,2,1,0:T(8,128)(2,1)}, f32[4,1,256]{2,1,0:T(1,128)}) custom-call(bf16[1184,1024]{1,0:T(8,128)(2,1)} %get-tuple-element.84.n_ref, bf16[1184,1024]{1,0:T(8,128)(2,1)} %get-tuple-element.85.g_ref.g2_ref, bf16[4,2,1024,1024]{3,2,1,0:T(8,128)(2,1)} %get-tuple-element.86.w1_ref.w2_ref, ...), custom_call_target="tpu_custom_call" | custom-call | flops 14898167808 | bytes 29097984 | tf_op jit(solution)/shard_map/mlp_1/pallas_call | solution.py:334
  185.3 44.7 %mlp_2.1 = (f32[1184,1024]{1,0:T(8,128)}, f32[1184,1024]{1,0:T(8,128)}, bf16[4,2,512,512]{3,2,1,0:T(8,128)(2,1)}, f32[4,1,512]{2,1,0:T(1,128)}) custom-call(bf16[1184,1024]{1,0:T(8,128)(2,1)} %get-tuple-element.84.n_ref, bf16[1184,1024]{1,0:T(8,128)(2,1)} %get-tuple-element.85.g_ref.g2_ref, bf16[4,2,1024,1024]{3,2,1,0:T(8,128)(2,1)} %get-tuple-element.86.w1_ref.w2_ref, ...), custom_call_target="tpu_custom_call" | custom-call | flops 29796335616 | bytes 29097984 | tf_op jit(solution)/shard_map/mlp_2/pallas_call | solution.py:334
  230.1 21.7 %turn.1 = (bf16[2,577,1024]{2,1,0:T(8,128)(2,1)}, f32[1184,1024]{1,0:T(8,128)}, bf16[1184,1024]{1,0:T(8,128)(2,1)}, bf16[4,1,512,256]{3,2,1,0:T(8,128)(2,1)}, f32[4,1024]{1,0:T(4,128)}) custom-call(f32[2]{0:T(128)} %fusion.1.alive_ref, f32[1184,1024]{1,0:T(8,128)} %get-tuple-element.83.resid_ref, f32[1184,1024]{1,0:T(8,128)} %get-tuple-element.91.y_ref, ...), custom_call_target="tpu_custom_call" | custom-call | flops 4966055936 | bytes 29097984 | tf_op jit(solution)/shard_map/turn/pallas_call | solution.py:428
  251.8 28.4 %unattend_0.1.grad_ref = bf16[3,1184,512]{2,1,0:T(8,128)(2,1)} custom-call(bf16[3,1184,1024]{2,1,0:T(8,128)(2,1)} %get-tuple-element.96.q_ref.k_ref.v_ref, bf16[3,1184,1024]{2,1,0:T(8,128)(2,1)} %get-tuple-element.96.q_ref.k_ref.v_ref, bf16[3,1184,1024]{2,1,0:T(8,128)(2,1)} %get-tuple-element.96.q_ref.k_ref.v_ref, bf16[1184,1024]{1,0:T(8,128)(2,1)} %get-tuple-element.97.g_ref), custom_call_target="tpu_custom_call" | custom-call | flops 14355005440 | bytes 8486912 | tf_op jit(solution)/shard_map/unattend_0/pallas_call | solution.py:495
  280.2 17.4 %close_0.1 = (f32[1184,1024]{1,0:T(8,128)}, bf16[4,5,512,128]{3,2,1,0:T(8,128)(2,1)}, f32[2,512]{1,0:T(2,128)}) custom-call(bf16[1184,1024]{1,0:T(8,128)(2,1)} %get-tuple-element.100.n_ref, bf16[3,1184,512]{2,1,0:T(8,128)(2,1)} %unattend_0.1.grad_ref, bf16[4,4,1024,256]{3,2,1,0:T(8,128)(2,1)} %get-tuple-element.94.w_ref, ...), custom_call_target="tpu_custom_call" | custom-call | flops 7449083904 | bytes 24248320 | tf_op jit(solution)/shard_map/close_0/pallas_call | solution.py:592
  297.6 28.6 %unattend_1.1.grad_ref = bf16[3,1184,512]{2,1,0:T(8,128)(2,1)} custom-call(bf16[3,1184,1024]{2,1,0:T(8,128)(2,1)} %get-tuple-element.96.q_ref.k_ref.v_ref, bf16[3,1184,1024]{2,1,0:T(8,128)(2,1)} %get-tuple-element.96.q_ref.k_ref.v_ref, bf16[3,1184,1024]{2,1,0:T(8,128)(2,1)} %get-tuple-element.96.q_ref.k_ref.v_ref, bf16[1184,1024]{1,0:T(8,128)(2,1)} %get-tuple-element.97.g_ref), custom_call_target="tpu_custom_call" | custom-call | flops 14355005440 | bytes 8486912 | tf_op jit(solution)/shard_map/unattend_1/pallas_call | solution.py:495
  326.3 17.7 %close_1.1 = (f32[1184,1024]{1,0:T(8,128)}, bf16[4,3,512,128]{3,2,1,0:T(8,128)(2,1)}, f32[2,512]{1,0:T(2,128)}) custom-call(bf16[1184,1024]{1,0:T(8,128)(2,1)} %get-tuple-element.100.n_ref, bf16[3,1184,512]{2,1,0:T(8,128)(2,1)} %unattend_1.1.grad_ref, bf16[4,4,1024,256]{3,2,1,0:T(8,128)(2,1)} %get-tuple-element.94.w_ref, f32[1184,1024]{1,0:T(8,128)} %get-tuple-element.105.refs_0_), custom_call_target="tpu_custom_call" | custom-call | flops 7449083904 | bytes 24248320 | tf_op jit(solution)/shard_map/close_1/pallas_call | solution.py:592
  344.0 10.3 %inner_mlp.1 = (f32[1,2,2,512,1024]{4,3,2,1,0:T(8,128)}, bf16[2,512,1024]{2,1,0:T(8,128)(2,1)}) custom-call(bf16[2,512,256]{2,1,0:T(8,128)(2,1)} %bitcast.49, bf16[2,512,256]{2,1,0:T(8,128)(2,1)} %bitcast.50, bf16[2,512,512]{2,1,0:T(8,128)(2,1)} %bitcast.45, f32[2,512,1024]{2,1,0:T(8,128)} %refs_4_.3, f32[1,2,2,512,1024]{4,3,2,1,0:T(8,128)} %refs_4_.2), custom_call_target="tpu_custom_call" | custom-call | flops 31457280 | bytes 25165824 | tf_op jit(solution)/shard_map/inner_mlp/pallas_call | solution.py:1056
  354.3 2.7 dynamic-slice_bitcast_fusion
  360.7 10.1 %finish.1 = (f32[2,577,1,1024]{3,2,1,0:T(1,128)}, f32[2,1024]{1,0:T(2,128)}) custom-call(f32[1184,1024]{1,0:T(8,128)} %get-tuple-element.112.acc_ref, f32[1184,1024]{1,0:T(8,128)} %get-tuple-element.113.gr_ref, bf16[1184,1024]{1,0:T(8,128)(2,1)} %get-tuple-element.114.x_ref, f32[12,1024]{1,0:T(8,128)} %refs_1_.6), custom_call_target="tpu_custom_call" | custom-call | flops 24248320 | bytes 16973824 | tf_op jit(solution)/shard_map/finish/pallas_call | solution.py:627
  370.8 2.0 concatenate.11.refs_0_
  372.8 14.0 %reduce-scatter.14.cloned.1.call-done = bf16[1,5,512,128]{3,2,1,0:T(8,128)(2,1)} async-done(((bf16[4,5,512,128]{3,2,1,0:T(8,128)(2,1)}), bf16[1,5,512,128]{3,2,1,0:T(8,128)(2,1)}) %reduce-scatter.14.cloned.1.call-update) | async-done | bytes 655376 | tf_op jit(solution)/shard_map/reduce_scatter | solution.py:1316
  386.8 6.5 %inner_early.1 = (f32[1,2,4,512,256]{4,3,2,1,0:T(8,128)}, bf16[5,512,128]{2,1,0:T(8,128)(2,1)}) custom-call(bf16[5,512,128]{2,1,0:T(8,128)(2,1)} %bitcast.48, f32[4,512,256]{2,1,0:T(8,128)} %refs_1_.9, f32[1,2,4,512,256]{4,3,2,1,0:T(8,128)} %refs_2_.6), custom_call_target="tpu_custom_call" | custom-call | flops 9830400 | bytes 7864320 | tf_op jit(solution)/shard_map/inner_early/pallas_call | solution.py:1056
  394.8 2.4 collective-permute-start.5
  399.1 3.8 copy.30
  402.9 35.6 %group_early.1 = (bf16[2560,128]{1,0:T(8,128)(2,1)}, f32[2,12,1024]{2,1,0:T(8,128)}, f32[3,12,1024]{2,1,0:T(8,128)}, bf16[12,1024]{1,0:T(8,128)(2,1)}) custom-call(bf16[2560,128]{1,0:T(8,128)(2,1)} %bitcast.47, f32[12,1024]{1,0:T(8,128)} %concatenate.11.refs_0_, f32[12,1024]{1,0:T(8,128)} %refs_1_.6, f32[2,12,1024]{2,1,0:T(8,128)} %bitcast.51, ...), custom_call_target="tpu_custom_call" | custom-call | flops 1310720 | bytes 2621440 | tf_op jit(solution)/shard_map/group_early/pallas_call | solution.py:1275
  438.5 1.6 copy.32
  440.1 5.6 %outer_early.1 = (f32[3,4,512,256]{3,2,1,0:T(8,128)}, bf16[4,512,256]{2,1,0:T(8,128)(2,1)}) custom-call(s32[1]{0:T(128)} %bitcast.17.g_ref, bf16[5,512,128]{2,1,0:T(8,128)(2,1)} %bitcast.46, f32[4,512,256]{2,1,0:T(8,128)} %refs_1_.9, f32[4,512,256]{2,1,0:T(8,128)} %refs_2_.7), custom_call_target="tpu_custom_call" | custom-call | flops 3276800 | bytes 7864320 | tf_op jit(solution)/shard_map/outer_early/pallas_call | solution.py:1104
  446.7 10.4 %outer_mlp.1 = (f32[3,2,512,1024]{3,2,1,0:T(8,128)}, bf16[2,512,1024]{2,1,0:T(8,128)(2,1)}) custom-call(s32[1]{0:T(128)} %bitcast.17.g_ref, bf16[256,1024]{1,0:T(8,128)(2,1)} %copy-done.1, bf16[256,1024]{1,0:T(8,128)(2,1)} %collective-permute-done.3.refs_1_, bf16[256,1024]{1,0:T(8,128)(2,1)} %copy-done.3, bf16[256,1024]{1,0:T(8,128)(2,1)} %copy-done.2, ...), custom_call_target="tpu_custom_call" | custom-call | flops 10485760 | bytes 25165824 | tf_op jit(solution)/shard_map/outer_mlp/pallas_call | solution.py:1104
  457.1 4.3 inner_late.1
  461.4 16.2 %group_late.1 = bf16[1536,128]{1,0:T(8,128)(2,1)} custom-call(bf16[1536,128]{1,0:T(8,128)(2,1)} %bitcast.52), custom_call_target="tpu_custom_call" | custom-call | flops 786432 | bytes 1572864 | tf_op jit(solution)/shard_map/group_late/pallas_call | solution.py:1275
  477.6 3.9 outer_late.1
  (67 shorter events, 12.3 us)
Async XLA Ops:
  7.2 273.0 %reduce-scatter.6.cloned.1.call-start = ((), (), s32[]{:S(2)}) async-start(), calls=%async_computation.5 | async-start | bytes 2621440 | tf_op jit(solution)/shard_map/reduce_scatter | solution.py:1316
  159.3 167.0 %reduce-scatter.8.cloned.1.call-start = ((), (), s32[]{:S(2)}) async-start(), calls=%async_computation.6 | async-start | bytes 2621440 | tf_op jit(solution)/shard_map/reduce_scatter | solution.py:1316
  185.3 158.7 %reduce-scatter.10.cloned.1.call-start = ((), (), s32[]{:S(2)}) async-start(), calls=%async_computation.7 | async-start | bytes 5242880 | tf_op jit(solution)/shard_map/reduce_scatter | solution.py:1316
  230.0 156.7 %reduce-scatter.14.cloned.1.call-start = ((), (), s32[]{:S(2)}) async-start(), calls=%async_computation.9 | async-start | bytes 3276800 | tf_op jit(solution)/shard_map/reduce_scatter | solution.py:1316
  297.6 159.5 %reduce-scatter.12.cloned.1.call-start = ((), (), s32[]{:S(2)}) async-start(), calls=%async_computation.8 | async-start | bytes 1966080 | tf_op jit(solution)/shard_map/reduce_scatter | solution.py:1316
  354.3 6.3 %copy-start.9 = (f32[4,1,256]{2,1,0:T(1,128)S(1)}, f32[4,1,256]{2,1,0:T(1,128)}, u32[]{:S(2)}) copy-start(f32[4,1,256]{2,1,0:T(1,128)} %get-tuple-element.123) | copy-start | bytes 12292
  354.3 6.3 %copy-start.10 = (f32[4,1,256]{2,1,0:T(1,128)S(1)}, f32[4,1,256]{2,1,0:T(1,128)}, u32[]{:S(2)}) copy-start(f32[4,1,256]{2,1,0:T(1,128)} %get-tuple-element.124) | copy-start | bytes 12292
  354.3 6.3 %copy-start.8 = (f32[4,1,512]{2,1,0:T(1,128)S(1)}, f32[4,1,512]{2,1,0:T(1,128)}, u32[]{:S(2)}) copy-start(f32[4,1,512]{2,1,0:T(1,128)} %get-tuple-element.125) | copy-start | bytes 24580
  354.3 6.3 %copy-start.7 = (f32[4,1024]{1,0:T(4,128)S(1)}, f32[4,1024]{1,0:T(4,128)}, u32[]{:S(2)}) copy-start(f32[4,1024]{1,0:T(4,128)} %get-tuple-element.120) | copy-start | bytes 49156
  354.3 6.4 %copy-start.12 = (f32[2,512]{1,0:T(2,128)S(1)}, f32[2,512]{1,0:T(2,128)}, u32[]{:S(2)}) copy-start(f32[2,512]{1,0:T(2,128)} %get-tuple-element.122) | copy-start | bytes 12292
  354.3 6.4 %copy-start.11 = (f32[2,512]{1,0:T(2,128)S(1)}, f32[2,512]{1,0:T(2,128)}, u32[]{:S(2)}) copy-start(f32[2,512]{1,0:T(2,128)} %get-tuple-element.121) | copy-start | bytes 12292
  357.1 36.2 %collective-permute-start.2 = (bf16[256,1024]{1,0:T(8,128)(2,1)}, bf16[256,1024]{1,0:T(8,128)(2,1)S(1)}, u32[]{:S(2)}, u32[]{:S(2)}) collective-permute-start(bf16[256,1024]{1,0:T(8,128)(2,1)} %get-tuple-element.177), channel_id=1, source_target_pairs={{0,24},{8,0},{16,8},{24,16},{1,25},{9,1},{17,9},{25,17},{2,26},{10... | collective-permute-start | bytes 1572872 | tf_op jit(solution)/shard_map/ppermute | solution.py:1299
  358.6 34.6 %collective-permute-start.1 = (bf16[256,1024]{1,0:T(8,128)(2,1)}, bf16[256,1024]{1,0:T(8,128)(2,1)}, u32[]{:S(2)}, u32[]{:S(2)}) collective-permute-start(bf16[256,1024]{1,0:T(8,128)(2,1)} %get-tuple-element.178), channel_id=1, source_target_pairs={{0,16},{8,24},{16,0},{24,8},{1,17},{9,25},{17,1},{25,9},{2,18},{10... | collective-permute-start | bytes 1572872 | tf_op jit(solution)/shard_map/ppermute | solution.py:1299
  359.7 33.6 %collective-permute-start = (bf16[256,1024]{1,0:T(8,128)(2,1)}, bf16[256,1024]{1,0:T(8,128)(2,1)}, u32[]{:S(2)}, u32[]{:S(2)}) collective-permute-start(bf16[256,1024]{1,0:T(8,128)(2,1)} %get-tuple-element.179), channel_id=1, source_target_pairs={{0,8},{8,16},{16,24},{24,0},{1,9},{9,17},{17,25},{25,1},{2,10},{10... | collective-permute-start | bytes 1572872 | tf_op jit(solution)/shard_map/ppermute | solution.py:1299
  386.8 11.6 %copy-start.5 = (f32[1,2,12,1024]{3,1,2,0:T(2,128)S(1)}, f32[1,2,12,1024]{3,1,2,0:T(2,128)}, u32[]{:S(2)}) copy-start(f32[1,2,12,1024]{3,1,2,0:T(2,128)} %param.20) | copy-start | bytes 294916
  386.8 12.3 %copy-start = (bf16[2,577,1024]{2,1,0:T(8,128)(2,1)S(1)}, bf16[2,577,1024]{2,1,0:T(8,128)(2,1)}, u32[]{:S(2)}) copy-start(bf16[2,577,1024]{2,1,0:T(8,128)(2,1)} %get-tuple-element.95) | copy-start | bytes 7090180
  394.8 50.9 %copy-start.1 = (bf16[256,1024]{1,0:T(8,128)(2,1)}, bf16[256,1024]{1,0:T(8,128)(2,1)S(1)}, u32[]{:S(2)}) copy-start(bf16[256,1024]{1,0:T(8,128)(2,1)S(1)} %add_convert_fusion.refs_0_) | copy-start | bytes 1572868
  394.8 50.9 %collective-permute-start.5 = (bf16[256,1024]{1,0:T(8,128)(2,1)S(1)}, bf16[256,1024]{1,0:T(8,128)(2,1)S(1)}, u32[]{:S(2)}, u32[]{:S(2)}) collective-permute-start(bf16[256,1024]{1,0:T(8,128)(2,1)S(1)} %add_convert_fusion.refs_0_), channel_id=1, source_target_pairs={{0,24},{8,0},{16,8},{24,16},{1,25},{9,1},{17,9},{25,17},{2,26},{10... | collective-permute-start | bytes 1572872 | tf_op jit(solution)/shard_map/ppermute | solution.py:1299
  397.3 48.5 %collective-permute-start.4 = (bf16[256,1024]{1,0:T(8,128)(2,1)S(1)}, bf16[256,1024]{1,0:T(8,128)(2,1)S(1)}, u32[]{:S(2)}, u32[]{:S(2)}) collective-permute-start(bf16[256,1024]{1,0:T(8,128)(2,1)S(1)} %add_convert_fusion.refs_0_), channel_id=1, source_target_pairs={{0,16},{8,24},{16,0},{24,8},{1,17},{9,25},{17,1},{25,9},{2,18},{10... | collective-permute-start | bytes 1572872 | tf_op jit(solution)/shard_map/ppermute | solution.py:1299
  397.8 47.9 %collective-permute-start.3 = (bf16[256,1024]{1,0:T(8,128)(2,1)S(1)}, bf16[256,1024]{1,0:T(8,128)(2,1)}, u32[]{:S(2)}, u32[]{:S(2)}) collective-permute-start(bf16[256,1024]{1,0:T(8,128)(2,1)S(1)} %add_convert_fusion.refs_0_), channel_id=1, source_target_pairs={{0,8},{8,16},{16,24},{24,0},{1,9},{9,17},{17,25},{25,1},{2,10},{10... | collective-permute-start | bytes 1572872 | tf_op jit(solution)/shard_map/ppermute | solution.py:1299
  445.7 0.8 copy-start.2
  445.7 1.0 copy-start.3
  477.6 3.9 copy-start.4
  477.6 4.6 copy-start.6
Sparse Core Ops, SparseCore 0:
  159.4 48.3 reduce-scatter.5
  210.2 43.1 reduce-scatter.7
  255.7 76.1 reduce-scatter.9
  334.1 52.5 reduce-scatter.13
  389.0 37.0 reduce-scatter.11

commit v4 on v2

--- a/solution.py
+++ b/solution.py
@@ -454,7 +454,68 @@
     )(alive, resid, branch, grad_normed, grad_two, attended, w_attn, vec)
 
 
-def unattend_kernel(seq, q_ref, k_ref, v_ref, g_ref, out_ref):
+def carrier(groups, paired, diff_ref, total_ref, mine, landed, sends, receives, loaded):
+    g, f, t = lax.axis_index("group"), lax.axis_index("fsdp"), lax.axis_index("tensor")
+    quarter = landed.shape[1]
+
+    def rows(n):
+        return pl.ds(pl.multiple_of(n * quarter, quarter), quarter)
+
+    def other(k):
+        return (lax.rem(g + k, groups), f, t)
+
+    def part(k):
+        return pltpu.make_async_remote_copy(
+            src_ref=diff_ref.at[rows(lax.rem(g + k, groups)), :],
+            dst_ref=landed.at[k],
+            send_sem=sends.at[k],
+            recv_sem=receives.at[k],
+            device_id=other(k),
+            device_id_type=MESH,
+        )
+
+    keep = pltpu.make_async_copy(diff_ref.at[rows(g), :], mine, loaded.at[0])
+
+    def begin():
+        barrier = pltpu.get_barrier_semaphore()
+        if paired:
+            pl.semaphore_signal(barrier, inc=1, device_id=partner(), device_id_type=MESH)
+        for k in range(1, groups):
+            pl.semaphore_signal(barrier, inc=1, device_id=other(k), device_id_type=MESH)
+        pl.semaphore_wait(barrier, groups - 1 + int(paired))
+        for k in range(1, groups):
+            part(k).start()
+        keep.start()
+
+    def end():
+        keep.wait()
+        total = mine[...].astype(F32)
+        for k in range(1, groups):
+            part(k).wait()
+            total = total + landed[k].astype(F32)
+        total_ref[...] = total.astype(LOW)
+
+    return begin, end
+
+
+def carrier_scratch(groups, quarter, lanes):
+    dma = pltpu.SemaphoreType.DMA
+    return [
+        pltpu.VMEM((quarter, lanes), LOW),
+        pltpu.VMEM((groups, quarter, lanes), LOW),
+        dma((groups,)),
+        dma((groups,)),
+        dma((1,)),
+    ]
+
+
+def unattend_kernel(seq, groups, q_ref, k_ref, v_ref, g_ref, *refs):
+    if groups:
+        diff_ref, out_ref, total_ref, *scratch = refs
+        begin, end = carrier(groups, False, diff_ref, total_ref, *scratch)
+        pl.when((pl.program_id(0) == 0) & (pl.program_id(1) == 0))(begin)
+    else:
+        (out_ref,) = refs
     span = q_ref.shape[1]
     scale = HD**-0.5
     q, k, v, g = q_ref[0], k_ref[0], v_ref[0], g_ref[...]
@@ -478,9 +539,12 @@
     out_ref[0] = (jnp.where(lane, parts[0][0], parts[1][0]) * scale).astype(LOW)
     out_ref[1] = (jnp.where(lane, parts[0][1], parts[1][1]) * scale).astype(LOW)
     out_ref[2] = jnp.where(lane, parts[0][2], parts[1][2]).astype(LOW)
-
-
-def unattend(qkv, grad_attended, images, seq, part, parts, shards):
+    if groups:
+        at_end = (pl.program_id(0) == pl.num_programs(0) - 1) & (pl.program_id(1) == pl.num_programs(1) - 1)
+        pl.when(at_end)(end)
+
+
+def unattend(qkv, grad_attended, images, seq, part, parts, shards, diff=None, groups=0):
     _, rows, width = qkv.shape
     span = rows // images
     pair = 2 * HD
@@ -492,18 +556,29 @@
     def take(j):
         return pl.BlockSpec((1, span, pair), lambda i, h: (j, i, spot(h)))
 
+    in_specs = [take(0), take(1), take(2), pl.BlockSpec((span, pair), lambda i, h: (i, spot(h)))]
+    out_specs = [pl.BlockSpec((3, span, pair), lambda i, h: (0, i, h))]
+    out_shape = [jax.ShapeDtypeStruct((3, rows, width // parts), LOW)]
+    scratch = []
+    if groups:
+        quarter, lanes = diff.shape[0] // groups, diff.shape[1]
+        in_specs.append(pl.BlockSpec(memory_space=pl.ANY))
+        out_specs.append(pl.BlockSpec((quarter, lanes), lambda i, h: (0, 0)))
+        out_shape.append(jax.ShapeDtypeStruct((quarter, lanes), LOW))
+        scratch = carrier_scratch(groups, quarter, lanes)
     return pl.pallas_call(
-        functools.partial(unattend_kernel, seq),
+        functools.partial(unattend_kernel, seq, groups),
         grid=(images, width // pair // parts),
-        in_specs=[take(0), take(1), take(2), pl.BlockSpec((span, pair), lambda i, h: (i, spot(h)))],
-        out_specs=pl.BlockSpec((3, span, pair), lambda i, h: (0, i, h)),
-        out_shape=jax.ShapeDtypeStruct((3, rows, width // parts), LOW),
-        compiler_params=params(),
+        in_specs=in_specs,
+        out_specs=out_specs,
+        out_shape=out_shape,
+        scratch_shapes=scratch,
+        compiler_params=params(9 if groups else None),
         cost_estimate=cost(
             40 * rows * span * width // parts, 14 * rows * width // parts, rows * span * (width // HD) // parts
         ),
         name=f"unattend_{part}",
-    )(qkv, qkv, qkv, grad_attended)
+    )(qkv, qkv, qkv, grad_attended, *([diff] if groups else []))
 
 
 def close_kernel(pairwise, groups, first, final, n_ref, grad_ref, w_ref, *refs):
@@ -523,38 +598,8 @@
         if not final:
             pl.when(j == 0)(greet_partner)
     if pairwise and final:
-        mine, landed, sends_two, receives_two, loaded = exchange
-        g, f, t = lax.axis_index("group"), lax.axis_index("fsdp"), lax.axis_index("tensor")
-        quarter = landed.shape[1]
-
-        def rows(n):
-            return pl.ds(pl.multiple_of(n * quarter, quarter), quarter)
-
-        def other(k):
-            return (lax.rem(g + k, groups), f, t)
-
-        def part(k):
-            return pltpu.make_async_remote_copy(
-                src_ref=diff_ref.at[rows(lax.rem(g + k, groups)), :],
-                dst_ref=landed.at[k],
-                send_sem=sends_two.at[k],
-                recv_sem=receives_two.at[k],
-                device_id=other(k),
-                device_id_type=MESH,
-            )
-
-        keep = pltpu.make_async_copy(diff_ref.at[rows(g), :], mine, loaded.at[0])
-
-        @pl.when(j == 0)
-        def _():
-            barrier = pltpu.get_barrier_semaphore()
-            pl.semaphore_signal(barrier, inc=1, device_id=partner(), device_id_type=MESH)
-            for k in range(1, groups):
-                pl.semaphore_signal(barrier, inc=1, device_id=other(k), device_id_type=MESH)
-            pl.semaphore_wait(barrier, groups)
-            for k in range(1, groups):
-                part(k).start()
-            keep.start()
+        begin, end = carrier(groups, True, diff_ref, total_ref, *exchange)
+        pl.when(j == 0)(begin)
 
     @pl.when(j == 0)
     def _():
@@ -600,12 +645,7 @@
                         dw_ref[t, 3 + n] = more_ref[t, 0, :, n * cols : (n + 1) * cols]
         acc_ref[...] = acc_scr[...]
         if pairwise and final:
-            keep.wait()
-            total = mine[...].astype(F32)
-            for k in range(1, groups):
-                part(k).wait()
-                total = total + landed[k].astype(F32)
-            total_ref[...] = total.astype(LOW)
+            end()
 
 
 def close(part, parts, normed, grads, w_attn, carry, more, ending, fsdp, groups):
@@ -640,15 +680,7 @@
         in_specs.append(pl.BlockSpec(memory_space=pl.ANY))
         out_specs.append(pl.BlockSpec((quarter, lanes_two), lambda j: (0, 0), pipeline_mode=single))
         out_shape.append(jax.ShapeDtypeStruct((quarter, lanes_two), LOW))
-        dma = pltpu.SemaphoreType.DMA
-        extra = [
-            *extra,
-            pltpu.VMEM((quarter, lanes_two), LOW),
-            pltpu.VMEM((groups, quarter, lanes_two), LOW),
-            dma((groups,)),
-            dma((groups,)),
-            dma((1,)),
-        ]
+        extra = [*extra, *carrier_scratch(groups, quarter, lanes_two)]
     return pl.pallas_call(
         functools.partial(close_kernel, pairwise, groups, first, final),
         grid=(3,),
@@ -913,8 +945,6 @@
     m_hold[...] = m_wide[...].astype(LOW)
     keeps[1].start()
     maps(z)
-    for i in range(images):
-        g2_scr[pl.ds(i * span, seq), :] = (g_ref[:, i, :].astype(F32) * alive_ref[i]).astype(LOW)
     both(land, 0, 2)
     both(relay, 0, 1)
     keeps[1].wait()
@@ -969,6 +999,8 @@
     at = 1 + min(segments, total - 3)
     puts.append(pltpu.make_async_copy(att_scr, att_out, ws.at[3]))
     puts[-1].start()
+    for i in range(images):
+        g2_scr[pl.ds(i * span, seq), :] = (g_ref[:, i, :].astype(F32) * alive_ref[i]).astype(LOW)
     while at < total - 2:
         advance(at)
         at += 1
@@ -1433,7 +1465,7 @@
     pairwise = fsdp == 2
     me = lax.axis_index("group").astype(jnp.int32).reshape(1)
     half = attn_master.shape[2] // PARTS
-    grads = unattend(qkv, grad_attended, images, seq, 0, PARTS, tensor_size)
+    (grads,) = unattend(qkv, grad_attended, images, seq, 0, PARTS, tensor_size)
     grads, mlp_grads[0] = lax.optimization_barrier((grads, mlp_grads[0]))
     carry, dw_early, head_sums = close(
         0, PARTS, normed_one, grads, w_attn, None, dw_out, None, fsdp, groups
@@ -1444,17 +1476,24 @@
     early_grad = scatter_gradient(dw_early)
     head_sums = [head_sums]
     carry, mlp_grads[1] = lax.optimization_barrier((carry, mlp_grads[1]))
-    grads = unattend(qkv, grad_attended, images, seq, 1, PARTS, tensor_size)
-
-    mlp_grads[0], grads = lax.optimization_barrier((mlp_grads[0], grads))
-    mlp_inner, mlp_diff = inner_step(
-        beside, mlp_grads, lambda u: (u, 0), 2, mlp_master.shape[2], mlp_master, mlp_moments, None, "inner_mlp"
-    )
-    carry, mlp_diff = lax.optimization_barrier((carry, mlp_diff))
-    ending = mlp_diff.reshape(-1, mlp_diff.shape[-1])
-    carry, *mlp_own, dw_late, sums = close(
-        1, PARTS, normed_one, grads, w_attn, carry, None, ending, fsdp, groups
-    )
+    hidden = mlp_master.shape[2] // 2
+    mlp_inner, diff_one = inner_step(
+        beside, mlp_grads[:2], lambda u: (u, 0), 2, hidden, mlp_master, mlp_moments, None, "inner_mlp_0"
+    )
+    riding = groups if pairwise else 0
+    grads, *own_one = unattend(
+        qkv, grad_attended, images, seq, 1, PARTS, tensor_size, diff_one.reshape(-1, hidden), riding
+    )
+    mlp_grads[2], grads = lax.optimization_barrier((mlp_grads[2], grads))
+    mlp_inner, diff_two = inner_step(
+        beside, mlp_grads[2:], lambda u: (u, 1), 2, hidden, mlp_master, mlp_moments, mlp_inner, "inner_mlp_1"
+    )
+    carry, diff_two = lax.optimization_barrier((carry, diff_two))
+    carry, *own_two, dw_late, sums = close(
+        1, PARTS, normed_one, grads, w_attn, carry, None, diff_two.reshape(-1, hidden), fsdp, groups
+    )
+    mlp_own = [beside(*own_one, *own_two)] if pairwise else []
+    mlp_diff = beside(diff_one, diff_two)
     patches_grad, sums_one = finish(carry, grad_resid, x_rows, vec, images, seq)
     if not pairwise:
         mlp_own = [exchange_parts(mlp_diff, groups)]

time: 484 us -> 479 us (0.990)
  Pallas kernels: 441 us -> 434 us
    pallas_call x2, Pallas kernels: 50.3 us -> 39.4 us  [close(): pl.pallas_call(functools.partial(close_kernel, pairwise, groups, first, f...]
    pallas_call x3 -> x4, Pallas kernels: 20.9 us -> 22.8 us  [inner_step(): pl.pallas_call(functools.partial(inner_kernel, join, count), grid=(units,...]
where the time goes in v4:
time: 479 us; the launch traced here: 470 us
  Pallas kernels  434 us (91%)
  between operations  14.5 us (3%)
  local copies, waits for them, and re-layouts  13.5 us (3%)
    pallas_call x1, Pallas kernels, front(): pl.pallas_call(functools.partial(front_kernel, images, seq), in_specs=[pl...  124 us
    pallas_call x3, Pallas kernels, mlp(): pl.pallas_call(functools.partial(mlp_kernel, first, pairwise), grid=(step...  96 us
    pallas_call x2, Pallas kernels, unattend(): pl.pallas_call(functools.partial(unattend_kernel, seq, groups), grid=(ima...  59.1 us
    pallas_call x2, Pallas kernels, group_sum(): pl.pallas_call(functools.partial(group_kernel, groups, shards, bool(vecto...  41.6 us
    pallas_call x2, Pallas kernels, close(): pl.pallas_call(functools.partial(close_kernel, pairwise, groups, first, f...  39.4 us
    pallas_call x4, Pallas kernels, inner_step(): pl.pallas_call(functools.partial(inner_kernel, join, count), grid=(units,...  22.8 us
    pallas_call x1, Pallas kernels, turn(): pl.pallas_call(functools.partial(turn_kernel, seq, pairwise), grid=(image...  21.7 us
    pallas_call x3, Pallas kernels, outer_step(): pl.pallas_call(functools.partial(outer_kernel, groups, slots, each), grid...  19.9 us
  transfers between devices with their start and end apart: 8, of which 1 were waited for; matrix products, arithmetic and copies ran while one was open for 2% of the time, Pallas kernels for 56%

profile of v4, /device:TPU:0, one launch (start us, length us, event | category | flops | bytes accessed | tf_op | source)
XLA Modules:
  0.0 469.5 jit_solution(3461568929346709654)
XLA Ops:
  10.0 123.8 %front.1 = (bf16[4,4,1024,256]{3,2,1,0:T(8,128)(2,1)}, bf16[4,2,1024,1024]{3,2,1,0:T(8,128)(2,1)}, bf16[1184,1024]{1,0:T(8,128)(2,1)}, bf16[3,1184,1024]{2,1,0:T...) custom-call(f32[2]{0:T(128)} %fusion.alive_ref, ...), custom_call_target="tpu_custom_call" | custom-call | flops 9932111872 | bytes 36372480 | tf_op jit(solution)/shard_map/front/pallas_call | solution.py:1078
  133.8 25.5 %mlp_0.1 = (f32[1184,1024]{1,0:T(8,128)}, f32[1184,1024]{1,0:T(8,128)}, bf16[4,2,512,256]{3,2,1,0:T(8,128)(2,1)}, f32[4,1,256]{2,1,0:T(1,128)}) custom-call(bf16[1184,1024]{1,0:T(8,128)(2,1)} %get-tuple-element.82.n_ref, bf16[1184,1024]{1,0:T(8,128)(2,1)} %get-tuple-element.83.g_ref.g2_ref, bf16[4,2,1024,1024]{3,2,1,0:T(8,128)(2,1)} %get-tuple-element.84.w1_ref.w2_ref, ...), custom_call_target="tpu_custom_call" | custom-call | flops 14898167808 | bytes 29097984 | tf_op jit(solution)/shard_map/mlp_0/pallas_call | solution.py:334
  159.3 25.9 %mlp_1.1 = (f32[1184,1024]{1,0:T(8,128)}, f32[1184,1024]{1,0:T(8,128)}, bf16[4,2,512,256]{3,2,1,0:T(8,128)(2,1)}, f32[4,1,256]{2,1,0:T(1,128)}) custom-call(bf16[1184,1024]{1,0:T(8,128)(2,1)} %get-tuple-element.82.n_ref, bf16[1184,1024]{1,0:T(8,128)(2,1)} %get-tuple-element.83.g_ref.g2_ref, bf16[4,2,1024,1024]{3,2,1,0:T(8,128)(2,1)} %get-tuple-element.84.w1_ref.w2_ref, ...), custom_call_target="tpu_custom_call" | custom-call | flops 14898167808 | bytes 29097984 | tf_op jit(solution)/shard_map/mlp_1/pallas_call | solution.py:334
  185.3 44.6 %mlp_2.1 = (f32[1184,1024]{1,0:T(8,128)}, f32[1184,1024]{1,0:T(8,128)}, bf16[4,2,512,512]{3,2,1,0:T(8,128)(2,1)}, f32[4,1,512]{2,1,0:T(1,128)}) custom-call(bf16[1184,1024]{1,0:T(8,128)(2,1)} %get-tuple-element.82.n_ref, bf16[1184,1024]{1,0:T(8,128)(2,1)} %get-tuple-element.83.g_ref.g2_ref, bf16[4,2,1024,1024]{3,2,1,0:T(8,128)(2,1)} %get-tuple-element.84.w1_ref.w2_ref, ...), custom_call_target="tpu_custom_call" | custom-call | flops 29796335616 | bytes 29097984 | tf_op jit(solution)/shard_map/mlp_2/pallas_call | solution.py:334
  230.1 21.7 %turn.1 = (bf16[2,577,1024]{2,1,0:T(8,128)(2,1)}, f32[1184,1024]{1,0:T(8,128)}, bf16[1184,1024]{1,0:T(8,128)(2,1)}, bf16[4,1,512,256]{3,2,1,0:T(8,128)(2,1)}, f32[4,1024]{1,0:T(4,128)}) custom-call(f32[2]{0:T(128)} %fusion.alive_ref, f32[1184,1024]{1,0:T(8,128)} %get-tuple-element.81.resid_ref, f32[1184,1024]{1,0:T(8,128)} %get-tuple-element.89.y_ref, ...), custom_call_target="tpu_custom_call" | custom-call | flops 4966055936 | bytes 29097984 | tf_op jit(solution)/shard_map/turn/pallas_call | solution.py:428
  251.7 28.4 %unattend_0.1.grad_ref = bf16[3,1184,512]{2,1,0:T(8,128)(2,1)} custom-call(bf16[3,1184,1024]{2,1,0:T(8,128)(2,1)} %get-tuple-element.96.q_ref.k_ref.v_ref, bf16[3,1184,1024]{2,1,0:T(8,128)(2,1)} %get-tuple-element.96.q_ref.k_ref.v_ref, bf16[3,1184,1024]{2,1,0:T(8,128)(2,1)} %get-tuple-element.96.q_ref.k_ref.v_ref, bf16[1184,1024]{1,0:T(8,128)(2,1)} %get-tuple-element.97.g_ref), custom_call_target="tpu_custom_call" | custom-call | flops 14355005440 | bytes 8486912 | tf_op jit(solution)/shard_map/unattend_0/pallas_call | solution.py:569
  280.1 17.4 %close_0.1 = (f32[1184,1024]{1,0:T(8,128)}, bf16[4,5,512,128]{3,2,1,0:T(8,128)(2,1)}, f32[2,512]{1,0:T(2,128)}) custom-call(bf16[1184,1024]{1,0:T(8,128)(2,1)} %get-tuple-element.94.n_ref, bf16[3,1184,512]{2,1,0:T(8,128)(2,1)} %unattend_0.1.grad_ref, bf16[4,4,1024,256]{3,2,1,0:T(8,128)(2,1)} %get-tuple-element.92.w_ref, ...), custom_call_target="tpu_custom_call" | custom-call | flops 7449083904 | bytes 24248320 | tf_op jit(solution)/shard_map/close_0/pallas_call | solution.py:684
  297.6 6.2 %inner_mlp_0.1 = (f32[1,2,2,512,1024]{4,3,2,1,0:T(8,128)}, bf16[2,512,512]{2,1,0:T(8,128)(2,1)}) custom-call(bf16[2,512,256]{2,1,0:T(8,128)(2,1)} %bitcast.42, bf16[2,512,256]{2,1,0:T(8,128)(2,1)} %bitcast.43, f32[2,512,1024]{2,1,0:T(8,128)} %refs_4_.1, f32[1,2,2,512,1024]{4,3,2,1,0:T(8,128)} %refs_2_.7), custom_call_target="tpu_custom_call" | custom-call | flops 15728640 | bytes 12582912 | tf_op jit(solution)/shard_map/inner_mlp_0/pallas_call | solution.py:1148
  303.8 30.7 %unattend_1.1 = (bf16[3,1184,512]{2,1,0:T(8,128)(2,1)}, bf16[256,512]{1,0:T(8,128)(2,1)}) custom-call(bf16[3,1184,1024]{2,1,0:T(8,128)(2,1)} %get-tuple-element.96.q_ref.k_ref.v_ref, bf16[3,1184,1024]{2,1,0:T(8,128)(2,1)} %get-tuple-element.96.q_ref.k_ref.v_ref, bf16[3,1184,1024]{2,1,0:T(8,128)(2,1)} %get-tuple-element.96.q_ref.k_ref.v_ref, ...), custom_call_target="tpu_custom_call" | custom-call | flops 14355005440 | bytes 8486912 | tf_op jit(solution)/shard_map/unattend_1/pallas_call | solution.py:569
  334.5 6.0 %inner_mlp_1.1 = (f32[1,2,2,512,1024]{4,3,2,1,0:T(8,128)}, bf16[2,512,512]{2,1,0:T(8,128)(2,1)}) custom-call(bf16[2,512,512]{2,1,0:T(8,128)(2,1)} %bitcast.37, f32[2,512,1024]{2,1,0:T(8,128)} %refs_4_.1, f32[1,2,2,512,1024]{4,3,2,1,0:T(8,128)} %refs_2_.7, f32[1,2,2,512,1024]{4,3,2,1,0:T(8,128)} %get-tuple-element.110.refs_3_), custom_call_target="tpu_custom_call", output_to_operand_aliasing={{0}: (3, {})} | custom-call | flops 15728640 | bytes 12582912 | tf_op jit(solution)/shard_map/inner_mlp_1/pallas_call | solution.py:1148
  340.5 22.0 %close_1.1 = (f32[1184,1024]{1,0:T(8,128)}, bf16[256,512]{1,0:T(8,128)(2,1)}, bf16[4,3,512,128]{3,2,1,0:T(8,128)(2,1)}, f32[2,512]{1,0:T(2,128)}) custom-call(bf16[1184,1024]{1,0:T(8,128)(2,1)} %get-tuple-element.94.n_ref, bf16[3,1184,512]{2,1,0:T(8,128)(2,1)} %get-tuple-element.107.grad_ref, bf16[4,4,1024,256]{3,2,1,0:T(8,128)(2,1)} %get-tuple-element.92.w_ref, ...), custom_call_target="tpu_custom_call" | custom-call | flops 7449083904 | bytes 24248320 | tf_op jit(solution)/shard_map/close_1/pallas_call | solution.py:684
  363.8 1.6 collective-permute-start.2
  368.4 3.8 copy.31
  372.3 9.8 %finish.1 = (f32[2,577,1,1024]{3,2,1,0:T(1,128)}, f32[2,1024]{1,0:T(2,128)}) custom-call(f32[1184,1024]{1,0:T(8,128)} %get-tuple-element.114.acc_ref, f32[1184,1024]{1,0:T(8,128)} %get-tuple-element.115.gr_ref, bf16[1184,1024]{1,0:T(8,128)(2,1)} %get-tuple-element.116.x_ref, f32[12,1024]{1,0:T(8,128)} %refs_1_.8), custom_call_target="tpu_custom_call" | custom-call | flops 24248320 | bytes 16973824 | tf_op jit(solution)/shard_map/finish/pallas_call | solution.py:719
  382.1 2.0 concatenate.14.refs_0_
  384.1 2.6 reduce-scatter.14.cloned.1.call-done
  386.7 6.3 %inner_early.1 = (f32[1,2,4,512,256]{4,3,2,1,0:T(8,128)}, bf16[5,512,128]{2,1,0:T(8,128)(2,1)}) custom-call(bf16[5,512,128]{2,1,0:T(8,128)(2,1)} %bitcast.40, f32[4,512,256]{2,1,0:T(8,128)} %refs_1_.11, f32[1,2,4,512,256]{4,3,2,1,0:T(8,128)} %refs_2_.10), custom_call_target="tpu_custom_call" | custom-call | flops 9830400 | bytes 7864320 | tf_op jit(solution)/shard_map/inner_early/pallas_call | solution.py:1148
  393.0 26.5 %group_early.1 = (bf16[2560,128]{1,0:T(8,128)(2,1)}, f32[2,12,1024]{2,1,0:T(8,128)}, f32[3,12,1024]{2,1,0:T(8,128)}, bf16[12,1024]{1,0:T(8,128)(2,1)}) custom-call(bf16[2560,128]{1,0:T(8,128)(2,1)} %bitcast.39, f32[12,1024]{1,0:T(8,128)} %concatenate.14.refs_0_, f32[12,1024]{1,0:T(8,128)} %refs_1_.8, f32[2,12,1024]{2,1,0:T(8,128)} %bitcast.41, ...), custom_call_target="tpu_custom_call" | custom-call | flops 1310720 | bytes 2621440 | tf_op jit(solution)/shard_map/group_early/pallas_call | solution.py:1367
  419.5 1.6 copy.33
  421.1 5.6 %outer_early.1 = (f32[3,4,512,256]{3,2,1,0:T(8,128)}, bf16[4,512,256]{2,1,0:T(8,128)(2,1)}) custom-call(s32[1]{0:T(128)} %bitcast.17.g_ref, bf16[5,512,128]{2,1,0:T(8,128)(2,1)} %bitcast.38, f32[4,512,256]{2,1,0:T(8,128)} %refs_1_.11, f32[4,512,256]{2,1,0:T(8,128)} %refs_2_.11), custom_call_target="tpu_custom_call" | custom-call | flops 3276800 | bytes 7864320 | tf_op jit(solution)/shard_map/outer_early/pallas_call | solution.py:1196
  427.5 10.4 %outer_mlp.1 = (f32[3,2,512,1024]{3,2,1,0:T(8,128)}, bf16[2,512,1024]{2,1,0:T(8,128)(2,1)}) custom-call(s32[1]{0:T(128)} %bitcast.17.g_ref, bf16[256,1024]{1,0:T(8,128)(2,1)} %copy-done.1, bf16[256,1024]{1,0:T(8,128)(2,1)} %collective-permute-done.refs_1_, bf16[256,1024]{1,0:T(8,128)(2,1)} %collective-permute-done.1.refs_2_, bf16[256,1024]{1,0:T(8,128)(2,1)} %copy-done.2, ...), custom_call_target="tpu_custom_call" | custom-call | flops 10485760 | bytes 25165824 | tf_op jit(solution)/shard_map/outer_mlp/pallas_call | solution.py:1196
  437.9 4.3 inner_late.1
  442.2 15.1 %group_late.1 = bf16[1536,128]{1,0:T(8,128)(2,1)} custom-call(bf16[1536,128]{1,0:T(8,128)(2,1)} %bitcast.44), custom_call_target="tpu_custom_call" | custom-call | flops 786432 | bytes 1572864 | tf_op jit(solution)/shard_map/group_late/pallas_call | solution.py:1367
  457.4 3.9 outer_late.1
  (60 shorter events, 9.4 us)
Async XLA Ops:
  7.2 273.0 %reduce-scatter.8.cloned.1.call-start = ((), (), s32[]{:S(2)}) async-start(), calls=%async_computation.6 | async-start | bytes 2621440 | tf_op jit(solution)/shard_map/reduce_scatter | solution.py:1408
  159.3 138.3 %reduce-scatter.10.cloned.1.call-start = ((), (), s32[]{:S(2)}) async-start(), calls=%async_computation.7 | async-start | bytes 2621440 | tf_op jit(solution)/shard_map/reduce_scatter | solution.py:1408
  185.3 149.2 %reduce-scatter.6.cloned.1.call-start = ((), (), s32[]{:S(2)}) async-start(), calls=%async_computation.5 | async-start | bytes 5242880 | tf_op jit(solution)/shard_map/reduce_scatter | solution.py:1408
  230.0 156.7 %reduce-scatter.14.cloned.1.call-start = ((), (), s32[]{:S(2)}) async-start(), calls=%async_computation.9 | async-start | bytes 3276800 | tf_op jit(solution)/shard_map/reduce_scatter | solution.py:1408
  297.5 140.4 %reduce-scatter.12.cloned.1.call-start = ((), (), s32[]{:S(2)}) async-start(), calls=%async_computation.8 | async-start | bytes 1966080 | tf_op jit(solution)/shard_map/reduce_scatter | solution.py:1408
  340.5 22.1 %copy-start.3 = (bf16[256,512]{1,0:T(8,128)(2,1)S(1)}, bf16[256,512]{1,0:T(8,128)(2,1)}, u32[]{:S(2)}) copy-start(bf16[256,512]{1,0:T(8,128)(2,1)} %get-tuple-element.130) | copy-start | bytes 786436
  340.5 26.4 %copy-start.5 = (f32[1,2,12,1024]{3,1,2,0:T(2,128)S(1)}, f32[1,2,12,1024]{3,1,2,0:T(2,128)}, u32[]{:S(2)}) copy-start(f32[1,2,12,1024]{3,1,2,0:T(2,128)} %param.20) | copy-start | bytes 294916
  362.6 5.8 %copy-start = (bf16[2,577,1024]{2,1,0:T(8,128)(2,1)S(1)}, bf16[2,577,1024]{2,1,0:T(8,128)(2,1)}, u32[]{:S(2)}) copy-start(bf16[2,577,1024]{2,1,0:T(8,128)(2,1)} %get-tuple-element.93) | copy-start | bytes 7090180
  362.6 9.7 %copy-start.7 = (f32[4,1024]{1,0:T(4,128)S(1)}, f32[4,1024]{1,0:T(4,128)}, u32[]{:S(2)}) copy-start(f32[4,1024]{1,0:T(4,128)} %get-tuple-element.122) | copy-start | bytes 49156
  363.8 18.4 %copy-start.1 = (bf16[256,1024]{1,0:T(8,128)(2,1)}, bf16[256,1024]{1,0:T(8,128)(2,1)S(1)}, u32[]{:S(2)}) copy-start(bf16[256,1024]{1,0:T(8,128)(2,1)S(1)} %constant_dynamic-update-slice_fusion.refs_0_) | copy-start | bytes 1572868
  363.8 62.9 %collective-permute-start.2 = (bf16[256,1024]{1,0:T(8,128)(2,1)S(1)}, bf16[256,1024]{1,0:T(8,128)(2,1)S(1)}, u32[]{:S(2)}, u32[]{:S(2)}) collective-permute-start(bf16[256,1024]{1,0:T(8,128)(2,1)S(1)} %constant_dynamic-update-slice_fusion.refs_0_), channel_id=1, source_target_pairs={{0,24},{8,0},{16,8},{24,16},{1,25},{9,1},{17,9},{25,17},{2,26},{10... | collective-permute-start | bytes 1572872 | tf_op jit(solution)/shard_map/ppermute | solution.py:1391
  365.4 61.3 %collective-permute-start.1 = (bf16[256,1024]{1,0:T(8,128)(2,1)S(1)}, bf16[256,1024]{1,0:T(8,128)(2,1)}, u32[]{:S(2)}, u32[]{:S(2)}) collective-permute-start(bf16[256,1024]{1,0:T(8,128)(2,1)S(1)} %constant_dynamic-update-slice_fusion.refs_0_), channel_id=1, source_target_pairs={{0,16},{8,24},{16,0},{24,8},{1,17},{9,25},{17,1},{25,9},{2,18},{10... | collective-permute-start | bytes 1572872 | tf_op jit(solution)/shard_map/ppermute | solution.py:1391
  366.7 60.0 %collective-permute-start = (bf16[256,1024]{1,0:T(8,128)(2,1)S(1)}, bf16[256,1024]{1,0:T(8,128)(2,1)}, u32[]{:S(2)}, u32[]{:S(2)}) collective-permute-start(bf16[256,1024]{1,0:T(8,128)(2,1)S(1)} %constant_dynamic-update-slice_fusion.refs_0_), channel_id=1, source_target_pairs={{0,8},{8,16},{16,24},{24,0},{1,9},{9,17},{17,25},{25,1},{2,10},{10... | collective-permute-start | bytes 1572872 | tf_op jit(solution)/shard_map/ppermute | solution.py:1391
  367.0 5.2 %copy-start.9 = (f32[4,1,256]{2,1,0:T(1,128)S(1)}, f32[4,1,256]{2,1,0:T(1,128)}, u32[]{:S(2)}) copy-start(f32[4,1,256]{2,1,0:T(1,128)} %get-tuple-element.126) | copy-start | bytes 12292
  367.0 5.2 %copy-start.8 = (f32[4,1,512]{2,1,0:T(1,128)S(1)}, f32[4,1,512]{2,1,0:T(1,128)}, u32[]{:S(2)}) copy-start(f32[4,1,512]{2,1,0:T(1,128)} %get-tuple-element.127) | copy-start | bytes 24580
  367.7 4.6 copy-start.10
  367.7 4.6 copy-start.11
  426.7 0.8 copy-start.2
  457.3 3.9 copy-start.4
  457.4 4.6 copy-start.6
Sparse Core Ops, SparseCore 0:
  159.4 48.3 reduce-scatter.7
  210.2 43.1 reduce-scatter.9
  255.7 76.0 reduce-scatter.5
  334.1 52.6 reduce-scatter.13
  389.0 37.0 reduce-scatter.11

commit v5 on v4

--- a/solution.py
+++ b/solution.py
@@ -930,23 +930,30 @@
     n_scr[...] = jnp.zeros_like(n_scr)
     x_all[...] = jnp.zeros_like(x_all)
     g2_scr[...] = jnp.zeros_like(g2_scr)
-    for i in range(images):
+
+    def norm_image(i):
         here = pl.ds(i * span, seq)
         image = x_ref[:, i, :]
         x_all[here, :] = image
         normal, _ = centred(image.astype(F32))
         n_scr[here, :] = (normal * vec_ref[0:1] + vec_ref[1:2]).astype(LOW)
-    puts = [pltpu.make_async_copy(n_scr, n_out, ws.at[1])]
-    puts[0].start()
-    puts.append(pltpu.make_async_copy(x_all, x_out, ws.at[7]))
-    puts[-1].start()
+
+    norm_image(0)
     both(land, 0, 1)
+    for i in range(1, images):
+        norm_image(i)
+    puts = [
+        pltpu.make_async_copy(n_scr, n_out, ws.at[1]),
+        pltpu.make_async_copy(x_all, x_out, ws.at[7]),
+    ]
+    for put in puts:
+        put.start()
+    both(land, 0, 2)
+    both(relay, 0, 1)
     loads[1].wait()
     m_hold[...] = m_wide[...].astype(LOW)
     keeps[1].start()
     maps(z)
-    both(land, 0, 2)
-    both(relay, 0, 1)
     keeps[1].wait()
     both(land, 0, 3)
     for n in range(1, count):

time: 479 us -> 477 us (level)
  no operation moved by 1% of the time
where the time goes in v5:
time: 477 us; the launch traced here: 468 us
  Pallas kernels  432 us (91%)
  between operations  14.5 us (3%)
  local copies, waits for them, and re-layouts  13.5 us (3%)
    pallas_call x1, Pallas kernels, front(): pl.pallas_call(functools.partial(front_kernel, images, seq), in_specs=[pl...  122 us
    pallas_call x3, Pallas kernels, mlp(): pl.pallas_call(functools.partial(mlp_kernel, first, pairwise), grid=(step...  96.8 us
    pallas_call x2, Pallas kernels, unattend(): pl.pallas_call(functools.partial(unattend_kernel, seq, groups), grid=(ima...  59.1 us
    pallas_call x2, Pallas kernels, group_sum(): pl.pallas_call(functools.partial(group_kernel, groups, shards, bool(vecto...  40.6 us
    pallas_call x2, Pallas kernels, close(): pl.pallas_call(functools.partial(close_kernel, pairwise, groups, first, f...  39.4 us
    pallas_call x4, Pallas kernels, inner_step(): pl.pallas_call(functools.partial(inner_kernel, join, count), grid=(units,...  22.8 us
    pallas_call x1, Pallas kernels, turn(): pl.pallas_call(functools.partial(turn_kernel, seq, pairwise), grid=(image...  21.5 us
    pallas_call x3, Pallas kernels, outer_step(): pl.pallas_call(functools.partial(outer_kernel, groups, slots, each), grid...  19.9 us
  transfers between devices with their start and end apart: 8, of which 1 were waited for; matrix products, arithmetic and copies ran while one was open for 2% of the time, Pallas kernels for 56%

profile of v5, /device:TPU:0, one launch (start us, length us, event | category | flops | bytes accessed | tf_op | source)
XLA Modules:
  0.0 468.3 jit_solution(762465442149660658)
XLA Ops:
  10.0 121.8 %front.1 = (bf16[4,4,1024,256]{3,2,1,0:T(8,128)(2,1)}, bf16[4,2,1024,1024]{3,2,1,0:T(8,128)(2,1)}, bf16[1184,1024]{1,0:T(8,128)(2,1)}, bf16[3,1184,1024]{2,1,0:T...) custom-call(f32[2]{0:T(128)} %fusion.alive_ref, ...), custom_call_target="tpu_custom_call" | custom-call | flops 9932111872 | bytes 36372480 | tf_op jit(solution)/shard_map/front/pallas_call | solution.py:1085
  131.8 26.3 %mlp_0.1 = (f32[1184,1024]{1,0:T(8,128)}, f32[1184,1024]{1,0:T(8,128)}, bf16[4,2,512,256]{3,2,1,0:T(8,128)(2,1)}, f32[4,1,256]{2,1,0:T(1,128)}) custom-call(bf16[1184,1024]{1,0:T(8,128)(2,1)} %get-tuple-element.82.n_ref, bf16[1184,1024]{1,0:T(8,128)(2,1)} %get-tuple-element.83.g_ref.g2_ref, bf16[4,2,1024,1024]{3,2,1,0:T(8,128)(2,1)} %get-tuple-element.84.w1_ref.w2_ref, ...), custom_call_target="tpu_custom_call" | custom-call | flops 14898167808 | bytes 29097984 | tf_op jit(solution)/shard_map/mlp_0/pallas_call | solution.py:334
  158.1 25.4 %mlp_1.1 = (f32[1184,1024]{1,0:T(8,128)}, f32[1184,1024]{1,0:T(8,128)}, bf16[4,2,512,256]{3,2,1,0:T(8,128)(2,1)}, f32[4,1,256]{2,1,0:T(1,128)}) custom-call(bf16[1184,1024]{1,0:T(8,128)(2,1)} %get-tuple-element.82.n_ref, bf16[1184,1024]{1,0:T(8,128)(2,1)} %get-tuple-element.83.g_ref.g2_ref, bf16[4,2,1024,1024]{3,2,1,0:T(8,128)(2,1)} %get-tuple-element.84.w1_ref.w2_ref, ...), custom_call_target="tpu_custom_call" | custom-call | flops 14898167808 | bytes 29097984 | tf_op jit(solution)/shard_map/mlp_1/pallas_call | solution.py:334
  183.6 45.1 %mlp_2.1 = (f32[1184,1024]{1,0:T(8,128)}, f32[1184,1024]{1,0:T(8,128)}, bf16[4,2,512,512]{3,2,1,0:T(8,128)(2,1)}, f32[4,1,512]{2,1,0:T(1,128)}) custom-call(bf16[1184,1024]{1,0:T(8,128)(2,1)} %get-tuple-element.82.n_ref, bf16[1184,1024]{1,0:T(8,128)(2,1)} %get-tuple-element.83.g_ref.g2_ref, bf16[4,2,1024,1024]{3,2,1,0:T(8,128)(2,1)} %get-tuple-element.84.w1_ref.w2_ref, ...), custom_call_target="tpu_custom_call" | custom-call | flops 29796335616 | bytes 29097984 | tf_op jit(solution)/shard_map/mlp_2/pallas_call | solution.py:334
  228.8 21.5 %turn.1 = (bf16[2,577,1024]{2,1,0:T(8,128)(2,1)}, f32[1184,1024]{1,0:T(8,128)}, bf16[1184,1024]{1,0:T(8,128)(2,1)}, bf16[4,1,512,256]{3,2,1,0:T(8,128)(2,1)}, f32[4,1024]{1,0:T(4,128)}) custom-call(f32[2]{0:T(128)} %fusion.alive_ref, f32[1184,1024]{1,0:T(8,128)} %get-tuple-element.81.resid_ref, f32[1184,1024]{1,0:T(8,128)} %get-tuple-element.89.y_ref, ...), custom_call_target="tpu_custom_call" | custom-call | flops 4966055936 | bytes 29097984 | tf_op jit(solution)/shard_map/turn/pallas_call | solution.py:428
  250.4 28.4 %unattend_0.1.grad_ref = bf16[3,1184,512]{2,1,0:T(8,128)(2,1)} custom-call(bf16[3,1184,1024]{2,1,0:T(8,128)(2,1)} %get-tuple-element.96.q_ref.k_ref.v_ref, bf16[3,1184,1024]{2,1,0:T(8,128)(2,1)} %get-tuple-element.96.q_ref.k_ref.v_ref, bf16[3,1184,1024]{2,1,0:T(8,128)(2,1)} %get-tuple-element.96.q_ref.k_ref.v_ref, bf16[1184,1024]{1,0:T(8,128)(2,1)} %get-tuple-element.97.g_ref), custom_call_target="tpu_custom_call" | custom-call | flops 14355005440 | bytes 8486912 | tf_op jit(solution)/shard_map/unattend_0/pallas_call | solution.py:569
  278.8 17.2 %close_0.1 = (f32[1184,1024]{1,0:T(8,128)}, bf16[4,5,512,128]{3,2,1,0:T(8,128)(2,1)}, f32[2,512]{1,0:T(2,128)}) custom-call(bf16[1184,1024]{1,0:T(8,128)(2,1)} %get-tuple-element.94.n_ref, bf16[3,1184,512]{2,1,0:T(8,128)(2,1)} %unattend_0.1.grad_ref, bf16[4,4,1024,256]{3,2,1,0:T(8,128)(2,1)} %get-tuple-element.92.w_ref, ...), custom_call_target="tpu_custom_call" | custom-call | flops 7449083904 | bytes 24248320 | tf_op jit(solution)/shard_map/close_0/pallas_call | solution.py:684
  296.0 6.2 %inner_mlp_0.1 = (f32[1,2,2,512,1024]{4,3,2,1,0:T(8,128)}, bf16[2,512,512]{2,1,0:T(8,128)(2,1)}) custom-call(bf16[2,512,256]{2,1,0:T(8,128)(2,1)} %bitcast.42, bf16[2,512,256]{2,1,0:T(8,128)(2,1)} %bitcast.43, f32[2,512,1024]{2,1,0:T(8,128)} %refs_4_.1, f32[1,2,2,512,1024]{4,3,2,1,0:T(8,128)} %refs_2_.7), custom_call_target="tpu_custom_call" | custom-call | flops 15728640 | bytes 12582912 | tf_op jit(solution)/shard_map/inner_mlp_0/pallas_call | solution.py:1155
  302.3 30.6 %unattend_1.1 = (bf16[3,1184,512]{2,1,0:T(8,128)(2,1)}, bf16[256,512]{1,0:T(8,128)(2,1)}) custom-call(bf16[3,1184,1024]{2,1,0:T(8,128)(2,1)} %get-tuple-element.96.q_ref.k_ref.v_ref, bf16[3,1184,1024]{2,1,0:T(8,128)(2,1)} %get-tuple-element.96.q_ref.k_ref.v_ref, bf16[3,1184,1024]{2,1,0:T(8,128)(2,1)} %get-tuple-element.96.q_ref.k_ref.v_ref, ...), custom_call_target="tpu_custom_call" | custom-call | flops 14355005440 | bytes 8486912 | tf_op jit(solution)/shard_map/unattend_1/pallas_call | solution.py:569
  332.9 6.0 %inner_mlp_1.1 = (f32[1,2,2,512,1024]{4,3,2,1,0:T(8,128)}, bf16[2,512,512]{2,1,0:T(8,128)(2,1)}) custom-call(bf16[2,512,512]{2,1,0:T(8,128)(2,1)} %bitcast.37, f32[2,512,1024]{2,1,0:T(8,128)} %refs_4_.1, f32[1,2,2,512,1024]{4,3,2,1,0:T(8,128)} %refs_2_.7, f32[1,2,2,512,1024]{4,3,2,1,0:T(8,128)} %get-tuple-element.110.refs_3_), custom_call_target="tpu_custom_call", output_to_operand_aliasing={{0}: (3, {})} | custom-call | flops 15728640 | bytes 12582912 | tf_op jit(solution)/shard_map/inner_mlp_1/pallas_call | solution.py:1155
  338.9 22.2 %close_1.1 = (f32[1184,1024]{1,0:T(8,128)}, bf16[256,512]{1,0:T(8,128)(2,1)}, bf16[4,3,512,128]{3,2,1,0:T(8,128)(2,1)}, f32[2,512]{1,0:T(2,128)}) custom-call(bf16[1184,1024]{1,0:T(8,128)(2,1)} %get-tuple-element.94.n_ref, bf16[3,1184,512]{2,1,0:T(8,128)(2,1)} %get-tuple-element.107.grad_ref, bf16[4,4,1024,256]{3,2,1,0:T(8,128)(2,1)} %get-tuple-element.92.w_ref, ...), custom_call_target="tpu_custom_call" | custom-call | flops 7449083904 | bytes 24248320 | tf_op jit(solution)/shard_map/close_1/pallas_call | solution.py:684
  362.4 1.5 collective-permute-start.2
  366.9 3.8 copy.31
  370.9 9.8 %finish.1 = (f32[2,577,1,1024]{3,2,1,0:T(1,128)}, f32[2,1024]{1,0:T(2,128)}) custom-call(f32[1184,1024]{1,0:T(8,128)} %get-tuple-element.114.acc_ref, f32[1184,1024]{1,0:T(8,128)} %get-tuple-element.115.gr_ref, bf16[1184,1024]{1,0:T(8,128)(2,1)} %get-tuple-element.116.x_ref, f32[12,1024]{1,0:T(8,128)} %refs_1_.8), custom_call_target="tpu_custom_call" | custom-call | flops 24248320 | bytes 16973824 | tf_op jit(solution)/shard_map/finish/pallas_call | solution.py:719
  380.7 2.0 concatenate.14.refs_0_
  382.6 3.8 reduce-scatter.14.cloned.1.call-done
  386.5 6.3 %inner_early.1 = (f32[1,2,4,512,256]{4,3,2,1,0:T(8,128)}, bf16[5,512,128]{2,1,0:T(8,128)(2,1)}) custom-call(bf16[5,512,128]{2,1,0:T(8,128)(2,1)} %bitcast.40, f32[4,512,256]{2,1,0:T(8,128)} %refs_1_.11, f32[1,2,4,512,256]{4,3,2,1,0:T(8,128)} %refs_2_.10), custom_call_target="tpu_custom_call" | custom-call | flops 9830400 | bytes 7864320 | tf_op jit(solution)/shard_map/inner_early/pallas_call | solution.py:1155
  392.8 25.9 %group_early.1 = (bf16[2560,128]{1,0:T(8,128)(2,1)}, f32[2,12,1024]{2,1,0:T(8,128)}, f32[3,12,1024]{2,1,0:T(8,128)}, bf16[12,1024]{1,0:T(8,128)(2,1)}) custom-call(bf16[2560,128]{1,0:T(8,128)(2,1)} %bitcast.39, f32[12,1024]{1,0:T(8,128)} %concatenate.14.refs_0_, f32[12,1024]{1,0:T(8,128)} %refs_1_.8, f32[2,12,1024]{2,1,0:T(8,128)} %bitcast.41, ...), custom_call_target="tpu_custom_call" | custom-call | flops 1310720 | bytes 2621440 | tf_op jit(solution)/shard_map/group_early/pallas_call | solution.py:1374
  418.7 1.6 copy.33
  420.4 5.6 %outer_early.1 = (f32[3,4,512,256]{3,2,1,0:T(8,128)}, bf16[4,512,256]{2,1,0:T(8,128)(2,1)}) custom-call(s32[1]{0:T(128)} %bitcast.17.g_ref, bf16[5,512,128]{2,1,0:T(8,128)(2,1)} %bitcast.38, f32[4,512,256]{2,1,0:T(8,128)} %refs_1_.11, f32[4,512,256]{2,1,0:T(8,128)} %refs_2_.11), custom_call_target="tpu_custom_call" | custom-call | flops 3276800 | bytes 7864320 | tf_op jit(solution)/shard_map/outer_early/pallas_call | solution.py:1203
  426.7 10.4 %outer_mlp.1 = (f32[3,2,512,1024]{3,2,1,0:T(8,128)}, bf16[2,512,1024]{2,1,0:T(8,128)(2,1)}) custom-call(s32[1]{0:T(128)} %bitcast.17.g_ref, bf16[256,1024]{1,0:T(8,128)(2,1)} %copy-done.1, bf16[256,1024]{1,0:T(8,128)(2,1)} %collective-permute-done.refs_1_, bf16[256,1024]{1,0:T(8,128)(2,1)} %collective-permute-done.1.refs_2_, bf16[256,1024]{1,0:T(8,128)(2,1)} %copy-done.2, ...), custom_call_target="tpu_custom_call" | custom-call | flops 10485760 | bytes 25165824 | tf_op jit(solution)/shard_map/outer_mlp/pallas_call | solution.py:1203
  437.1 4.3 inner_late.1
  441.5 14.7 %group_late.1 = bf16[1536,128]{1,0:T(8,128)(2,1)} custom-call(bf16[1536,128]{1,0:T(8,128)(2,1)} %bitcast.44), custom_call_target="tpu_custom_call" | custom-call | flops 786432 | bytes 1572864 | tf_op jit(solution)/shard_map/group_late/pallas_call | solution.py:1374
  456.2 3.9 outer_late.1
  (60 shorter events, 9.4 us)
Async XLA Ops:
  7.2 271.6 %reduce-scatter.8.cloned.1.call-start = ((), (), s32[]{:S(2)}) async-start(), calls=%async_computation.6 | async-start | bytes 2621440 | tf_op jit(solution)/shard_map/reduce_scatter | solution.py:1415
  158.1 137.9 %reduce-scatter.10.cloned.1.call-start = ((), (), s32[]{:S(2)}) async-start(), calls=%async_computation.7 | async-start | bytes 2621440 | tf_op jit(solution)/shard_map/reduce_scatter | solution.py:1415
  183.6 149.4 %reduce-scatter.6.cloned.1.call-start = ((), (), s32[]{:S(2)}) async-start(), calls=%async_computation.5 | async-start | bytes 5242880 | tf_op jit(solution)/shard_map/reduce_scatter | solution.py:1415
  228.8 157.7 %reduce-scatter.14.cloned.1.call-start = ((), (), s32[]{:S(2)}) async-start(), calls=%async_computation.9 | async-start | bytes 3276800 | tf_op jit(solution)/shard_map/reduce_scatter | solution.py:1415
  296.0 141.2 %reduce-scatter.12.cloned.1.call-start = ((), (), s32[]{:S(2)}) async-start(), calls=%async_computation.8 | async-start | bytes 1966080 | tf_op jit(solution)/shard_map/reduce_scatter | solution.py:1415
  338.9 22.3 %copy-start.3 = (bf16[256,512]{1,0:T(8,128)(2,1)S(1)}, bf16[256,512]{1,0:T(8,128)(2,1)}, u32[]{:S(2)}) copy-start(bf16[256,512]{1,0:T(8,128)(2,1)} %get-tuple-element.130) | copy-start | bytes 786436
  338.9 26.6 %copy-start.5 = (f32[1,2,12,1024]{3,1,2,0:T(2,128)S(1)}, f32[1,2,12,1024]{3,1,2,0:T(2,128)}, u32[]{:S(2)}) copy-start(f32[1,2,12,1024]{3,1,2,0:T(2,128)} %param.20) | copy-start | bytes 294916
  361.1 5.8 %copy-start = (bf16[2,577,1024]{2,1,0:T(8,128)(2,1)S(1)}, bf16[2,577,1024]{2,1,0:T(8,128)(2,1)}, u32[]{:S(2)}) copy-start(bf16[2,577,1024]{2,1,0:T(8,128)(2,1)} %get-tuple-element.93) | copy-start | bytes 7090180
  361.1 9.7 %copy-start.7 = (f32[4,1024]{1,0:T(4,128)S(1)}, f32[4,1024]{1,0:T(4,128)}, u32[]{:S(2)}) copy-start(f32[4,1024]{1,0:T(4,128)} %get-tuple-element.122) | copy-start | bytes 49156
  362.4 18.3 %copy-start.1 = (bf16[256,1024]{1,0:T(8,128)(2,1)}, bf16[256,1024]{1,0:T(8,128)(2,1)S(1)}, u32[]{:S(2)}) copy-start(bf16[256,1024]{1,0:T(8,128)(2,1)S(1)} %constant_dynamic-update-slice_fusion.refs_0_) | copy-start | bytes 1572868
  362.4 63.6 %collective-permute-start.2 = (bf16[256,1024]{1,0:T(8,128)(2,1)S(1)}, bf16[256,1024]{1,0:T(8,128)(2,1)S(1)}, u32[]{:S(2)}, u32[]{:S(2)}) collective-permute-start(bf16[256,1024]{1,0:T(8,128)(2,1)S(1)} %constant_dynamic-update-slice_fusion.refs_0_), channel_id=1, source_target_pairs={{0,24},{8,0},{16,8},{24,16},{1,25},{9,1},{17,9},{25,17},{2,26},{10... | collective-permute-start | bytes 1572872 | tf_op jit(solution)/shard_map/ppermute | solution.py:1398
  363.9 62.0 %collective-permute-start.1 = (bf16[256,1024]{1,0:T(8,128)(2,1)S(1)}, bf16[256,1024]{1,0:T(8,128)(2,1)}, u32[]{:S(2)}, u32[]{:S(2)}) collective-permute-start(bf16[256,1024]{1,0:T(8,128)(2,1)S(1)} %constant_dynamic-update-slice_fusion.refs_0_), channel_id=1, source_target_pairs={{0,16},{8,24},{16,0},{24,8},{1,17},{9,25},{17,1},{25,9},{2,18},{10... | collective-permute-start | bytes 1572872 | tf_op jit(solution)/shard_map/ppermute | solution.py:1398
  365.3 60.7 %collective-permute-start = (bf16[256,1024]{1,0:T(8,128)(2,1)S(1)}, bf16[256,1024]{1,0:T(8,128)(2,1)}, u32[]{:S(2)}, u32[]{:S(2)}) collective-permute-start(bf16[256,1024]{1,0:T(8,128)(2,1)S(1)} %constant_dynamic-update-slice_fusion.refs_0_), channel_id=1, source_target_pairs={{0,8},{8,16},{16,24},{24,0},{1,9},{9,17},{17,25},{25,1},{2,10},{10... | collective-permute-start | bytes 1572872 | tf_op jit(solution)/shard_map/ppermute | solution.py:1398
  365.5 5.2 %copy-start.9 = (f32[4,1,256]{2,1,0:T(1,128)S(1)}, f32[4,1,256]{2,1,0:T(1,128)}, u32[]{:S(2)}) copy-start(f32[4,1,256]{2,1,0:T(1,128)} %get-tuple-element.126) | copy-start | bytes 12292
  365.5 5.2 %copy-start.8 = (f32[4,1,512]{2,1,0:T(1,128)S(1)}, f32[4,1,512]{2,1,0:T(1,128)}, u32[]{:S(2)}) copy-start(f32[4,1,512]{2,1,0:T(1,128)} %get-tuple-element.127) | copy-start | bytes 24580
  366.2 4.6 copy-start.10
  366.2 4.6 copy-start.11
  425.9 0.8 copy-start.2
  456.1 3.9 copy-start.4
  456.2 4.6 copy-start.6
Sparse Core Ops, SparseCore 0:
  158.2 49.2 reduce-scatter.7
  209.9 43.1 reduce-scatter.9
  255.4 76.0 reduce-scatter.5
  333.8 52.5 reduce-scatter.13
  388.7 37.0 reduce-scatter.11

commit v6 on v5

--- a/solution.py
+++ b/solution.py
@@ -519,13 +519,14 @@
     span = q_ref.shape[1]
     scale = HD**-0.5
     q, k, v, g = q_ref[0], k_ref[0], v_ref[0], g_ref[...]
+    scaled = (k.astype(F32) * scale).astype(LOW)
     parts = []
     for h in range(2):
-        scores = dot(half_lanes(k, h), q, NT)
+        scores = dot(half_lanes(scaled, h), q, NT)
         row = lax.broadcasted_iota(jnp.int32, scores.shape, 0)
         scores = jnp.where(row < seq, scores, -1e30)
         top = jnp.max(scores, axis=0, keepdims=True)
-        raised = jnp.exp((scores - top) * scale)
+        raised = jnp.exp(scores - top)
         total = jnp.sum(raised, axis=0, keepdims=True)
         probs = raised * (1.0 / total)
         gp = dot(half_lanes(v, h), g, NT)

time: 477 us -> 476 us (level)
  transfers between devices with their start and end apart: 8 -> 8, of which waited for: 1 -> 1; matrix products, arithmetic and copies ran while one was open for 2% -> 2% of each run, Pallas kernels for 56% -> 55%
where the time goes in v6:
time: 476 us; the launch traced here: 467 us
  Pallas kernels  429 us (90%)
  between operations  14.5 us (3%)
  local copies, waits for them, and re-layouts  13.5 us (3%)
  waiting for transfers between devices  4.8 us (1%)
    pallas_call x1, Pallas kernels, front(): pl.pallas_call(functools.partial(front_kernel, images, seq), in_specs=[pl...  122 us
    pallas_call x3, Pallas kernels, mlp(): pl.pallas_call(functools.partial(mlp_kernel, first, pairwise), grid=(step...  96.8 us
    pallas_call x2, Pallas kernels, unattend(): pl.pallas_call(functools.partial(unattend_kernel, seq, groups), grid=(ima...  57.9 us
    pallas_call x2, Pallas kernels, group_sum(): pl.pallas_call(functools.partial(group_kernel, groups, shards, bool(vecto...  39.2 us
    pallas_call x2, Pallas kernels, close(): pl.pallas_call(functools.partial(close_kernel, pairwise, groups, first, f...  39 us
    pallas_call x4, Pallas kernels, inner_step(): pl.pallas_call(functools.partial(inner_kernel, join, count), grid=(units,...  22.8 us
    pallas_call x1, Pallas kernels, turn(): pl.pallas_call(functools.partial(turn_kernel, seq, pairwise), grid=(image...  21.5 us
    pallas_call x3, Pallas kernels, outer_step(): pl.pallas_call(functools.partial(outer_kernel, groups, slots, each), grid...  19.9 us
  transfers between devices with their start and end apart: 8, of which 1 were waited for; matrix products, arithmetic and copies ran while one was open for 2% of the time, Pallas kernels for 55%

profile of v6, /device:TPU:0, one launch (start us, length us, event | category | flops | bytes accessed | tf_op | source)
XLA Modules:
  0.0 466.9 jit_solution(11355506913000663344)
XLA Ops:
  10.0 121.8 %front.1 = (bf16[4,4,1024,256]{3,2,1,0:T(8,128)(2,1)}, bf16[4,2,1024,1024]{3,2,1,0:T(8,128)(2,1)}, bf16[1184,1024]{1,0:T(8,128)(2,1)}, bf16[3,1184,1024]{2,1,0:T...) custom-call(f32[2]{0:T(128)} %fusion.alive_ref, ...), custom_call_target="tpu_custom_call" | custom-call | flops 9932111872 | bytes 36372480 | tf_op jit(solution)/shard_map/front/pallas_call | solution.py:1086
  131.8 26.3 %mlp_0.1 = (f32[1184,1024]{1,0:T(8,128)}, f32[1184,1024]{1,0:T(8,128)}, bf16[4,2,512,256]{3,2,1,0:T(8,128)(2,1)}, f32[4,1,256]{2,1,0:T(1,128)}) custom-call(bf16[1184,1024]{1,0:T(8,128)(2,1)} %get-tuple-element.82.n_ref, bf16[1184,1024]{1,0:T(8,128)(2,1)} %get-tuple-element.83.g_ref.g2_ref, bf16[4,2,1024,1024]{3,2,1,0:T(8,128)(2,1)} %get-tuple-element.84.w1_ref.w2_ref, ...), custom_call_target="tpu_custom_call" | custom-call | flops 14898167808 | bytes 29097984 | tf_op jit(solution)/shard_map/mlp_0/pallas_call | solution.py:334
  158.1 25.4 %mlp_1.1 = (f32[1184,1024]{1,0:T(8,128)}, f32[1184,1024]{1,0:T(8,128)}, bf16[4,2,512,256]{3,2,1,0:T(8,128)(2,1)}, f32[4,1,256]{2,1,0:T(1,128)}) custom-call(bf16[1184,1024]{1,0:T(8,128)(2,1)} %get-tuple-element.82.n_ref, bf16[1184,1024]{1,0:T(8,128)(2,1)} %get-tuple-element.83.g_ref.g2_ref, bf16[4,2,1024,1024]{3,2,1,0:T(8,128)(2,1)} %get-tuple-element.84.w1_ref.w2_ref, ...), custom_call_target="tpu_custom_call" | custom-call | flops 14898167808 | bytes 29097984 | tf_op jit(solution)/shard_map/mlp_1/pallas_call | solution.py:334
  183.6 45.1 %mlp_2.1 = (f32[1184,1024]{1,0:T(8,128)}, f32[1184,1024]{1,0:T(8,128)}, bf16[4,2,512,512]{3,2,1,0:T(8,128)(2,1)}, f32[4,1,512]{2,1,0:T(1,128)}) custom-call(bf16[1184,1024]{1,0:T(8,128)(2,1)} %get-tuple-element.82.n_ref, bf16[1184,1024]{1,0:T(8,128)(2,1)} %get-tuple-element.83.g_ref.g2_ref, bf16[4,2,1024,1024]{3,2,1,0:T(8,128)(2,1)} %get-tuple-element.84.w1_ref.w2_ref, ...), custom_call_target="tpu_custom_call" | custom-call | flops 29796335616 | bytes 29097984 | tf_op jit(solution)/shard_map/mlp_2/pallas_call | solution.py:334
  228.8 21.5 %turn.1 = (bf16[2,577,1024]{2,1,0:T(8,128)(2,1)}, f32[1184,1024]{1,0:T(8,128)}, bf16[1184,1024]{1,0:T(8,128)(2,1)}, bf16[4,1,512,256]{3,2,1,0:T(8,128)(2,1)}, f32[4,1024]{1,0:T(4,128)}) custom-call(f32[2]{0:T(128)} %fusion.alive_ref, f32[1184,1024]{1,0:T(8,128)} %get-tuple-element.81.resid_ref, f32[1184,1024]{1,0:T(8,128)} %get-tuple-element.89.y_ref, ...), custom_call_target="tpu_custom_call" | custom-call | flops 4966055936 | bytes 29097984 | tf_op jit(solution)/shard_map/turn/pallas_call | solution.py:428
  250.4 27.8 %unattend_0.1.grad_ref = bf16[3,1184,512]{2,1,0:T(8,128)(2,1)} custom-call(bf16[3,1184,1024]{2,1,0:T(8,128)(2,1)} %get-tuple-element.96.q_ref.k_ref.v_ref, bf16[3,1184,1024]{2,1,0:T(8,128)(2,1)} %get-tuple-element.96.q_ref.k_ref.v_ref, bf16[3,1184,1024]{2,1,0:T(8,128)(2,1)} %get-tuple-element.96.q_ref.k_ref.v_ref, bf16[1184,1024]{1,0:T(8,128)(2,1)} %get-tuple-element.97.g_ref), custom_call_target="tpu_custom_call" | custom-call | flops 14355005440 | bytes 8486912 | tf_op jit(solution)/shard_map/unattend_0/pallas_call | solution.py:570
  278.1 17.0 %close_0.1 = (f32[1184,1024]{1,0:T(8,128)}, bf16[4,5,512,128]{3,2,1,0:T(8,128)(2,1)}, f32[2,512]{1,0:T(2,128)}) custom-call(bf16[1184,1024]{1,0:T(8,128)(2,1)} %get-tuple-element.94.n_ref, bf16[3,1184,512]{2,1,0:T(8,128)(2,1)} %unattend_0.1.grad_ref, bf16[4,4,1024,256]{3,2,1,0:T(8,128)(2,1)} %get-tuple-element.92.w_ref, ...), custom_call_target="tpu_custom_call" | custom-call | flops 7449083904 | bytes 24248320 | tf_op jit(solution)/shard_map/close_0/pallas_call | solution.py:685
  295.3 6.2 %inner_mlp_0.1 = (f32[1,2,2,512,1024]{4,3,2,1,0:T(8,128)}, bf16[2,512,512]{2,1,0:T(8,128)(2,1)}) custom-call(bf16[2,512,256]{2,1,0:T(8,128)(2,1)} %bitcast.42, bf16[2,512,256]{2,1,0:T(8,128)(2,1)} %bitcast.43, f32[2,512,1024]{2,1,0:T(8,128)} %refs_4_.1, f32[1,2,2,512,1024]{4,3,2,1,0:T(8,128)} %refs_2_.7), custom_call_target="tpu_custom_call" | custom-call | flops 15728640 | bytes 12582912 | tf_op jit(solution)/shard_map/inner_mlp_0/pallas_call | solution.py:1156
  301.5 30.2 %unattend_1.1 = (bf16[3,1184,512]{2,1,0:T(8,128)(2,1)}, bf16[256,512]{1,0:T(8,128)(2,1)}) custom-call(bf16[3,1184,1024]{2,1,0:T(8,128)(2,1)} %get-tuple-element.96.q_ref.k_ref.v_ref, bf16[3,1184,1024]{2,1,0:T(8,128)(2,1)} %get-tuple-element.96.q_ref.k_ref.v_ref, bf16[3,1184,1024]{2,1,0:T(8,128)(2,1)} %get-tuple-element.96.q_ref.k_ref.v_ref, ...), custom_call_target="tpu_custom_call" | custom-call | flops 14355005440 | bytes 8486912 | tf_op jit(solution)/shard_map/unattend_1/pallas_call | solution.py:570
  331.7 6.0 %inner_mlp_1.1 = (f32[1,2,2,512,1024]{4,3,2,1,0:T(8,128)}, bf16[2,512,512]{2,1,0:T(8,128)(2,1)}) custom-call(bf16[2,512,512]{2,1,0:T(8,128)(2,1)} %bitcast.37, f32[2,512,1024]{2,1,0:T(8,128)} %refs_4_.1, f32[1,2,2,512,1024]{4,3,2,1,0:T(8,128)} %refs_2_.7, f32[1,2,2,512,1024]{4,3,2,1,0:T(8,128)} %get-tuple-element.110.refs_3_), custom_call_target="tpu_custom_call", output_to_operand_aliasing={{0}: (3, {})} | custom-call | flops 15728640 | bytes 12582912 | tf_op jit(solution)/shard_map/inner_mlp_1/pallas_call | solution.py:1156
  337.7 22.0 %close_1.1 = (f32[1184,1024]{1,0:T(8,128)}, bf16[256,512]{1,0:T(8,128)(2,1)}, bf16[4,3,512,128]{3,2,1,0:T(8,128)(2,1)}, f32[2,512]{1,0:T(2,128)}) custom-call(bf16[1184,1024]{1,0:T(8,128)(2,1)} %get-tuple-element.94.n_ref, bf16[3,1184,512]{2,1,0:T(8,128)(2,1)} %get-tuple-element.107.grad_ref, bf16[4,4,1024,256]{3,2,1,0:T(8,128)(2,1)} %get-tuple-element.92.w_ref, ...), custom_call_target="tpu_custom_call" | custom-call | flops 7449083904 | bytes 24248320 | tf_op jit(solution)/shard_map/close_1/pallas_call | solution.py:685
  360.9 2.3 collective-permute-start.2
  366.1 3.8 copy.31
  370.1 9.8 %finish.1 = (f32[2,577,1,1024]{3,2,1,0:T(1,128)}, f32[2,1024]{1,0:T(2,128)}) custom-call(f32[1184,1024]{1,0:T(8,128)} %get-tuple-element.114.acc_ref, f32[1184,1024]{1,0:T(8,128)} %get-tuple-element.115.gr_ref, bf16[1184,1024]{1,0:T(8,128)(2,1)} %get-tuple-element.116.x_ref, f32[12,1024]{1,0:T(8,128)} %refs_1_.8), custom_call_target="tpu_custom_call" | custom-call | flops 24248320 | bytes 16973824 | tf_op jit(solution)/shard_map/finish/pallas_call | solution.py:720
  379.8 2.0 concatenate.14.refs_0_
  381.8 4.7 reduce-scatter.14.cloned.1.call-done
  386.5 6.3 %inner_early.1 = (f32[1,2,4,512,256]{4,3,2,1,0:T(8,128)}, bf16[5,512,128]{2,1,0:T(8,128)(2,1)}) custom-call(bf16[5,512,128]{2,1,0:T(8,128)(2,1)} %bitcast.40, f32[4,512,256]{2,1,0:T(8,128)} %refs_1_.11, f32[1,2,4,512,256]{4,3,2,1,0:T(8,128)} %refs_2_.10), custom_call_target="tpu_custom_call" | custom-call | flops 9830400 | bytes 7864320 | tf_op jit(solution)/shard_map/inner_early/pallas_call | solution.py:1156
  392.8 24.6 %group_early.1 = (bf16[2560,128]{1,0:T(8,128)(2,1)}, f32[2,12,1024]{2,1,0:T(8,128)}, f32[3,12,1024]{2,1,0:T(8,128)}, bf16[12,1024]{1,0:T(8,128)(2,1)}) custom-call(bf16[2560,128]{1,0:T(8,128)(2,1)} %bitcast.39, f32[12,1024]{1,0:T(8,128)} %concatenate.14.refs_0_, f32[12,1024]{1,0:T(8,128)} %refs_1_.8, f32[2,12,1024]{2,1,0:T(8,128)} %bitcast.41, ...), custom_call_target="tpu_custom_call" | custom-call | flops 1310720 | bytes 2621440 | tf_op jit(solution)/shard_map/group_early/pallas_call | solution.py:1375
  417.3 1.6 copy.33
  419.0 5.6 %outer_early.1 = (f32[3,4,512,256]{3,2,1,0:T(8,128)}, bf16[4,512,256]{2,1,0:T(8,128)(2,1)}) custom-call(s32[1]{0:T(128)} %bitcast.17.g_ref, bf16[5,512,128]{2,1,0:T(8,128)(2,1)} %bitcast.38, f32[4,512,256]{2,1,0:T(8,128)} %refs_1_.11, f32[4,512,256]{2,1,0:T(8,128)} %refs_2_.11), custom_call_target="tpu_custom_call" | custom-call | flops 3276800 | bytes 7864320 | tf_op jit(solution)/shard_map/outer_early/pallas_call | solution.py:1204
  425.3 10.4 %outer_mlp.1 = (f32[3,2,512,1024]{3,2,1,0:T(8,128)}, bf16[2,512,1024]{2,1,0:T(8,128)(2,1)}) custom-call(s32[1]{0:T(128)} %bitcast.17.g_ref, bf16[256,1024]{1,0:T(8,128)(2,1)} %copy-done.1, bf16[256,1024]{1,0:T(8,128)(2,1)} %collective-permute-done.refs_1_, bf16[256,1024]{1,0:T(8,128)(2,1)} %collective-permute-done.1.refs_2_, bf16[256,1024]{1,0:T(8,128)(2,1)} %copy-done.2, ...), custom_call_target="tpu_custom_call" | custom-call | flops 10485760 | bytes 25165824 | tf_op jit(solution)/shard_map/outer_mlp/pallas_call | solution.py:1204
  435.8 4.3 inner_late.1
  440.1 14.6 %group_late.1 = bf16[1536,128]{1,0:T(8,128)(2,1)} custom-call(bf16[1536,128]{1,0:T(8,128)(2,1)} %bitcast.44), custom_call_target="tpu_custom_call" | custom-call | flops 786432 | bytes 1572864 | tf_op jit(solution)/shard_map/group_late/pallas_call | solution.py:1375
  454.7 3.9 outer_late.1
  (60 shorter events, 9.2 us)
Async XLA Ops:
  7.2 271.0 %reduce-scatter.8.cloned.1.call-start = ((), (), s32[]{:S(2)}) async-start(), calls=%async_computation.6 | async-start | bytes 2621440 | tf_op jit(solution)/shard_map/reduce_scatter | solution.py:1416
  158.1 137.2 %reduce-scatter.10.cloned.1.call-start = ((), (), s32[]{:S(2)}) async-start(), calls=%async_computation.7 | async-start | bytes 2621440 | tf_op jit(solution)/shard_map/reduce_scatter | solution.py:1416
  183.6 148.1 %reduce-scatter.6.cloned.1.call-start = ((), (), s32[]{:S(2)}) async-start(), calls=%async_computation.5 | async-start | bytes 5242880 | tf_op jit(solution)/shard_map/reduce_scatter | solution.py:1416
  228.8 157.7 %reduce-scatter.14.cloned.1.call-start = ((), (), s32[]{:S(2)}) async-start(), calls=%async_computation.9 | async-start | bytes 3276800 | tf_op jit(solution)/shard_map/reduce_scatter | solution.py:1416
  295.2 140.6 %reduce-scatter.12.cloned.1.call-start = ((), (), s32[]{:S(2)}) async-start(), calls=%async_computation.8 | async-start | bytes 1966080 | tf_op jit(solution)/shard_map/reduce_scatter | solution.py:1416
  337.7 22.0 %copy-start.3 = (bf16[256,512]{1,0:T(8,128)(2,1)S(1)}, bf16[256,512]{1,0:T(8,128)(2,1)}, u32[]{:S(2)}) copy-start(bf16[256,512]{1,0:T(8,128)(2,1)} %get-tuple-element.130) | copy-start | bytes 786436
  337.7 27.0 %copy-start.5 = (f32[1,2,12,1024]{3,1,2,0:T(2,128)S(1)}, f32[1,2,12,1024]{3,1,2,0:T(2,128)}, u32[]{:S(2)}) copy-start(f32[1,2,12,1024]{3,1,2,0:T(2,128)} %param.20) | copy-start | bytes 294916
  359.7 6.4 %copy-start = (bf16[2,577,1024]{2,1,0:T(8,128)(2,1)S(1)}, bf16[2,577,1024]{2,1,0:T(8,128)(2,1)}, u32[]{:S(2)}) copy-start(bf16[2,577,1024]{2,1,0:T(8,128)(2,1)} %get-tuple-element.93) | copy-start | bytes 7090180
  359.7 10.2 %copy-start.7 = (f32[4,1024]{1,0:T(4,128)S(1)}, f32[4,1024]{1,0:T(4,128)}, u32[]{:S(2)}) copy-start(f32[4,1024]{1,0:T(4,128)} %get-tuple-element.122) | copy-start | bytes 49156
  360.9 18.9 %copy-start.1 = (bf16[256,1024]{1,0:T(8,128)(2,1)}, bf16[256,1024]{1,0:T(8,128)(2,1)S(1)}, u32[]{:S(2)}) copy-start(bf16[256,1024]{1,0:T(8,128)(2,1)S(1)} %constant_dynamic-update-slice_fusion.refs_0_) | copy-start | bytes 1572868
  360.9 63.6 %collective-permute-start.2 = (bf16[256,1024]{1,0:T(8,128)(2,1)S(1)}, bf16[256,1024]{1,0:T(8,128)(2,1)S(1)}, u32[]{:S(2)}, u32[]{:S(2)}) collective-permute-start(bf16[256,1024]{1,0:T(8,128)(2,1)S(1)} %constant_dynamic-update-slice_fusion.refs_0_), channel_id=1, source_target_pairs={{0,24},{8,0},{16,8},{24,16},{1,25},{9,1},{17,9},{25,17},{2,26},{10... | collective-permute-start | bytes 1572872 | tf_op jit(solution)/shard_map/ppermute | solution.py:1399
  363.3 61.3 %collective-permute-start.1 = (bf16[256,1024]{1,0:T(8,128)(2,1)S(1)}, bf16[256,1024]{1,0:T(8,128)(2,1)}, u32[]{:S(2)}, u32[]{:S(2)}) collective-permute-start(bf16[256,1024]{1,0:T(8,128)(2,1)S(1)} %constant_dynamic-update-slice_fusion.refs_0_), channel_id=1, source_target_pairs={{0,16},{8,24},{16,0},{24,8},{1,17},{9,25},{17,1},{25,9},{2,18},{10... | collective-permute-start | bytes 1572872 | tf_op jit(solution)/shard_map/ppermute | solution.py:1399
  363.8 60.7 %collective-permute-start = (bf16[256,1024]{1,0:T(8,128)(2,1)S(1)}, bf16[256,1024]{1,0:T(8,128)(2,1)}, u32[]{:S(2)}, u32[]{:S(2)}) collective-permute-start(bf16[256,1024]{1,0:T(8,128)(2,1)S(1)} %constant_dynamic-update-slice_fusion.refs_0_), channel_id=1, source_target_pairs={{0,8},{8,16},{16,24},{24,0},{1,9},{9,17},{17,25},{25,1},{2,10},{10... | collective-permute-start | bytes 1572872 | tf_op jit(solution)/shard_map/ppermute | solution.py:1399
  364.7 5.2 %copy-start.9 = (f32[4,1,256]{2,1,0:T(1,128)S(1)}, f32[4,1,256]{2,1,0:T(1,128)}, u32[]{:S(2)}) copy-start(f32[4,1,256]{2,1,0:T(1,128)} %get-tuple-element.126) | copy-start | bytes 12292
  364.7 5.2 %copy-start.8 = (f32[4,1,512]{2,1,0:T(1,128)S(1)}, f32[4,1,512]{2,1,0:T(1,128)}, u32[]{:S(2)}) copy-start(f32[4,1,512]{2,1,0:T(1,128)} %get-tuple-element.127) | copy-start | bytes 24580
  365.4 4.6 copy-start.10
  365.4 4.6 copy-start.11
  424.5 0.8 copy-start.2
  454.7 3.9 copy-start.4
  454.7 4.6 copy-start.6
Sparse Core Ops, SparseCore 0:
  158.2 49.2 reduce-scatter.7
  209.9 43.1 reduce-scatter.9
  255.4 76.0 reduce-scatter.5
  333.8 52.5 reduce-scatter.13
  388.7 37.0 reduce-scatter.11
